TPU v7x, 8 devices: a whole 2x2x1 slice. The times are simulated.
8 devices in a mesh: data: 4 (over z, y, x), stage: 2 (over core).
Axes of the slice: x: 2, y: 2, z: 1, core: 2. Of those that a mesh axis runs over, the one named last changes fastest.
Arguments:
- x: bfloat16 [4, 32, 32, 2048], P(None, 'data')
- g: bfloat16 [4, 32, 32, 2048], P(None, 'data')
- w_gate: bfloat16 [2, 1, 2048, 8192], P('stage', None, 'data')
- w_in: bfloat16 [2, 1, 2048, 8192], P('stage', None, 'data')
- w_out: bfloat16 [2, 1, 8192, 2048], P('stage', None, 'data')
Outputs:
- output 1: bfloat16 [4, 32, 32, 2048], P(None, 'data')
- output 2: float32 [2, 1, 2048, 8192], P('stage', None, 'data')
- output 3: float32 [2, 1, 2048, 8192], P('stage', None, 'data')
- output 4: float32 [2, 1, 8192, 2048], P('stage', None, 'data')
All inputs are finite; a program needn't handle non-finite values.
Results may differ from a plain program's by a relative error of at most 0.0116315.
Values are sent between devices in bfloat16 or wider.
A program may use at most 1 GiB of HBM per device.

v0:
```python
import jax
import jax.numpy as jnp
from jax import lax
from jax.sharding import PartitionSpec as P


def rms_f32(row_vals):
    return row_vals * lax.rsqrt(jnp.mean(row_vals * row_vals, axis=-1, keepdims=True) + 1e-6)


def layer_fwd(tokens, w_gate, w_in, w_out):
    normed = rms_f32(tokens.astype(jnp.float32)).astype(jnp.bfloat16)
    pre_gate = jnp.dot(normed, w_gate, preferred_element_type=jnp.float32)
    pre_in = jnp.dot(normed, w_in, preferred_element_type=jnp.float32)
    hidden = (pre_gate * jax.nn.sigmoid(pre_gate) * pre_in).astype(jnp.bfloat16)
    branch = jnp.dot(hidden, w_out, preferred_element_type=jnp.float32)
    return tokens + branch.astype(jnp.bfloat16)


def layer_bwd(tokens, d_next, w_gate, w_in, w_out):
    normed_f, rms_pull = jax.vjp(rms_f32, tokens.astype(jnp.float32))
    normed = normed_f.astype(jnp.bfloat16)
    pre_gate = jnp.dot(normed, w_gate, preferred_element_type=jnp.float32)
    pre_in = jnp.dot(normed, w_in, preferred_element_type=jnp.float32)
    sigma_gate = jax.nn.sigmoid(pre_gate)
    gate_act = pre_gate * sigma_gate
    hidden = (gate_act * pre_in).astype(jnp.bfloat16)
    d_wout = jnp.einsum('tf,td->fd', hidden, d_next, preferred_element_type=jnp.float32)
    d_hidden = jnp.einsum('td,fd->tf', d_next, w_out, preferred_element_type=jnp.float32)
    d_gate = (d_hidden * pre_in * sigma_gate * (1.0 + pre_gate * (1.0 - sigma_gate))).astype(jnp.bfloat16)
    d_up = (d_hidden * gate_act).astype(jnp.bfloat16)
    d_wgate = jnp.einsum('td,tf->df', normed, d_gate, preferred_element_type=jnp.float32)
    d_win = jnp.einsum('td,tf->df', normed, d_up, preferred_element_type=jnp.float32)
    d_normed = jnp.einsum('tf,df->td', d_gate, w_gate, preferred_element_type=jnp.float32) + jnp.einsum('tf,df->td', d_up, w_in, preferred_element_type=jnp.float32)
    d_resid = rms_pull(d_normed)[0]
    d_prev = (d_next.astype(jnp.float32) + d_resid).astype(jnp.bfloat16)
    return d_prev, d_wgate, d_win, d_wout


def solution(mesh):
    stages = mesh.shape['stage']
    act_spec = P(None, 'data', None, None)
    weight_spec = P('stage', None, 'data', None)
    fwd_pairs = [(source_id, source_id + 1) for source_id in range(stages - 1)]
    bwd_pairs = [(source_id + 1, source_id) for source_id in range(stages - 1)]

    def per_device(x, g, w_gate, w_in, w_out):
        n_micro, batch_mb, seq_len, dmodel = x.shape
        layers = w_gate.shape[1]
        ffn_dim = w_gate.shape[3]
        row_count = batch_mb * seq_len
        stage_idx = lax.axis_index('stage')
        x_micro = x.reshape(n_micro, row_count, dmodel)
        g_micro = g.reshape(n_micro, row_count, dmodel)
        n_ticks = n_micro + stages - 1

        gate_full = lax.all_gather(w_gate[0], 'data', axis=1, tiled=True)
        in_full = lax.all_gather(w_in[0], 'data', axis=1, tiled=True)
        out_full = lax.all_gather(w_out[0], 'data', axis=1, tiled=True)

        def fwd_tick(loop_state, tick_id):
            received, saved_in = loop_state
            micro_id = tick_id - stage_idx
            is_valid = (micro_id >= 0) & (micro_id < n_micro)
            micro_slot = jnp.clip(micro_id, 0, n_micro - 1)
            fresh_in = lax.dynamic_index_in_dim(x_micro, micro_slot, 0, keepdims=False)
            block_in = jnp.where(stage_idx == 0, fresh_in, received)

            def run_stage(operands):
                tokens, stored_in = operands
                layer_inputs = []
                for layer_id in range(layers):
                    layer_inputs.append(tokens)
                    tokens = layer_fwd(tokens, gate_full[layer_id], in_full[layer_id], out_full[layer_id])
                stored_in = lax.dynamic_update_index_in_dim(stored_in, jnp.stack(layer_inputs), micro_slot, 0)
                return tokens, stored_in

            def skip_stage(operands):
                return operands

            block_out, saved_in = lax.cond(is_valid, run_stage, skip_stage, (block_in, saved_in))
            sent_out = lax.ppermute(block_out, 'stage', fwd_pairs)
            return (sent_out, saved_in), None

        saved_init = jnp.zeros((n_micro, layers, row_count, dmodel), jnp.bfloat16)
        recv_init = jnp.zeros((row_count, dmodel), jnp.bfloat16)
        (_, saved_in), _ = lax.scan(fwd_tick, (recv_init, saved_init), jnp.arange(n_ticks))

        gate_shard, in_shard, out_shard, saved_in = lax.optimization_barrier((w_gate[0], w_in[0], w_out[0], saved_in))
        gate_back = lax.all_gather(gate_shard, 'data', axis=1, tiled=True)
        in_back = lax.all_gather(in_shard, 'data', axis=1, tiled=True)
        out_back = lax.all_gather(out_shard, 'data', axis=1, tiled=True)

        def bwd_tick(loop_state, tick_id):
            received, grad_sums, dx_buf = loop_state
            micro_id = tick_id - (stages - 1 - stage_idx)
            is_valid = (micro_id >= 0) & (micro_id < n_micro)
            micro_slot = jnp.clip(micro_id, 0, n_micro - 1)
            fresh_in = lax.dynamic_index_in_dim(g_micro, micro_slot, 0, keepdims=False)
            d_out = jnp.where(stage_idx == stages - 1, fresh_in, received)

            def run_stage(operands):
                d_cur, old_sums, dx_store = operands
                layer_inputs = lax.dynamic_index_in_dim(saved_in, micro_slot, 0, keepdims=False)
                gate_sums = list(old_sums[0])
                in_sums = list(old_sums[1])
                out_sums = list(old_sums[2])
                for layer_id in reversed(range(layers)):
                    d_cur, d_wgate, d_win, d_wout = layer_bwd(layer_inputs[layer_id], d_cur, gate_back[layer_id], in_back[layer_id], out_back[layer_id])
                    gate_sums[layer_id] = gate_sums[layer_id] + d_wgate
                    in_sums[layer_id] = in_sums[layer_id] + d_win
                    out_sums[layer_id] = out_sums[layer_id] + d_wout
                dx_store = lax.dynamic_update_index_in_dim(dx_store, d_cur, micro_slot, 0)
                return d_cur, (tuple(gate_sums), tuple(in_sums), tuple(out_sums)), dx_store

            def skip_stage(operands):
                return operands

            d_in, grad_sums, dx_buf = lax.cond(is_valid, run_stage, skip_stage, (d_out, grad_sums, dx_buf))
            sent_out = lax.ppermute(d_in, 'stage', bwd_pairs)
            return (sent_out, grad_sums, dx_buf), None

        zero_up = jnp.zeros((dmodel, ffn_dim), jnp.float32)
        zero_down = jnp.zeros((ffn_dim, dmodel), jnp.float32)
        grad_init = (tuple(zero_up for _ in range(layers)), tuple(zero_up for _ in range(layers)), tuple(zero_down for _ in range(layers)))
        dx_init = jnp.zeros((n_micro, row_count, dmodel), jnp.bfloat16)
        (_, grad_sums, dx_buf), _ = lax.scan(bwd_tick, (recv_init, grad_init, dx_init), jnp.arange(n_ticks))

        gate_grad = lax.psum_scatter(jnp.stack(grad_sums[0]), 'data', scatter_dimension=1, tiled=True)
        in_grad = lax.psum_scatter(jnp.stack(grad_sums[1]), 'data', scatter_dimension=1, tiled=True)
        out_grad = lax.psum_scatter(jnp.stack(grad_sums[2]), 'data', scatter_dimension=1, tiled=True)
        dx_own = jnp.where(stage_idx == 0, dx_buf, jnp.zeros_like(dx_buf))
        d_x = lax.psum(dx_own, 'stage').reshape(x.shape)
        return d_x, gate_grad[None], in_grad[None], out_grad[None]

    return jax.shard_map(per_device, mesh=mesh, in_specs=(act_spec, act_spec, weight_spec, weight_spec, weight_spec), out_specs=(act_spec, weight_spec, weight_spec, weight_spec), check_vma=False)
```

profile of v0, /device:TPU:0, one launch (start us, length us, event | category | flops | bytes accessed | tf_op | source)
XLA Modules:
  0.0 5081.4 jit_solution(11531503241194693269)
XLA Ops:
  9.4 294.8 %all-gather.16.cloned.1.call-done = bf16[1,1,2048,8192]{3,2,1,0:T(8,128)(2,1)} async-done(((bf16[1,1,512,8192]{3,2,1,0:T(8,128)(2,1)}), bf16[1,1,2048,8192]{3,2,1,0:T(8,128)(2,1)}) %all-gather.16.cloned.1.call-update) | async-done | bytes 33554448 | tf_op jit(solution)/shard_map/all_gather | solution.py:57
  304.2 293.4 %all-gather.18.cloned.1.call-done = bf16[1,1,2048,8192]{3,2,1,0:T(8,128)(2,1)} async-done(((bf16[1,1,512,8192]{3,2,1,0:T(8,128)(2,1)}), bf16[1,1,2048,8192]{3,2,1,0:T(8,128)(2,1)}) %all-gather.18.cloned.1.call-update) | async-done | bytes 33554448 | tf_op jit(solution)/shard_map/all_gather | solution.py:58
  597.6 293.4 %all-gather.20.cloned.1.call-done = bf16[1,1,8192,2048]{3,2,1,0:T(8,128)(2,1)} async-done(((bf16[1,1,2048,2048]{3,2,1,0:T(8,128)(2,1)}), bf16[1,1,8192,2048]{3,2,1,0:T(8,128)(2,1)}) %all-gather.20.cloned.1.call-update) | async-done | bytes 33554448 | tf_op jit(solution)/shard_map/all_gather | solution.py:59
  893.6 268.6 %while.33 = (s32[]{:T(128)}, bf16[256,2048]{1,0:T(8,128)(2,1)S(1)}, bf16[4,1,256,2048]{3,2,1,0:T(8,128)(2,1)}, s32[5]{0:T(128)S(1)}, s32[]{:T(128)}, /*index=5*/...) while((s32[]{:T(128)}, bf16[256,2048]{1,0:T(8,128)(2,1)S(1)}, ...), condition=%wide.region_4.5_spmd, body=%wide.region_0.4_spmd.sunk | while | flops 25790251008 | bytes 131077480 | solution.py:87
  1111.0 49.0 collective-permute-start
  1163.5 290.5 %all-gather.10.cloned.1.call-done = bf16[1,8192,2048]{2,1,0:T(8,128)(2,1)} async-done(((bf16[1,2048,2048]{2,1,0:T(8,128)(2,1)}), bf16[1,8192,2048]{2,1,0:T(8,128)(2,1)}) %all-gather.10.cloned.1.call-update) | async-done | bytes 33554448 | tf_op jit(solution)/shard_map/all_gather | solution.py:92
  1454.0 293.2 %all-gather.12.cloned.1.call-done = bf16[1,2048,8192]{2,1,0:T(8,128)(2,1)} async-done(((bf16[1,512,8192]{2,1,0:T(8,128)(2,1)}), bf16[1,2048,8192]{2,1,0:T(8,128)(2,1)}) %all-gather.12.cloned.1.call-update) | async-done | bytes 33554448 | tf_op jit(solution)/shard_map/all_gather | solution.py:91
  1747.3 293.2 %all-gather.14.cloned.1.call-done = bf16[1,2048,8192]{2,1,0:T(8,128)(2,1)} async-done(((bf16[1,512,8192]{2,1,0:T(8,128)(2,1)}), bf16[1,2048,8192]{2,1,0:T(8,128)(2,1)}) %all-gather.14.cloned.1.call-update) | async-done | bytes 33554448 | tf_op jit(solution)/shard_map/all_gather | solution.py:90
  2107.2 1267.1 %while.34 = (s32[]{:T(128)}, bf16[256,2048]{1,0:T(8,128)(2,1)S(1)}, f32[2048,8192]{1,0:T(8,128)}, f32[2048,8192]{1,0:T(8,128)}, f32[8192,2048]{1,0:T(8,128)}, /*...) while((s32[]{:T(128)}, bf16[256,2048]{1,0:T(8,128)(2,1)S(1)}, ...), condition=%wide.region_10.11_spmd, body=%wide.region_5.10_spmd.sunk | while | flops 68824334336 | bytes 674248192 | solution.py:127
  2112.7 246.7 %collective-permute-done.1 = bf16[256,2048]{1,0:T(8,128)(2,1)S(1)} collective-permute-done((bf16[256,2048]{1,0:T(8,128)(2,1)}, bf16[256,2048]{1,0:T(8,128)(2,1)S(1)}, u32[]{:S(2)}, u32[]{:S(2)}) %collective-permute-start.1) | collective-permute-done | bytes 1048608 | tf_op jit(solution)/shard_map/while/body/eval_jaxpr/ppermute | solution.py:120
  2362.6 246.0 %conditional.5 = (bf16[256,2048]{1,0:T(8,128)(2,1)}, f32[2048,8192]{1,0:T(8,128)}, f32[2048,8192]{1,0:T(8,128)}, f32[8192,2048]{1,0:T(8,128)}, bf16[4,256,2048]{2,1,0:T(8,128)(2,1)}) conditional(s32[]{:T(128)} %convert_element_type.135, (bf16[256,2048]{1,0:T(8,128)(2,1)S(1)}, f32[2048,8192]{1,0:T(8,128)}, f32[2048,8192]{1,0:T(8,128)}, ...), branch_computations={%region_6.6_spmd, %region_7.9_spmd} | conditional | flops 68823810048 | bytes 666907776 | solution.py:119
  2457.7 54.4 %convolution_add_fusion.2 = f32[8192,2048]{1,0:T(8,128)} fusion(f32[8192,2048]{1,0:T(8,128)} %get-tuple-element.291, bf16[256,2048]{1,0:T(8,128)(2,1)S(1)} %get-tuple-element.283, f32[256,8192]{1,0:T(8,128)} %fusion.43, f32[256,8192]{1,0:T(8,128)} %fusion.39), kind=kOutput, calls=%fused_computation.36 | convolution fusion | flops 8619294720 | bytes 152043520 | tf_op jit(solution)/shard_map/while/body/eval_jaxpr/cond/branch_1_fun/tf,td->fd/dot_general | solution.py:28
  2512.1 48.3 convolution_add_fusion
  2616.4 246.0 %conditional.5 = (bf16[256,2048]{1,0:T(8,128)(2,1)}, f32[2048,8192]{1,0:T(8,128)}, f32[2048,8192]{1,0:T(8,128)}, f32[8192,2048]{1,0:T(8,128)}, bf16[4,256,2048]{2,1,0:T(8,128)(2,1)}) conditional(s32[]{:T(128)} %convert_element_type.135, (bf16[256,2048]{1,0:T(8,128)(2,1)S(1)}, f32[2048,8192]{1,0:T(8,128)}, f32[2048,8192]{1,0:T(8,128)}, ...), branch_computations={%region_6.6_spmd, %region_7.9_spmd} | conditional | flops 68823810048 | bytes 666907776 | solution.py:119
  2711.4 54.4 %convolution_add_fusion.2 = f32[8192,2048]{1,0:T(8,128)} fusion(f32[8192,2048]{1,0:T(8,128)} %get-tuple-element.291, bf16[256,2048]{1,0:T(8,128)(2,1)S(1)} %get-tuple-element.283, f32[256,8192]{1,0:T(8,128)} %fusion.43, f32[256,8192]{1,0:T(8,128)} %fusion.39), kind=kOutput, calls=%fused_computation.36 | convolution fusion | flops 8619294720 | bytes 152043520 | tf_op jit(solution)/shard_map/while/body/eval_jaxpr/cond/branch_1_fun/tf,td->fd/dot_general | solution.py:28
  2765.8 48.3 convolution_add_fusion
  2870.1 246.0 %conditional.5 = (bf16[256,2048]{1,0:T(8,128)(2,1)}, f32[2048,8192]{1,0:T(8,128)}, f32[2048,8192]{1,0:T(8,128)}, f32[8192,2048]{1,0:T(8,128)}, bf16[4,256,2048]{2,1,0:T(8,128)(2,1)}) conditional(s32[]{:T(128)} %convert_element_type.135, (bf16[256,2048]{1,0:T(8,128)(2,1)S(1)}, f32[2048,8192]{1,0:T(8,128)}, f32[2048,8192]{1,0:T(8,128)}, ...), branch_computations={%region_6.6_spmd, %region_7.9_spmd} | conditional | flops 68823810048 | bytes 666907776 | solution.py:119
  2965.1 54.4 %convolution_add_fusion.2 = f32[8192,2048]{1,0:T(8,128)} fusion(f32[8192,2048]{1,0:T(8,128)} %get-tuple-element.291, bf16[256,2048]{1,0:T(8,128)(2,1)S(1)} %get-tuple-element.283, f32[256,8192]{1,0:T(8,128)} %fusion.43, f32[256,8192]{1,0:T(8,128)} %fusion.39), kind=kOutput, calls=%fused_computation.36 | convolution fusion | flops 8619294720 | bytes 152043520 | tf_op jit(solution)/shard_map/while/body/eval_jaxpr/cond/branch_1_fun/tf,td->fd/dot_general | solution.py:28
  3019.5 48.3 convolution_add_fusion
  3123.8 246.0 %conditional.5 = (bf16[256,2048]{1,0:T(8,128)(2,1)}, f32[2048,8192]{1,0:T(8,128)}, f32[2048,8192]{1,0:T(8,128)}, f32[8192,2048]{1,0:T(8,128)}, bf16[4,256,2048]{2,1,0:T(8,128)(2,1)}) conditional(s32[]{:T(128)} %convert_element_type.135, (bf16[256,2048]{1,0:T(8,128)(2,1)S(1)}, f32[2048,8192]{1,0:T(8,128)}, f32[2048,8192]{1,0:T(8,128)}, ...), branch_computations={%region_6.6_spmd, %region_7.9_spmd} | conditional | flops 68823810048 | bytes 666907776 | solution.py:119
  3218.9 54.4 %convolution_add_fusion.2 = f32[8192,2048]{1,0:T(8,128)} fusion(f32[8192,2048]{1,0:T(8,128)} %get-tuple-element.291, bf16[256,2048]{1,0:T(8,128)(2,1)S(1)} %get-tuple-element.283, f32[256,8192]{1,0:T(8,128)} %fusion.43, f32[256,8192]{1,0:T(8,128)} %fusion.39), kind=kOutput, calls=%fused_computation.36 | convolution fusion | flops 8619294720 | bytes 152043520 | tf_op jit(solution)/shard_map/while/body/eval_jaxpr/cond/branch_1_fun/tf,td->fd/dot_general | solution.py:28
  3400.7 557.2 %reduce-scatter.14.cloned.1.call-done = f32[1,32,131072]{2,1,0:T(8,128)} async-done(((f32[1,128,131072]{2,1,0:T(8,128)}), f32[1,32,131072]{2,1,0:T(8,128)}) %reduce-scatter.14.cloned.1.call-update) | async-done | bytes 16777232
  3957.9 556.0 %reduce-scatter.10.cloned.1.call-done = f32[1,32,131072]{2,1,0:T(8,128)} async-done(((f32[1,128,131072]{2,1,0:T(8,128)}), f32[1,32,131072]{2,1,0:T(8,128)}) %reduce-scatter.10.cloned.1.call-update) | async-done | bytes 16777232
  4513.9 555.9 %reduce-scatter.12.cloned.1.call-done = f32[1,32,131072]{2,1,0:T(8,128)} async-done(((f32[1,128,131072]{2,1,0:T(8,128)}), f32[1,32,131072]{2,1,0:T(8,128)}) %reduce-scatter.12.cloned.1.call-update) | async-done | bytes 16777232
  (139 shorter events, 1162.7 us)
Async XLA Ops:
  7.2 297.0 %all-gather.16.cloned.1.call-start = ((), (), s32[]{:S(2)}) async-start(), calls=%async_computation.7 | async-start | bytes 41943040 | tf_op jit(solution)/shard_map/all_gather | solution.py:57
  7.9 589.7 %all-gather.18.cloned.1.call-start = ((), (), s32[]{:S(2)}) async-start(), calls=%async_computation.8 | async-start | bytes 41943040 | tf_op jit(solution)/shard_map/all_gather | solution.py:58
  8.6 882.3 %all-gather.20.cloned.1.call-start = ((), (), s32[]{:S(2)}) async-start(), calls=%async_computation.9 | async-start | bytes 41943040 | tf_op jit(solution)/shard_map/all_gather | solution.py:59
  9.4 1444.6 %all-gather.10.cloned.1.call-start = ((), (), s32[]{:S(2)}) async-start(), calls=%async_computation.3 | async-start | bytes 41943040 | tf_op jit(solution)/shard_map/all_gather | solution.py:92
  943.0 3.6 collective-permute-start
  995.9 4.5 collective-permute-start
  1049.9 4.5 collective-permute-start
  1103.8 4.5 collective-permute-start
  1111.0 51.2 %collective-permute-start = (bf16[256,2048]{1,0:T(8,128)(2,1)S(1)}, bf16[256,2048]{1,0:T(8,128)(2,1)S(1)}, u32[]{:S(2)}, u32[]{:S(2)}) collective-permute-start(bf16[256,2048]{1,0:T(8,128)(2,1)S(1)} %get-tuple-element.528), channel_id=1, source_target_pairs={{0,1},{2,3},{4,5},{6,7}} | collective-permute-start | bytes 3145736 | tf_op jit(solution)/shard_map/while/body/eval_jaxpr/ppermute | solution.py:82
  1162.3 585.0 %all-gather.12.cloned.1.call-start = ((), (), s32[]{:S(2)}) async-start(), calls=%async_computation.4 | async-start | bytes 41943040 | tf_op jit(solution)/shard_map/all_gather | solution.py:91
  1162.9 877.6 %all-gather.14.cloned.1.call-start = ((), (), s32[]{:S(2)}) async-start(), calls=%async_computation.5 | async-start | bytes 41943040 | tf_op jit(solution)/shard_map/all_gather | solution.py:90
  1163.4 2237.2 %all-reduce.2.cloned.1.call-start = ((), (), s32[]{:S(2)}) async-start(), calls=%async_computation.6 | async-start | bytes 8388608 | tf_op jit(solution)/shard_map/psum | solution.py:133
  2111.5 248.0 %collective-permute-start.1 = (bf16[256,2048]{1,0:T(8,128)(2,1)}, bf16[256,2048]{1,0:T(8,128)(2,1)S(1)}, u32[]{:S(2)}, u32[]{:S(2)}) collective-permute-start(bf16[256,2048]{1,0:T(8,128)(2,1)} %get-tuple-element.544), channel_id=1, source_target_pairs={{1,0},{3,2},{5,4},{7,6}} | collective-permute-start | bytes 3145736 | tf_op jit(solution)/shard_map/while/body/eval_jaxpr/ppermute | solution.py:120
  2608.6 4.5 collective-permute-start.1
  2862.3 4.5 collective-permute-start.1
  3116.1 4.5 collective-permute-start.1
  3369.8 4.5 collective-permute-start.1
  3378.8 579.1 %reduce-scatter.14.cloned.1.call-start = ((), (), s32[]{:S(2)}) async-start(), calls=%async_computation.12 | async-start | bytes 83886080
  3379.6 1134.3 %reduce-scatter.10.cloned.1.call-start = ((), (), s32[]{:S(2)}) async-start(), calls=%async_computation.10 | async-start | bytes 83886080
  3380.3 1689.5 %reduce-scatter.12.cloned.1.call-start = ((), (), s32[]{:S(2)}) async-start(), calls=%async_computation.11 | async-start | bytes 83886080
Sparse Core Ops, SparseCore 0:
  9.7 294.4 all-gather.15
  306.0 291.5 all-gather.17
  599.4 291.5 all-gather.19
  1162.4 291.5 all-gather.9
  1455.6 291.5 all-gather.11
  1748.9 291.5 all-gather.13
  3378.9 21.6 all-reduce.1
  3404.2 553.5 reduce-scatter.13
  3961.4 552.4 reduce-scatter.9
  4517.3 552.4 reduce-scatter.11
where the time goes:
time: 5080 us
  waiting for transfers between devices  3720 us (73%)
  matrix products  1150 us (23%)
  local copies, waits for them, and re-layouts  88.4 us (2%)
  starting transfers between devices  64.1 us (1%)
    unnamed x13, waiting for transfers between devices  1670 us
    all_gather x1, waiting for transfers between devices, per_device(): gate_full = lax.all_gather(w_gate[0], 'data', axis=1, tiled=True)  295 us
    all_gather x1, waiting for transfers between devices, per_device(): out_full = lax.all_gather(w_out[0], 'data', axis=1, tiled=True)  293 us
    all_gather x1, waiting for transfers between devices, per_device(): in_full = lax.all_gather(w_in[0], 'data', axis=1, tiled=True)  293 us
    all_gather x1, waiting for transfers between devices, per_device(): gate_back = lax.all_gather(gate_shard, 'data', axis=1, tiled=True)  293 us
    all_gather x1, waiting for transfers between devices, per_device(): in_back = lax.all_gather(in_shard, 'data', axis=1, tiled=True)  293 us
    all_gather x1, waiting for transfers between devices, per_device(): out_back = lax.all_gather(out_shard, 'data', axis=1, tiled=True)  291 us
    ppermute x5, waiting for transfers between devices, bwd_tick(): sent_out = lax.ppermute(d_in, 'stage', bwd_pairs)  260 us
  transfers between devices with their start and end apart: 20, of which 20 were waited for; matrix products, arithmetic and copies ran while one was open for 0% of the time, Pallas kernels for 0%

commit v1 on v0

v1 whole, which is shorter than its diff:
```python
import jax
import jax.numpy as jnp
from jax import lax
from jax.sharding import PartitionSpec as P

N_CHUNKS = 2


def rms_f32(row_vals):
    return row_vals * lax.rsqrt(jnp.mean(row_vals * row_vals, axis=-1, keepdims=True) + 1e-6)


def mm(lhs, rhs, lhs_dim, rhs_dim):
    return lax.dot_general(lhs, rhs, (((lhs_dim,), (rhs_dim,)), ((), ())), preferred_element_type=jnp.float32)


def normed_of(tokens):
    return rms_f32(tokens.astype(jnp.float32)).astype(jnp.bfloat16)


def block_grads(normed, d_out, w_gate, w_in, w_out):
    pre_gate = mm(normed, w_gate, 1, 0)
    pre_in = mm(normed, w_in, 1, 0)
    d_hidden = mm(d_out, w_out, 1, 1)
    sigma = jax.nn.sigmoid(pre_gate)
    gate_act = pre_gate * sigma
    hidden = (gate_act * pre_in).astype(jnp.bfloat16)
    d_gate = (d_hidden * pre_in * sigma * (1.0 + pre_gate * (1.0 - sigma))).astype(jnp.bfloat16)
    d_up = (d_hidden * gate_act).astype(jnp.bfloat16)
    d_normed = mm(d_gate, w_gate, 1, 1) + mm(d_up, w_in, 1, 1)
    return hidden, d_gate, d_up, d_normed


def through_norm(tokens, d_out, d_normed):
    _, rms_pull = jax.vjp(rms_f32, tokens.astype(jnp.float32))
    return (d_out.astype(jnp.float32) + rms_pull(d_normed)[0]).astype(jnp.bfloat16)


def solution(mesh):
    chips = mesh.shape['data']
    act_spec = P(None, 'data', None, None)
    weight_spec = P('stage', None, 'data', None)

    def per_device(x, g, w_gate, w_in, w_out):
        n_micro, batch_mb, seq_len, dmodel = x.shape
        ffn = w_gate.shape[3]
        cols = ffn // chips
        core = lax.axis_index('stage')
        half = batch_mb * seq_len // 2
        per_chunk = n_micro // N_CHUNKS

        def columns_of(shard):
            pieces = lax.all_to_all(shard.reshape(-1, chips, cols), 'data', 1, 0)
            return lax.all_gather(pieces.reshape(-1, cols), 'stage')

        gate_all = columns_of(w_gate[0, 0])
        in_all = columns_of(w_in[0, 0])
        out_all = lax.all_gather(w_out[0, 0], 'stage')

        def my_rows(arr):
            rows = arr.reshape(n_micro, 2, half, dmodel)
            rows = lax.dynamic_index_in_dim(rows, core, 1, keepdims=False)
            return rows.reshape(N_CHUNKS, per_chunk * half, dmodel)

        def everywhere(rows):
            return lax.all_gather(rows, 'data', axis=0, tiled=True)

        def summed(partial):
            return lax.psum_scatter(partial, 'data', scatter_dimension=0, tiled=True)

        x_rows, g_rows = my_rows(x), my_rows(g)
        dx_rows = []
        saved = [[], []]
        for c in range(N_CHUNKS):
            x_all = everywhere(x_rows[c])
            n0 = normed_of(x_all)
            pre_gate = mm(n0, gate_all[0], 1, 0)
            pre_in = mm(n0, in_all[0], 1, 0)
            hidden = (pre_gate * jax.nn.sigmoid(pre_gate) * pre_in).astype(jnp.bfloat16)
            branch = summed(mm(hidden, out_all[0], 1, 0))
            h_rows = x_rows[c] + branch.astype(jnp.bfloat16)
            n1 = normed_of(everywhere(h_rows))
            g_all = everywhere(g_rows[c])
            hidden1, d_gate1, d_up1, d_n1 = block_grads(n1, g_all, gate_all[1], in_all[1], out_all[1])
            e_rows = through_norm(h_rows, g_rows[c], summed(d_n1))
            e_all = everywhere(e_rows)
            hidden0, d_gate0, d_up0, d_n0 = block_grads(n0, e_all, gate_all[0], in_all[0], out_all[0])
            dx_rows.append(through_norm(x_rows[c], e_rows, summed(d_n0)))
            saved[0].append((n0, e_all, hidden0, d_gate0, d_up0))
            saved[1].append((n1, g_all, hidden1, d_gate1, d_up1))

        d_parts = [[], [], []]
        for block in range(2):
            normed, d_out, hidden, d_gate, d_up = [jnp.concatenate(parts) for parts in zip(*saved[block])]
            d_parts[0].append(mm(normed, d_gate, 0, 0))
            d_parts[1].append(mm(normed, d_up, 0, 0))
            d_parts[2].append(mm(hidden, d_out, 0, 0))
        d_gate_w, d_in_w, d_out_w = [lax.psum_scatter(jnp.stack(parts), 'stage', scatter_dimension=0) for parts in d_parts]

        def rows_of(full):
            pieces = lax.all_to_all(full.reshape(chips, -1, cols), 'data', 0, 0)
            return pieces.transpose(1, 0, 2).reshape(1, 1, -1, ffn)

        dx = lax.all_gather(jnp.stack(dx_rows).reshape(n_micro, half, dmodel), 'stage', axis=1, tiled=True)
        return dx.reshape(x.shape), rows_of(d_gate_w), rows_of(d_in_w), d_out_w[None, None]

    return jax.shard_map(per_device, mesh=mesh, in_specs=(act_spec, act_spec, weight_spec, weight_spec, weight_spec),
                         out_specs=(act_spec, weight_spec, weight_spec, weight_spec), check_vma=False)
```

time: 5080 us -> 1710 us (0.34)
  waiting for transfers between devices: 3720 us -> 842 us
  matrix products: 1150 us -> 478 us
  blocking collectives: 0 us -> 99.8 us
  other arithmetic: 37.8 us -> 110 us
  local copies, waits for them, and re-layouts: 88.4 us -> 140 us
    unnamed x13 -> x21, waiting for transfers between devices: 1670 us -> 1.89 us
    all_gather x6 -> x12, waiting for transfers between devices: 1760 us -> 198 us  [the longest x8 181 us: everywhere(): return lax.all_gather(rows, 'data', axis=0, tiled=True)]
    dot_general x40 -> x28, matrix products: 1150 us -> 478 us  [mm(): lax.dot_general(lhs, rhs, (((lhs_dim,), (rhs_dim,)), ((), ())), preferred...]
    all_to_all x0 -> x3, waiting for transfers between devices: none -> 446 us  [the longest x2 322 us: rows_of(): pieces = lax.all_to_all(full.reshape(chips, -1, cols), 'data', 0, 0)]
    ppermute x10 -> x0, waiting for transfers between devices: 271 us -> none  [the longest x5 260 us: bwd_tick(): sent_out = lax.ppermute(d_in, 'stage', bwd_pairs)]
    reduce_scatter x0 -> x9, waiting for transfers between devices: none -> 196 us  [the longest x6 196 us: summed(): return lax.psum_scatter(partial, 'data', scatter_dimension=0, tiled=True)]
    all_to_all x0 -> x1, blocking collectives: none -> 99.8 us  [columns_of(): pieces = lax.all_to_all(shard.reshape(-1, chips, cols), 'data', 1, 0)]
    broadcast_in_dim x6 -> x0, local copies, waits for them, and re-layouts: 66.3 us -> none  [the longest x2 42.3 us: per_device(): zero_up = jnp.zeros((dmodel, ffn_dim), jnp.float32)]
  transfers between devices with their start and end apart: 20 -> 24, of which waited for: 20 -> 15; matrix products, arithmetic and copies ran while one was open for 0% -> 41% of each run, Pallas kernels for 0% -> 0%
where the time goes in v1:
time: 1710 us
  waiting for transfers between devices  842 us (49%)
  matrix products  478 us (28%)
  local copies, waits for them, and re-layouts  140 us (8%)
  other arithmetic  110 us (6%)
  blocking collectives  99.8 us (6%)
  starting transfers between devices  22.1 us (1%)
    dot_general x28, matrix products, mm(): lax.dot_general(lhs, rhs, (((lhs_dim,), (rhs_dim,)), ((), ())), preferred...  478 us
    all_to_all x2, waiting for transfers between devices, rows_of(): pieces = lax.all_to_all(full.reshape(chips, -1, cols), 'data', 0, 0)  322 us
    reduce_scatter x6, waiting for transfers between devices, summed(): return lax.psum_scatter(partial, 'data', scatter_dimension=0, tiled=True)  196 us
    all_gather x8, waiting for transfers between devices, everywhere(): return lax.all_gather(rows, 'data', axis=0, tiled=True)  181 us
    all_to_all x1, waiting for transfers between devices, columns_of(): pieces = lax.all_to_all(shard.reshape(-1, chips, cols), 'data', 1, 0)  124 us
    all_to_all x1, blocking collectives, columns_of(): pieces = lax.all_to_all(shard.reshape(-1, chips, cols), 'data', 1, 0)  99.8 us
    another operation x3, other arithmetic, per_device(): jnp.stack(parts)  55.3 us
    transpose x2, local copies, waits for them, and re-layouts, rows_of(): return pieces.transpose(1, 0, 2).reshape(1, 1, -1, ffn)  41.8 us
  transfers between devices with their start and end apart: 24, of which 15 were waited for; matrix products, arithmetic and copies ran while one was open for 41% of the time, Pallas kernels for 0%

profile of v1, /device:TPU:0, one launch (start us, length us, event | category | flops | bytes accessed | tf_op | source)
XLA Modules:
  0.0 1706.5 jit_solution(8816182770625113659)
XLA Ops:
  28.6 123.9 %all-to-all-done = bf16[1,512,4,2048]{1,3,0,2:T(8,128)(2,1)} async-done(((bf16[1,512,4,2048]{1,3,0,2:T(8,128)(2,1)}), bf16[1,512,4,2048]{1,3,0,2:T(8,128)(2,1)}, u32[]{:S(2)}, u32[]{:S(2)}) %all-to-all-start) | async-done | bytes 8388640 | tf_op jit(solution)/shard_map/all_to_all | solution.py:53
  175.8 99.8 %all_to_all.40 = bf16[1,512,4,2048]{1,3,0,2:T(8,128)(2,1)} all-to-all(bf16[1,512,4,2048]{1,3,0,2:T(8,128)(2,1)} %bitcast.158), channel_id=1, replica_groups=mesh['data'=4,'stage'=2] {'data'}, dimensions={2} | all-to-all | bytes 16777216 | tf_op jit(solution)/shard_map/all_to_all | solution.py:53
  362.7 31.6 %all-gather.16.cloned.1.call-done = bf16[1024,2048]{1,0:T(8,128)(2,1)} async-done(((bf16[256,2048]{1,0:T(8,128)(2,1)}), bf16[1024,2048]{1,0:T(8,128)(2,1)}) %all-gather.16.cloned.1.call-update) | async-done | bytes 4194320 | tf_op jit(solution)/shard_map/all_gather | solution.py:66
  445.4 32.9 %reduce-scatter.16.cloned.1.call-done = f32[256,2048]{1,0:T(8,128)} async-done(((f32[1024,2048]{1,0:T(8,128)}), f32[256,2048]{1,0:T(8,128)}) %reduce-scatter.16.cloned.1.call-update) | async-done | bytes 2097168 | tf_op jit(solution)/shard_map/reduce_scatter | solution.py:69
  482.1 44.6 %all-gather.26.cloned.1.call-done = bf16[1024,2048]{1,0:T(8,128)(2,1)} async-done(((bf16[256,2048]{1,0:T(8,128)(2,1)}), bf16[1024,2048]{1,0:T(8,128)(2,1)}) %all-gather.26.cloned.1.call-update) | async-done | bytes 4194320 | tf_op jit(solution)/shard_map/all_gather | solution.py:66
  541.2 69.1 %reduce-scatter.10.cloned.1.call-done = f32[256,2048]{1,0:T(8,128)} async-done(((f32[1024,2048]{1,0:T(8,128)}), f32[256,2048]{1,0:T(8,128)}) %reduce-scatter.10.cloned.1.call-update) | async-done | bytes 2097168 | tf_op jit(solution)/shard_map/reduce_scatter | solution.py:69
  613.1 45.7 %all-gather.30.cloned.1.call-done = bf16[1024,2048]{1,0:T(8,128)(2,1)} async-done(((bf16[256,2048]{1,0:T(8,128)(2,1)}), bf16[1024,2048]{1,0:T(8,128)(2,1)}) %all-gather.30.cloned.1.call-update) | async-done | bytes 4194320 | tf_op jit(solution)/shard_map/all_gather | solution.py:66
  679.6 20.3 %multiply_convert_fusion = (bf16[1024,2048]{1,0:T(8,128)(2,1)}, bf16[1024,2048]{1,0:T(8,128)(2,1)}, bf16[1024,2048]{1,0:T(8,128)(2,1)}) fusion(f32[1024,2048]{1,0:T(8,128)} %fusion.55, f32[1024,2048]{1,0:T(8,128)} %fusion.36, bf16[1024,2048]{1,0:T(8,128)(2,1)S(1)} %fusion.7, bf16[2,2048,2048]{2,1,0:T(8,128)(2,1)} %all-gather.20.cloned.1.call-done), kind=kOutput, calls=%fused_computation.57 | convolution fusion | flops 8621391872 | bytes 41943040 | tf_op jit(solution)/shard_map/dot_general | solution.py:14
  776.3 20.7 %multiply_convert_fusion.1 = (bf16[1024,2048]{1,0:T(8,128)(2,1)}, bf16[1024,2048]{1,0:T(8,128)(2,1)}, bf16[1024,2048]{1,0:T(8,128)(2,1)}) fusion(f32[1024,2048]{1,0:T(8,128)} %fusion.57, f32[1024,2048]{1,0:T(8,128)} %fusion.37, bf16[1024,2048]{1,0:T(8,128)(2,1)S(1)} %fusion.3, bf16[2,2048,2048]{2,1,0:T(8,128)(2,1)} %all-gather.20.cloned.1.call-done), kind=kOutput, calls=%fused_computation.58 | convolution fusion | flops 8621391872 | bytes 41943040 | tf_op jit(solution)/shard_map/dot_general | solution.py:14
  845.1 78.0 %reduce-scatter.12.cloned.1.call-done = f32[256,2048]{1,0:T(8,128)} async-done(((f32[1024,2048]{1,0:T(8,128)}), f32[256,2048]{1,0:T(8,128)}) %reduce-scatter.12.cloned.1.call-update) | async-done | bytes 2097168 | tf_op jit(solution)/shard_map/reduce_scatter | solution.py:69
  928.4 43.0 %all-gather.32.cloned.1.call-done = bf16[1024,2048]{1,0:T(8,128)(2,1)} async-done(((bf16[256,2048]{1,0:T(8,128)(2,1)}), bf16[1024,2048]{1,0:T(8,128)(2,1)}) %all-gather.32.cloned.1.call-update) | async-done | bytes 4194320 | tf_op jit(solution)/shard_map/all_gather | solution.py:66
  1019.7 19.8 %multiply_convert_fusion.7 = (bf16[1024,2048]{1,0:T(8,128)(2,1)}, bf16[1024,2048]{1,0:T(8,128)(2,1)S(1)}) fusion(f32[1024,2048]{1,0:T(8,128)} %copy-done.15, f32[1024,2048]{1,0:T(8,128)} %get-tuple-element.37, bf16[1024,2048]{1,0:T(8,128)(2,1)} %all-gather.24.cloned.1.call-done, bf16[2,1,2048,2048]{3,2,1,0:T(8,128)(2,1)} %all-gather.36.cloned.1.call-done), kind=kOutput, calls=%fused_computation.68 | convolution fusion | flops 8617197568 | bytes 37748736 | tf_op jit(solution)/shard_map/dot_general | solution.py:14
  1066.6 23.2 %convolution_bitcast_fusion.2 = f32[1,2048,2048]{2,1,0:T(8,128)S(1)} fusion(bf16[1024,2048]{1,0:T(8,128)(2,1)} %get-tuple-element.17, bf16[1024,2048]{1,0:T(8,128)(2,1)} %get-tuple-element.14, bf16[1024,2048]{1,0:T(8,128)(2,1)} %copy-done.11, bf16[1024,2048]{1,0:T(8,128)(2,1)} %copy-done.12), kind=kOutput, calls=%fused_computation.13 | convolution fusion | flops 17213423616 | bytes 33554432 | tf_op jit(solution)/shard_map/dot_general | solution.py:14
  1089.8 24.5 %convolution_bitcast_fusion.3 = f32[1,2048,2048]{2,1,0:T(8,128)} fusion(bf16[1024,2048]{1,0:T(8,128)(2,1)} %get-tuple-element.20, bf16[1024,2048]{1,0:T(8,128)(2,1)} %get-tuple-element.18, bf16[1024,2048]{1,0:T(8,128)(2,1)} %fusion.5, bf16[1024,2048]{1,0:T(8,128)(2,1)} %copy-done.10), kind=kOutput, calls=%fused_computation.14 | convolution fusion | flops 17213423616 | bytes 33554432 | tf_op jit(solution)/shard_map/dot_general | solution.py:14
  1132.7 23.4 %convolution_bitcast_fusion.4 = f32[1,2048,2048]{2,1,0:T(8,128)S(1)} fusion(bf16[1024,2048]{1,0:T(8,128)(2,1)} %get-tuple-element.16, bf16[1024,2048]{1,0:T(8,128)(2,1)} %get-tuple-element.13, bf16[1024,2048]{1,0:T(8,128)(2,1)} %copy-done.11, bf16[1024,2048]{1,0:T(8,128)(2,1)} %copy-done.12), kind=kOutput, calls=%fused_computation.15 | convolution fusion | flops 17213423616 | bytes 33554432 | tf_op jit(solution)/shard_map/dot_general | solution.py:14
  1156.1 24.5 %convolution_bitcast_fusion.5 = f32[1,2048,2048]{2,1,0:T(8,128)} fusion(bf16[1024,2048]{1,0:T(8,128)(2,1)} %copy-done.19, bf16[1024,2048]{1,0:T(8,128)(2,1)} %copy-done.21, bf16[1024,2048]{1,0:T(8,128)(2,1)} %fusion.5, bf16[1024,2048]{1,0:T(8,128)(2,1)} %copy-done.10), kind=kOutput, calls=%fused_computation.16 | convolution fusion | flops 17213423616 | bytes 33554432 | tf_op jit(solution)/shard_map/dot_general | solution.py:14
  1208.8 23.4 %convolution_bitcast_fusion = f32[1,2048,2048]{2,1,0:T(8,128)S(1)} fusion(bf16[1024,2048]{1,0:T(8,128)(2,1)} %get-tuple-element.15, bf16[1024,2048]{1,0:T(8,128)(2,1)} %get-tuple-element.12, bf16[1024,2048]{1,0:T(8,128)(2,1)} %all-gather.26.cloned.1.call-done, bf16[1024,2048]{1,0:T(8,128)(2,1)} %all-gather.14.cloned.1.call-done), kind=kOutput, calls=%fused_computation.11 | convolution fusion | flops 17213423616 | bytes 33554432 | tf_op jit(solution)/shard_map/dot_general | solution.py:14
  1232.3 24.5 %convolution_bitcast_fusion.1 = f32[1,2048,2048]{2,1,0:T(8,128)} fusion(bf16[1024,2048]{1,0:T(8,128)(2,1)} %get-tuple-element.34, bf16[1024,2048]{1,0:T(8,128)(2,1)} %copy-done.16, bf16[1024,2048]{1,0:T(8,128)(2,1)} %all-gather.32.cloned.1.call-done, bf16[1024,2048]{1,0:T(8,128)(2,1)} %all-gather.24.cloned.1.call-done), kind=kOutput, calls=%fused_computation.12 | convolution fusion | flops 17213423616 | bytes 33554432 | tf_op jit(solution)/shard_map/dot_general | solution.py:14
  1282.3 182.2 %all-to-all-done.3 = f32[4,512,2048]{2,1,0:T(8,128)} async-done(((f32[4,512,2048]{2,1,0:T(8,128)}), f32[4,512,2048]{2,1,0:T(8,128)}, u32[]{:S(2)}, u32[]{:S(2)}) %all-to-all-start.3) | async-done | bytes 16777248 | tf_op jit(solution)/shard_map/all_to_all | solution.py:101
  1471.8 20.9 %copy.34 = f32[512,4,2048]{2,1,0:T(4,128)} copy(f32[512,4,2048]{2,0,1:T(8,128)} %bitcast.35) | data formatting | bytes 33554432 | tf_op jit(solution)/shard_map/transpose | solution.py:102
  1492.7 20.5 %reshape.161 = f32[1,1,512,8192]{3,2,1,0:T(8,128)} reshape(f32[512,4,2048]{2,1,0:T(4,128)} %copy.34) | data formatting | bytes 33554432 | tf_op jit(solution)/shard_map/reshape | solution.py:102
  1513.2 140.0 %all-to-all-done.2 = f32[4,512,2048]{2,1,0:T(8,128)} async-done(((f32[4,512,2048]{2,1,0:T(8,128)}), f32[4,512,2048]{2,1,0:T(8,128)}, u32[]{:S(2)}, u32[]{:S(2)}) %all-to-all-start.2) | async-done | bytes 16777248 | tf_op jit(solution)/shard_map/all_to_all | solution.py:101
  1653.2 20.9 %copy.33 = f32[512,4,2048]{2,1,0:T(4,128)} copy(f32[512,4,2048]{2,0,1:T(8,128)} %bitcast.31) | data formatting | bytes 33554432 | tf_op jit(solution)/shard_map/transpose | solution.py:102
  1674.1 20.5 %reshape.160 = f32[1,1,512,8192]{3,2,1,0:T(8,128)} reshape(f32[512,4,2048]{2,1,0:T(4,128)} %copy.33) | data formatting | bytes 33554432 | tf_op jit(solution)/shard_map/reshape | solution.py:102
  (161 shorter events, 513.7 us)
Async XLA Ops:
  19.1 133.4 %all-to-all-start = ((bf16[1,512,4,2048]{1,3,0,2:T(8,128)(2,1)}), bf16[1,512,4,2048]{1,3,0,2:T(8,128)(2,1)}, u32[]{:S(2)}, u32[]{:S(2)}) async-start(bf16[1,512,4,2048]{1,3,0,2:T(8,128)(2,1)} %bitcast.157), calls=%async_computation | async-start | bytes 16777216 | tf_op jit(solution)/shard_map/all_to_all | solution.py:53
  24.8 263.9 %all-gather.28.cloned.1.call-start = ((), (), s32[]{:S(2)}) async-start(), calls=%async_computation.23 | async-start | bytes 5242880 | tf_op jit(solution)/shard_map/all_gather | solution.py:66
  28.6 268.2 %all-gather.18.cloned.1.call-start = ((), (), s32[]{:S(2)}) async-start(), calls=%async_computation.15 | async-start | bytes 25165824 | tf_op jit(solution)/shard_map/all_gather | solution.py:54
  163.9 150.5 %all-gather.20.cloned.1.call-start = ((), (), s32[]{:S(2)}) async-start(), calls=%async_computation.16 | async-start | bytes 25165824 | tf_op jit(solution)/shard_map/all_gather | solution.py:54
  287.0 57.8 %all-gather.36.cloned.1.call-start = ((), (), s32[]{:S(2)}) async-start(), calls=%async_computation.33 | async-start | bytes 25165824 | tf_op jit(solution)/shard_map/all_gather | solution.py:58
  287.5 106.7 %all-gather.16.cloned.1.call-start = ((), (), s32[]{:S(2)}) async-start(), calls=%async_computation.14 | async-start | bytes 5242880 | tf_op jit(solution)/shard_map/all_gather | solution.py:66
  288.1 190.1 %reduce-scatter.16.cloned.1.call-start = ((), (), s32[]{:S(2)}) async-start(), calls=%async_computation.24 | async-start | bytes 10485760 | tf_op jit(solution)/shard_map/reduce_scatter | solution.py:69
  359.3 167.4 %all-gather.26.cloned.1.call-start = ((), (), s32[]{:S(2)}) async-start(), calls=%async_computation.22 | async-start | bytes 5242880 | tf_op jit(solution)/shard_map/all_gather | solution.py:66
  362.4 247.8 %reduce-scatter.10.cloned.1.call-start = ((), (), s32[]{:S(2)}) async-start(), calls=%async_computation.17 | async-start | bytes 10485760 | tf_op jit(solution)/shard_map/reduce_scatter | solution.py:69
  445.3 213.4 %all-gather.30.cloned.1.call-start = ((), (), s32[]{:S(2)}) async-start(), calls=%async_computation.25 | async-start | bytes 5242880 | tf_op jit(solution)/shard_map/all_gather | solution.py:66
  481.0 245.3 %all-gather.14.cloned.1.call-start = ((), (), s32[]{:S(2)}) async-start(), calls=%async_computation.13 | async-start | bytes 5242880 | tf_op jit(solution)/shard_map/all_gather | solution.py:66
  481.6 273.9 %all-gather.22.cloned.1.call-start = ((), (), s32[]{:S(2)}) async-start(), calls=%async_computation.18 | async-start | bytes 5242880 | tf_op jit(solution)/shard_map/all_gather | solution.py:66
  613.0 226.5 %reduce-scatter.18.cloned.1.call-start = ((), (), s32[]{:S(2)}) async-start(), calls=%async_computation.26 | async-start | bytes 10485760 | tf_op jit(solution)/shard_map/reduce_scatter | solution.py:69
  726.3 196.9 %reduce-scatter.12.cloned.1.call-start = ((), (), s32[]{:S(2)}) async-start(), calls=%async_computation.19 | async-start | bytes 10485760 | tf_op jit(solution)/shard_map/reduce_scatter | solution.py:69
  823.2 148.2 %all-gather.32.cloned.1.call-start = ((), (), s32[]{:S(2)}) async-start(), calls=%async_computation.27 | async-start | bytes 5242880 | tf_op jit(solution)/shard_map/all_gather | solution.py:66
  845.1 174.7 %all-gather.24.cloned.1.call-start = ((), (), s32[]{:S(2)}) async-start(), calls=%async_computation.20 | async-start | bytes 5242880 | tf_op jit(solution)/shard_map/all_gather | solution.py:66
  928.4 270.8 %reduce-scatter.20.cloned.1.call-start = ((), (), s32[]{:S(2)}) async-start(), calls=%async_computation.28 | async-start | bytes 10485760 | tf_op jit(solution)/shard_map/reduce_scatter | solution.py:69
  1018.0 184.2 %reduce-scatter.14.cloned.1.call-start = ((), (), s32[]{:S(2)}) async-start(), calls=%async_computation.21 | async-start | bytes 10485760 | tf_op jit(solution)/shard_map/reduce_scatter | solution.py:69
  1066.5 208.7 %reduce-scatter.24.cloned.1.call-start = ((), (), s32[]{:S(2)}) async-start(), calls=%async_computation.31 | async-start | bytes 50331648 | tf_op jit(solution)/shard_map/reduce_scatter | solution.py:98
  1132.6 149.6 %reduce-scatter.22.cloned.1.call-start = ((), (), s32[]{:S(2)}) async-start(), calls=%async_computation.30 | async-start | bytes 50331648 | tf_op jit(solution)/shard_map/reduce_scatter | solution.py:98
  1199.2 272.6 %all-gather.34.cloned.1.call-start = ((), (), s32[]{:S(2)}) async-start(), calls=%async_computation.29 | async-start | bytes 6291456 | tf_op jit(solution)/shard_map/all_gather | solution.py:104
  1208.8 485.8 %reduce-scatter.26.cloned.1.call-start = ((), (), s32[]{:S(2)}) async-start(), calls=%async_computation.32 | async-start | bytes 50331648 | tf_op jit(solution)/shard_map/reduce_scatter | solution.py:98
  1275.2 189.3 %all-to-all-start.3 = ((f32[4,512,2048]{2,1,0:T(8,128)}), f32[4,512,2048]{2,1,0:T(8,128)}, u32[]{:S(2)}, u32[]{:S(2)}) async-start(f32[4,512,2048]{2,1,0:T(8,128)} %bitcast.161), calls=%async_computation.11 | async-start | bytes 33554432 | tf_op jit(solution)/shard_map/all_to_all | solution.py:101
  1464.5 188.7 %all-to-all-start.2 = ((f32[4,512,2048]{2,1,0:T(8,128)}), f32[4,512,2048]{2,1,0:T(8,128)}, u32[]{:S(2)}, u32[]{:S(2)}) async-start(f32[4,512,2048]{2,1,0:T(8,128)} %bitcast.162), calls=%async_computation.9 | async-start | bytes 33554432 | tf_op jit(solution)/shard_map/all_to_all | solution.py:101
  (23 other events, 545.4 us)
Sparse Core Ops, SparseCore 0:
  28.7 117.5 all-gather.27
  164.0 27.9 all-gather.17
  287.1 27.2 all-gather.19
  315.8 28.9 all-gather.35
  346.4 47.8 all-gather.15
  397.7 80.5 reduce-scatter.15
  480.0 46.6 all-gather.25
  529.7 80.5 reduce-scatter.9
  612.1 46.6 all-gather.29
  660.4 46.6 all-gather.13
  708.8 46.6 all-gather.21
  758.9 80.5 reduce-scatter.17
  842.5 80.5 reduce-scatter.11
  924.8 46.6 all-gather.31
  973.1 46.6 all-gather.23
  1023.2 80.5 reduce-scatter.19
  1107.2 80.5 reduce-scatter.13
  1189.9 39.1 reduce-scatter.23
  1231.4 40.3 reduce-scatter.21
  1273.7 12.3 all-gather.33
  1288.9 40.3 reduce-scatter.25

commit v2 on v1

v2 whole, which is shorter than its diff:
```python
import jax
import jax.numpy as jnp
from jax import lax
from jax.experimental import pallas as pl
from jax.experimental.pallas import tpu as pltpu
from jax.sharding import PartitionSpec as P

MESH = pl.DeviceIdType.MESH
F32 = jnp.float32
BF16 = jnp.bfloat16
EPS = 1e-6

CHUNKS = 4
ROWS = 128
BLOCK_ROWS = 4 * ROWS
WIDTH = 2048
HALF = WIDTH // 2
QUARTER = WIDTH // 4
TILE = 256
TILES = WIDTH // TILE
CHAIN = 3 * CHUNKS
GRAD_TILES = 3 * TILES
SLOTS = 4
LO, HI = pl.ds(0, HALF), pl.ds(HALF, HALF)


def mm(lhs, rhs, rhs_dim):
    return lax.dot_general(lhs, rhs, (((1,), (rhs_dim,)), ((), ())), preferred_element_type=F32)


def start_all(copies):
    for copy in copies:
        copy.start()


def run_all(copies):
    start_all(copies)
    for copy in copies:
        copy.wait()


def step_kernel(x, g, wg_in, wi_in, wo_in,
                dx, dwg, dwi, dwo, act, wg, wi, wo, part, ra1, rb1, ra2, rb2, lhs, rhs,
                wbuf, ab, tb, dab, dbb, pst, keep, snd, ld, r2, own, new, outs,
                ag_send, ag_recv, rs_send, rs_recv, w_send, w_recv, f_send, f_recv, d_send, d_recv,
                op_send, op_recv, dx_send, dx_recv, gr_send, gr_recv, p_sem, l_sem, t_sem):
    chip = lax.axis_index('data')
    core = lax.axis_index('stage')
    cx, cy = chip % 2, chip // 2
    near = (cy * 2 + (1 - cx), (1 - cy) * 2 + cx, (1 - cy) * 2 + (1 - cx))
    other = 1 - core
    x_dev, y_dev, twin = (near[0], core), (near[1], core), (chip, other)
    w_ins, w_alls = (wg_in, wi_in), (wg, wi)

    def local(src, dst, sem):
        return pltpu.make_async_copy(src, dst, sem)

    def remote(src, dst, send, recv, dev):
        return pltpu.make_async_remote_copy(src_ref=src, dst_ref=dst, send_sem=send, recv_sem=recv, device_id=dev, device_id_type=MESH)

    def shard(kind, i, n, cols=slice(None)):
        return act.at[kind, i, pl.ds(n * ROWS, ROWS), cols]

    def ag_first(kind, i, src):
        return (remote(src, shard(kind, i, 2), ag_send.at[kind, i, 0], ag_recv.at[kind, i, 0], x_dev),
                remote(src, shard(kind, i, 1), ag_send.at[kind, i, 1], ag_recv.at[kind, i, 1], y_dev))

    def ag_second(kind, i):
        return (remote(shard(kind, i, 1, LO), shard(kind, i, 3, LO), ag_send.at[kind, i, 2], ag_recv.at[kind, i, 2], x_dev),
                remote(shard(kind, i, 2, HI), shard(kind, i, 3, HI), ag_send.at[kind, i, 3], ag_recv.at[kind, i, 3], y_dev))

    def ag_forward(kind, i):
        for copy in ag_first(kind, i, shard(kind, i, 0)):
            copy.wait_recv()
        start_all(ag_second(kind, i))

    def ag_arrived(kind, i):
        for copy in ag_second(kind, i):
            copy.wait_recv()

    def rs_first(task):
        return (remote(part.at[task, 1, :, :, LO], ra1.at[task], rs_send.at[task, 0], rs_recv.at[task, 0], x_dev),
                remote(part.at[task, :, 1, :, HI], rb1.at[task], rs_send.at[task, 1], rs_recv.at[task, 1], y_dev))

    def rs_second(task):
        slot = task % 2
        return (remote(snd.at[slot, 0], ra2.at[task], rs_send.at[task, 2], rs_recv.at[task, 2], y_dev),
                remote(snd.at[slot, 1], rb2.at[task], rs_send.at[task, 3], rs_recv.at[task, 3], x_dev))

    def rs_middle(task):
        slot = task % 2

        @pl.when(task >= 2)
        def _():
            for copy in rs_second(task - 2):
                copy.wait_send()

        mine = (part.at[task, 0, :, :, LO], part.at[task, :, 0, :, HI])
        for side, (came, received) in enumerate(zip((ra1, rb1), rs_first(task))):
            received.wait_recv()
            run_all((local(mine[side], ld.at[0], l_sem.at[0]), local(came.at[task], ld.at[1], l_sem.at[1])))
            snd[slot, side] = ld[0, 1] + ld[1, 1]
            keep[slot, :, pl.ds(side * HALF, HALF)] = ld[0, 0] + ld[1, 0]
            rs_second(task)[side].start()

    def dx_copies(i, slot):
        dst = dx.at[i, pl.ds(core * ROWS, ROWS)]
        return (local(new.at[slot], dst, dx_send.at[i, 0]), remote(new.at[slot], dst, dx_send.at[i, 1], dx_recv.at[i], twin))

    def dx_sent(i):
        stored, sent = dx_copies(i, i % 2)
        stored.wait()
        sent.wait_send()

    def rs_last(task):
        slot, kind, i = task % 2, task // CHUNKS, task % CHUNKS
        for copy in rs_second(task):
            copy.wait_recv()
        run_all((local(ra2.at[task], r2.at[:, LO], l_sem.at[0]), local(rb2.at[task], r2.at[:, HI], l_sem.at[1]),
                 local(shard((3 * kind + 1) // 2, i, 0), own.at[0], l_sem.at[2]), local(shard(kind % 2, i, 0), own.at[1], l_sem.at[3])))

        @pl.when(task >= 2 * CHUNKS + 2)
        def _():
            dx_sent(i - 2)

        def rows_step(r, _):
            rows = pl.ds(r * 32, 32)
            total = keep[slot, rows, :] + r2[rows, :]

            @pl.when(kind == 0)
            def _():
                new[slot, rows, :] = own[0, rows, :] + total.astype(BF16)

            @pl.when(kind > 0)
            def _():
                tok = own[1, rows, :].astype(F32)
                inv = lax.rsqrt(jnp.mean(tok * tok, axis=-1, keepdims=True) + EPS)
                dot = jnp.mean(tok * total, axis=-1, keepdims=True)
                resid = total * inv - tok * (inv * inv * inv * dot)
                new[slot, rows, :] = (own[0, rows, :].astype(F32) + resid).astype(BF16)
            return 0

        lax.fori_loop(0, ROWS // 32, rows_step, 0)

        @pl.when(kind < 2)
        def _():
            mine = shard(2 * kind + 1, i, 0)
            run_all((local(new.at[slot], mine, l_sem.at[0]),))
            start_all(ag_first(2 * kind + 1, i, mine))

        @pl.when(kind == 2)
        def _():
            start_all(dx_copies(i, slot))

    def w_copies(mtx, n):
        rows = pl.ds(chip * QUARTER + n * TILE, TILE)
        return [remote(w_ins[mtx].at[pl.ds(n * TILE, TILE), pl.ds(to * WIDTH, WIDTH)], w_alls[mtx].at[core, rows],
                       w_send.at[mtx, n, k], w_recv.at[mtx, n, k], (to, core)) for k, to in enumerate(near)]

    def w_forwards(mtx, n, block):
        pieces = [w_alls[mtx].at[block, pl.ds(came * QUARTER + n * TILE, TILE)] for came in near]
        return [remote(piece, piece, f_send.at[mtx, n, k], f_recv.at[mtx, n, k], twin) for k, piece in enumerate(pieces)]

    def w_pass_on(mtx, n):
        for came, onward in zip(w_copies(mtx, n), w_forwards(mtx, n, core)):
            came.wait_recv()
            onward.start()

    def w_twin(block):
        rows, cols = pl.ds(chip * QUARTER, QUARTER), pl.ds(chip * WIDTH, WIDTH)
        return (remote(wg_in.at[:, cols], wg.at[block, rows], d_send.at[0], d_recv.at[0], twin),
                remote(wi_in.at[:, cols], wi.at[block, rows], d_send.at[1], d_recv.at[1], twin),
                remote(wo_in, wo.at[block], d_send.at[2], d_recv.at[2], twin))

    def w_from_twin(block):
        for mtx in range(2):
            for n in range(2):
                for copy in w_forwards(mtx, n, block):
                    copy.wait_recv()
        for copy in w_twin(block):
            copy.wait_recv()

    def op_pairs(i, src):
        rows = pl.ds(i * BLOCK_ROWS, BLOCK_ROWS)
        return ((tb.at[0], lhs.at[0, src, :, rows]), (tb.at[1], lhs.at[1, src, :, rows]), (dab, rhs.at[0, src, rows]),
                (dbb, rhs.at[1, src, rows]), (ab.at[1], rhs.at[2, src, rows]))

    def op_start(n, i, block):
        src, dst = op_pairs(i, core)[n]

        @pl.when(block == core)
        def _():
            local(src, dst, op_send.at[n]).start()

        @pl.when(block != core)
        def _():
            remote(src, dst, op_send.at[n], op_recv.at[i, n], twin).start()

    def op_sent(i):
        for n, (src, dst) in enumerate(op_pairs(i, core)):
            local(src, dst, op_send.at[n]).wait()

    def op_arrived(i):
        for n, (src, dst) in enumerate(op_pairs(i, other)):
            remote(src, dst, op_send.at[n], op_recv.at[i, n], twin).wait_recv()

    def normalize():
        def rows_step(r, _):
            rows = pl.ds(r * 64, 64)
            tok = ab[0, rows, :].astype(F32)
            inv = lax.rsqrt(jnp.mean(tok * tok, axis=-1, keepdims=True) + EPS)
            ab[0, rows, :] = (tok * inv).astype(BF16)
            return 0

        lax.fori_loop(0, BLOCK_ROWS // 64, rows_step, 0)

    def write_partials(task, product):
        def tile_copy(n, slot):
            return local(pst.at[slot], part.at[task, :, :, :, pl.ds(n * TILE, TILE)], p_sem.at[slot])

        def half_step(side, _):
            def tile_step(t, _):
                n, slot = side * (TILES // 2) + t, t % 2

                @pl.when(t >= 2)
                def _():
                    tile_copy(n - 2, slot).wait()

                pst[slot] = product(pl.ds(n * TILE, TILE)).reshape(2, 2, ROWS, TILE)
                tile_copy(n, slot).start()
                return 0

            lax.fori_loop(0, TILES // 2, tile_step, 0)
            last = (side + 1) * (TILES // 2)
            tile_copy(last - 2, 0).wait()
            tile_copy(last - 1, 1).wait()
            for n in range(2):
                @pl.when(side == n)
                def _(n=n):
                    rs_first(task)[n].start()
            return 0

        lax.fori_loop(0, 2, half_step, 0)

    def forward(task):
        ag_arrived(0, task)
        run_all((local(act.at[0, task], ab.at[0], l_sem.at[0]),))
        normalize()

        def tile_step(t, _):
            cols = pl.ds(t * TILE, TILE)
            pre_gate = mm(ab[0], wbuf[0, :, cols], 0)
            pre_in = mm(ab[0], wbuf[1, :, cols], 0)
            dab[:, cols] = (pre_gate * jax.nn.sigmoid(pre_gate) * pre_in).astype(BF16)
            return 0

        lax.fori_loop(0, TILES, tile_step, 0)
        write_partials(task, lambda cols: mm(dab[...], wbuf[2, :, cols], 0))

    def backward(task):
        kind, i = task // CHUNKS, task % CHUNKS
        block = 2 - kind

        @pl.when(task > CHUNKS)
        def _():
            op_sent(i)

        @pl.when(kind == 1)
        def _():
            ag_arrived(1, i)
            ag_arrived(2, i)

        @pl.when(kind == 2)
        def _():
            ag_arrived(3, i)

        run_all((local(act.at[2 - kind, i], ab.at[0], l_sem.at[0]), local(act.at[kind + 1, i], ab.at[1], l_sem.at[1])))
        op_start(4, i, block)
        normalize()

        def turn_step(t, _):
            cols = pl.ds(t * TILE, TILE)
            tb[0, cols, :] = ab[0, :, cols].T
            return 0

        lax.fori_loop(0, TILES, turn_step, 0)
        op_start(0, i, block)

        def tile_step(t, _):
            cols = pl.ds(t * TILE, TILE)
            pre_gate = mm(ab[0], wbuf[0, :, cols], 0)
            pre_in = mm(ab[0], wbuf[1, :, cols], 0)
            d_hidden = mm(ab[1], wbuf[2, cols, :], 1)
            sigma = jax.nn.sigmoid(pre_gate)
            gate_act = pre_gate * sigma
            tb[1, cols, :] = (gate_act * pre_in).astype(BF16).T
            dab[:, cols] = (d_hidden * pre_in * sigma * (1.0 + pre_gate * (1.0 - sigma))).astype(BF16)
            dbb[:, cols] = (d_hidden * gate_act).astype(BF16)
            return 0

        lax.fori_loop(0, TILES, tile_step, 0)
        for n in (1, 2, 3):
            op_start(n, i, block)
        write_partials(task, lambda rows: mm(dab[...], wbuf[0, rows, :], 1) + mm(dbb[...], wbuf[1, rows, :], 1))

    def rhs_copies(t):
        slot = t % 2
        cols = pl.ds((t % TILES) * TILE, TILE)
        return [local(rhs.at[t // TILES, q, :, cols], tb.at[slot, :, pl.ds(q * TILE, TILE)], t_sem.at[slot, q]) for q in range(2)]

    def grad_sent(slot):
        for k in range(4):
            local(outs.at[slot, pl.ds(0, QUARTER)], dwo.at[pl.ds(0, QUARTER), pl.ds(0, TILE)], gr_send.at[slot, k]).wait()

    def grad_tile(t):
        mtx, slot = t // TILES, t % SLOTS
        col = (t % TILES) * TILE

        @pl.when(t == 0)
        def _():
            op_sent(0)
            for i in range(CHUNKS):
                op_arrived(i)
            start_all(rhs_copies(0))

        @pl.when(t % (2 * TILES) == 0)
        def _():
            run_all([local(lhs.at[t // (2 * TILES), q], wbuf.at[q], l_sem.at[q]) for q in range(2)])

        @pl.when(t + 1 < GRAD_TILES)
        def _():
            start_all(rhs_copies(t + 1))

        for copy in rhs_copies(t):
            copy.wait()

        @pl.when(t >= SLOTS)
        def _():
            grad_sent(slot)

        def quarter_step(k, _):
            ax, ay = 1 - k % 2, ((k + 1) // 2) % 2
            to = (cy + ay - 2 * cy * ay) * 2 + (cx + ax - 2 * cx * ax)
            rows = pl.ds(to * QUARTER, QUARTER)
            outs[slot, rows, :] = mm(wbuf[0, rows, :], tb[t % 2, :, 0:TILE], 0) + mm(wbuf[1, rows, :], tb[t % 2, :, TILE:2 * TILE], 0)
            for n, dst in enumerate((dwg, dwi)):
                cols = pl.ds(chip * WIDTH + col, TILE)

                @pl.when((mtx == n) & (k < 3))
                def _():
                    remote(outs.at[slot, rows], dst.at[:, cols], gr_send.at[slot, k], gr_recv.at[n, k], (to, core)).start()

                @pl.when((mtx == n) & (k == 3))
                def _():
                    local(outs.at[slot, rows], dst.at[:, cols], gr_send.at[slot, k]).start()

            @pl.when(mtx == 2)
            def _():
                local(outs.at[slot, rows], dwo.at[rows, pl.ds(col, TILE)], gr_send.at[slot, k]).start()
            return 0

        lax.fori_loop(0, 4, quarter_step, 0)

    barrier = pltpu.get_barrier_semaphore()
    for dev in [(to, core) for to in near] + [twin]:
        pl.semaphore_signal(barrier, inc=1, device_id=dev, device_id_type=MESH)
    pl.semaphore_wait(barrier, 4)

    def my_rows(arr, i):
        return arr.at[i, pl.ds(core * ROWS, ROWS)]

    for i in range(2):
        start_all(ag_first(0, i, my_rows(x, i)))

    @pl.when(core == 0)
    def _():
        for mtx in range(2):
            for n in range(2):
                start_all(w_copies(mtx, n))

    start_all(w_twin(core))
    rows, cols = pl.ds(chip * QUARTER, QUARTER), pl.ds(chip * WIDTH, WIDTH)
    top = pl.ds(0, QUARTER)
    loads = [local(wg_in.at[:, cols], wbuf.at[0, top], l_sem.at[0]), local(wi_in.at[:, cols], wbuf.at[1, top], l_sem.at[1]),
             local(wo_in, wbuf.at[2], l_sem.at[2])]
    stores = [local(wbuf.at[0, top], wg.at[core, rows], l_sem.at[0]), local(wbuf.at[1, top], wi.at[core, rows], l_sem.at[1]),
              local(wbuf.at[2], wo.at[core], l_sem.at[2])]
    for n, (arr, kind) in enumerate(((x, 0), (g, 2))):
        for i in range(CHUNKS):
            spot = ab.at[n, pl.ds(i * ROWS, ROWS)]
            loads.append(local(my_rows(arr, i), spot, t_sem.at[n, i]))
            stores.append(local(spot, shard(kind, i, 0), t_sem.at[n, i]))
    run_all(loads)
    run_all(stores)
    for i in range(2):
        ag_forward(0, i)

    @pl.when(core == 0)
    def _():
        for mtx in range(2):
            for n in range(2):
                w_pass_on(mtx, n)

    @pl.when(core == 1)
    def _():
        w_from_twin(0)

    def tick_step(tick, _):
        @pl.when(tick < 2)
        def _():
            start_all(ag_first(0, tick + 2, my_rows(x, tick + 2)))

        @pl.when(tick < CHUNKS)
        def _():
            start_all(ag_first(2, tick, my_rows(g, tick)))

        for mtx in range(2):
            for n in range(2):
                @pl.when((tick == 2 * mtx + n) & (core == 1))
                def _(mtx=mtx, n=n):
                    start_all(w_copies(mtx, n))

        @pl.when((tick == CHUNKS) & (core == 0))
        def _():
            w_from_twin(1)

        @pl.when((tick < CHAIN) & (tick % CHUNKS == 0))
        def _():
            block = (tick // CHUNKS) % 2
            run_all([local(src.at[block], wbuf.at[n], l_sem.at[n]) for n, src in enumerate((wg, wi, wo))])

        @pl.when(tick < CHUNKS)
        def _():
            forward(tick)

        @pl.when((tick >= CHUNKS) & (tick < CHAIN))
        def _():
            backward(tick)

        @pl.when(tick >= CHAIN)
        def _():
            grad_tile(tick - CHAIN)

        @pl.when(tick < 2)
        def _():
            ag_forward(0, tick + 2)

        @pl.when(tick < CHUNKS)
        def _():
            ag_forward(2, tick)

        @pl.when((tick >= 3) & (tick < 3 + 2 * CHUNKS))
        def _():
            ag_forward(2 * ((tick - 3) // CHUNKS) + 1, (tick - 3) % CHUNKS)

        @pl.when((tick >= 2) & (tick < 2 + CHAIN))
        def _():
            rs_last(tick - 2)

        @pl.when((tick >= 1) & (tick < 1 + CHAIN))
        def _():
            rs_middle(tick - 1)

        for mtx in range(2):
            for n in range(2):
                @pl.when((tick == 2 * mtx + n) & (core == 1))
                def _(mtx=mtx, n=n):
                    w_pass_on(mtx, n)
        return 0

    lax.fori_loop(0, CHAIN + GRAD_TILES, tick_step, 0)

    for n, dst in enumerate((dwg, dwi)):
        for k, came in enumerate(near):
            block = dst.at[:, pl.ds(came * WIDTH, WIDTH)]
            local(block, block, gr_recv.at[n, k]).wait()
    for slot in range(SLOTS):
        grad_sent(slot)
    for i in range(CHUNKS):
        dx_copies(i, 0)[1].wait_recv()
    dx_sent(2)
    dx_sent(3)

    def drain_gathers(n, _):
        kind, i = n // CHUNKS, n % CHUNKS
        for copy in ag_first(kind, i, shard(kind, i, 0)) + ag_second(kind, i):
            copy.wait_send()
        return 0

    def drain_sums(task, _):
        for copy in rs_first(task):
            copy.wait_send()
        return 0

    lax.fori_loop(0, 4 * CHUNKS, drain_gathers, 0)
    lax.fori_loop(0, CHAIN, drain_sums, 0)
    for task in (CHAIN - 2, CHAIN - 1):
        for copy in rs_second(task):
            copy.wait_send()
    for mtx in range(2):
        for n in range(2):
            for copy in w_copies(mtx, n) + w_forwards(mtx, n, core):
                copy.wait_send()
    for copy in w_twin(core):
        copy.wait_send()


def solution(mesh):
    act_spec = P(None, 'data', None, None)
    weight_spec = P('stage', None, 'data', None)

    def per_device(x, g, w_gate, w_in, w_out):
        flat = (CHUNKS, 2 * ROWS, WIDTH)
        dma = pltpu.SemaphoreType.DMA
        any_space = pl.BlockSpec(memory_space=pl.ANY)

        def arr(*shape, dtype=BF16):
            return jax.ShapeDtypeStruct(shape, dtype)

        out_shapes = [
            arr(*flat), arr(QUARTER, 4 * WIDTH, dtype=F32), arr(QUARTER, 4 * WIDTH, dtype=F32), arr(WIDTH, WIDTH, dtype=F32),
            arr(4, CHUNKS, BLOCK_ROWS, WIDTH), arr(2, WIDTH, WIDTH), arr(2, WIDTH, WIDTH), arr(2, WIDTH, WIDTH),
            arr(CHAIN, 2, 2, ROWS, WIDTH, dtype=F32),
            arr(CHAIN, 2, ROWS, HALF, dtype=F32), arr(CHAIN, 2, ROWS, HALF, dtype=F32),
            arr(CHAIN, ROWS, HALF, dtype=F32), arr(CHAIN, ROWS, HALF, dtype=F32),
            arr(2, 2, WIDTH, WIDTH), arr(3, 2, WIDTH, WIDTH),
        ]
        scratch = [
            pltpu.VMEM((3, WIDTH, WIDTH), BF16), pltpu.VMEM((2, BLOCK_ROWS, WIDTH), BF16), pltpu.VMEM((2, WIDTH, BLOCK_ROWS), BF16),
            pltpu.VMEM((BLOCK_ROWS, WIDTH), BF16), pltpu.VMEM((BLOCK_ROWS, WIDTH), BF16),
            pltpu.VMEM((2, 2, 2, ROWS, TILE), F32), pltpu.VMEM((2, ROWS, WIDTH), F32), pltpu.VMEM((2, 2, ROWS, HALF), F32),
            pltpu.VMEM((2, 2, ROWS, HALF), F32), pltpu.VMEM((ROWS, WIDTH), F32), pltpu.VMEM((2, ROWS, WIDTH), BF16),
            pltpu.VMEM((2, ROWS, WIDTH), BF16), pltpu.VMEM((SLOTS, WIDTH, TILE), F32),
            dma((4, CHUNKS, 4)), dma((4, CHUNKS, 4)), dma((CHAIN, 4)), dma((CHAIN, 4)),
            dma((2, 2, 3)), dma((2, 2, 3)), dma((2, 2, 3)), dma((2, 2, 3)), dma((3,)), dma((3,)),
            dma((5,)), dma((CHUNKS, 5)), dma((CHUNKS, 2)), dma((CHUNKS,)), dma((SLOTS, 4)), dma((2, 3)),
            dma((2,)), dma((4,)), dma((2, 4)),
        ]
        results = pl.pallas_call(
            step_kernel, out_shape=out_shapes, in_specs=[any_space] * 5, out_specs=[any_space] * len(out_shapes),
            scratch_shapes=scratch, name='mlp_step',
            compiler_params=pltpu.CompilerParams(collective_id=0, has_side_effects=True, vmem_limit_bytes=67_043_328),
        )(x.reshape(flat), g.reshape(flat), w_gate[0, 0], w_in[0, 0], w_out[0, 0])
        dx, d_gate, d_in, d_out = results[:4]
        return dx.reshape(x.shape), d_gate[None, None], d_in[None, None], d_out[None, None]

    return jax.shard_map(per_device, mesh=mesh, in_specs=(act_spec, act_spec, weight_spec, weight_spec, weight_spec),
                         out_specs=(act_spec, weight_spec, weight_spec, weight_spec), check_vma=False)
```

time: 1710 us -> 1320 us (0.77)
  Pallas kernels: 0 us -> 1270 us
  waiting for transfers between devices: 842 us -> 0 us
  matrix products: 478 us -> 0 us
  other arithmetic: 110 us -> 0.01 us
  local copies, waits for them, and re-layouts: 140 us -> 37.5 us
  blocking collectives: 99.8 us -> 0 us
  starting transfers between devices: 22.1 us -> 0 us
    pallas_call x0 -> x1, Pallas kernels: none -> 1270 us  [per_device(): pl.pallas_call(step_kernel, out_shape=out_shapes, in_specs=[any_space] *...]
    dot_general x28 -> x0, matrix products: 478 us -> none  [mm(): lax.dot_general(lhs, rhs, (((lhs_dim,), (rhs_dim,)), ((), ())), preferred...]
    all_to_all x3 -> x0, waiting for transfers between devices: 446 us -> none  [the longest x2 322 us: rows_of(): pieces = lax.all_to_all(full.reshape(chips, -1, cols), 'data', 0, 0)]
    all_gather x12 -> x0, waiting for transfers between devices: 198 us -> none  [the longest x8 181 us: everywhere(): return lax.all_gather(rows, 'data', axis=0, tiled=True)]
    reduce_scatter x9 -> x0, waiting for transfers between devices: 196 us -> none  [the longest x6 196 us: summed(): return lax.psum_scatter(partial, 'data', scatter_dimension=0, tiled=True)]
    all_to_all x1 -> x0, blocking collectives: 99.8 us -> none  [columns_of(): pieces = lax.all_to_all(shard.reshape(-1, chips, cols), 'data', 1, 0)]
    another operation x6 -> x0, other arithmetic: 59.6 us -> none  [the longest x3 55.3 us: per_device(): jnp.stack(parts)]
    transpose x2 -> x0, local copies, waits for them, and re-layouts: 41.8 us -> none  [rows_of(): return pieces.transpose(1, 0, 2).reshape(1, 1, -1, ffn)]
  transfers between devices with their start and end apart: 24 -> 0, of which waited for: 15 -> 0; matrix products, arithmetic and copies ran while one was open for 41% -> 0% of each run, Pallas kernels for 0% -> 0%
where the time goes in v2:
time: 1320 us; the launch traced here: 1310 us
  Pallas kernels  1270 us (96%)
  local copies, waits for them, and re-layouts  37.5 us (3%)
    pallas_call x1, Pallas kernels, per_device(): pl.pallas_call(step_kernel, out_shape=out_shapes, in_specs=[any_space] *...  1270 us
    unnamed x20, local copies, waits for them, and re-layouts  37.5 us

profile of v2, /device:TPU:0, one launch (start us, length us, event | category | flops | bytes accessed | tf_op | source)
XLA Modules:
  0.0 1309.5 jit_solution(14325651055141037120)
XLA Ops:
  0.6 1271.4 %mlp_step.1 = (bf16[4,256,2048]{2,1,0:T(8,128)(2,1)}, f32[512,8192]{1,0:T(8,128)}, f32[512,8192]{1,0:T(8,128)}, f32[2048,2048]{1,0:T(8,128)}, bf16[4,4,512,2048]...) custom-call(bf16[4,256,2048]{2,1,0:T(8,128)(2,1)} %bitcast.20, ...), custom_call_target="tpu_custom_call" | custom-call | tf_op jit(solution)/shard_map/mlp_step/pallas_call | solution.py:539
  1272.0 0.0 slice-start.4
  1272.0 4.9 copy.13
  1277.0 0.0 slice-start.5
  1277.0 0.0 slice-start.6
  1277.0 0.0 slice-start.7
  1277.0 0.0 slice-start
  1277.0 0.0 slice-start.1
  1277.0 13.4 %copy.14 = f32[1,1,512,8192]{3,2,1,0:T(8,128)} copy(f32[1,1,512,8192]{3,2,1,0:T(8,128)} %bitcast.15) | data formatting | bytes 33554432
  1290.4 0.0 slice-done.4
  1290.4 0.0 slice-done.5
  1290.4 0.0 slice-done.6
  1290.4 1.9 slice-done.7
  1292.3 0.0 slice-start.2
  1292.3 0.0 slice-start.3
  1292.3 8.5 copy.15
  1300.8 0.0 slice-done
  1300.8 0.0 slice-done.1
  1300.8 1.4 slice-done.2
  1302.2 1.2 slice-done.3
  1303.4 6.2 copy.16
  (2 shorter events, 0.0 us)
Async XLA Ops:
  1272.0 18.4 %slice-start.4 = ((s8[16777216]{0:T(1024)(128)(4,1)}), s8[4194304]{0:T(1024)(128)(4,1)S(1)}, s32[]{:S(2)}) async-start(s8[16777216]{0:T(1024)(128)(4,1)} %bitcast.12), calls=%async_computation.4 | async-start | bytes 8388608
  1277.0 13.4 %slice-start.5 = ((s8[16777216]{0:T(1024)(128)(4,1)}), s8[4194304]{0:T(1024)(128)(4,1)S(1)}, s32[]{:S(2)}) async-start(s8[16777216]{0:T(1024)(128)(4,1)} %bitcast.12), calls=%async_computation.5 | async-start | bytes 8388608
  1277.0 13.4 %slice-start.6 = ((s8[16777216]{0:T(1024)(128)(4,1)}), s8[4194304]{0:T(1024)(128)(4,1)S(1)}, s32[]{:S(2)}) async-start(s8[16777216]{0:T(1024)(128)(4,1)} %bitcast.12), calls=%async_computation.6 | async-start | bytes 8388608
  1277.0 15.3 %slice-start.7 = ((s8[16777216]{0:T(1024)(128)(4,1)}), s8[4194304]{0:T(1024)(128)(4,1)S(1)}, s32[]{:S(2)}) async-start(s8[16777216]{0:T(1024)(128)(4,1)} %bitcast.12), calls=%async_computation.7 | async-start | bytes 8388608
  1277.0 23.8 %slice-start = ((s8[16777216]{0:T(1024)(128)(4,1)}), s8[4194304]{0:T(1024)(128)(4,1)S(1)}, s32[]{:S(2)}) async-start(s8[16777216]{0:T(1024)(128)(4,1)} %bitcast.9), calls=%async_computation | async-start | bytes 8388608
  1277.0 23.8 %slice-start.1 = ((s8[16777216]{0:T(1024)(128)(4,1)}), s8[4194304]{0:T(1024)(128)(4,1)S(1)}, s32[]{:S(2)}) async-start(s8[16777216]{0:T(1024)(128)(4,1)} %bitcast.9), calls=%async_computation.1 | async-start | bytes 8388608
  1292.3 9.9 slice-start.2
  1292.3 11.1 slice-start.3

commit v3 on v2

--- a/solution.py
+++ b/solution.py
@@ -19,7 +19,8 @@
 TILE = 256
 TILES = WIDTH // TILE
 CHAIN = 3 * CHUNKS
-GRAD_TILES = 3 * TILES
+TURN = CHUNKS
+SENT_TILES = 2 * TILES
 SLOTS = 4
 LO, HI = pl.ds(0, HALF), pl.ds(HALF, HALF)
 
@@ -41,9 +42,9 @@
 
 def step_kernel(x, g, wg_in, wi_in, wo_in,
                 dx, dwg, dwi, dwo, act, wg, wi, wo, part, ra1, rb1, ra2, rb2, lhs, rhs,
-                wbuf, ab, tb, dab, dbb, pst, keep, snd, ld, r2, own, new, outs,
+                wbuf, ab, tb, dab, dbb, pst, keep, snd, ld, r2, own, new, outs, wo_out,
                 ag_send, ag_recv, rs_send, rs_recv, w_send, w_recv, f_send, f_recv, d_send, d_recv,
-                op_send, op_recv, dx_send, dx_recv, gr_send, gr_recv, p_sem, l_sem, t_sem):
+                op_send, op_recv, dx_send, dx_recv, gr_send, gr_recv, p_sem, l_sem, t_sem, o_sem):
     chip = lax.axis_index('data')
     core = lax.axis_index('stage')
     cx, cy = chip % 2, chip // 2
@@ -303,10 +304,8 @@
             op_start(n, i, block)
         write_partials(task, lambda rows: mm(dab[...], wbuf[0, rows, :], 1) + mm(dbb[...], wbuf[1, rows, :], 1))
 
-    def rhs_copies(t):
-        slot = t % 2
-        cols = pl.ds((t % TILES) * TILE, TILE)
-        return [local(rhs.at[t // TILES, q, :, cols], tb.at[slot, :, pl.ds(q * TILE, TILE)], t_sem.at[slot, q]) for q in range(2)]
+    def rhs_copies(mtx, n, slot):
+        return [local(rhs.at[mtx, q, :, pl.ds(n * TILE, TILE)], tb.at[slot, :, pl.ds(q * TILE, TILE)], t_sem.at[slot, q]) for q in range(2)]
 
     def grad_sent(slot):
         for k in range(4):
@@ -321,17 +320,10 @@
             op_sent(0)
             for i in range(CHUNKS):
                 op_arrived(i)
-            start_all(rhs_copies(0))
-
-        @pl.when(t % (2 * TILES) == 0)
-        def _():
-            run_all([local(lhs.at[t // (2 * TILES), q], wbuf.at[q], l_sem.at[q]) for q in range(2)])
-
-        @pl.when(t + 1 < GRAD_TILES)
-        def _():
-            start_all(rhs_copies(t + 1))
-
-        for copy in rhs_copies(t):
+            start_all(rhs_copies(0, 0, 0))
+            run_all([local(lhs.at[0, q], wbuf.at[q], l_sem.at[q]) for q in range(2)])
+
+        for copy in rhs_copies(mtx, t % TILES, 0):
             copy.wait()
 
         @pl.when(t >= SLOTS)
@@ -342,21 +334,53 @@
             ax, ay = 1 - k % 2, ((k + 1) // 2) % 2
             to = (cy + ay - 2 * cy * ay) * 2 + (cx + ax - 2 * cx * ax)
             rows = pl.ds(to * QUARTER, QUARTER)
-            outs[slot, rows, :] = mm(wbuf[0, rows, :], tb[t % 2, :, 0:TILE], 0) + mm(wbuf[1, rows, :], tb[t % 2, :, TILE:2 * TILE], 0)
+            outs[slot, rows, :] = mm(wbuf[0, rows, :], tb[0, :, 0:TILE], 0) + mm(wbuf[1, rows, :], tb[0, :, TILE:2 * TILE], 0)
+            cols = pl.ds(chip * WIDTH + col, TILE)
             for n, dst in enumerate((dwg, dwi)):
-                cols = pl.ds(chip * WIDTH + col, TILE)
-
                 @pl.when((mtx == n) & (k < 3))
-                def _():
+                def _(n=n, dst=dst):
                     remote(outs.at[slot, rows], dst.at[:, cols], gr_send.at[slot, k], gr_recv.at[n, k], (to, core)).start()
 
                 @pl.when((mtx == n) & (k == 3))
-                def _():
+                def _(dst=dst):
                     local(outs.at[slot, rows], dst.at[:, cols], gr_send.at[slot, k]).start()
-
-            @pl.when(mtx == 2)
+            return 0
+
+        lax.fori_loop(0, 4, quarter_step, 0)
+
+        @pl.when(t + 1 < SENT_TILES)
+        def _():
+            start_all(rhs_copies((t + 1) // TILES, (t + 1) % TILES, 0))
+
+    def out_loads(k, slot):
+        return [local(lhs.at[1, q, pl.ds(k * QUARTER, QUARTER)], wbuf.at[2, pl.ds(slot * HALF + q * QUARTER, QUARTER)], o_sem.at[slot, q]) for q in range(2)]
+
+    def out_store(n, k, slot):
+        return local(wo_out.at[slot], dwo.at[pl.ds(k * QUARTER, QUARTER), pl.ds(n * TILE, TILE)], o_sem.at[slot, 2])
+
+    def out_tile(n):
+        start_all(rhs_copies(2, n, 1))
+        start_all(out_loads(0, 0))
+        for copy in rhs_copies(2, n, 1):
+            copy.wait()
+
+        def quarter_step(k, _):
+            slot = k % 2
+
+            @pl.when(k < 3)
             def _():
-                local(outs.at[slot, rows], dwo.at[rows, pl.ds(col, TILE)], gr_send.at[slot, k]).start()
+                start_all(out_loads(k + 1, 1 - slot))
+
+            for copy in out_loads(k, slot):
+                copy.wait()
+
+            @pl.when(4 * n + k >= 2)
+            def _():
+                out_store(n, k, slot).wait()
+
+            top, low = pl.ds(slot * HALF, QUARTER), pl.ds(slot * HALF + QUARTER, QUARTER)
+            wo_out[slot] = mm(wbuf[2, top, :], tb[1, :, 0:TILE], 0) + mm(wbuf[2, low, :], tb[1, :, TILE:2 * TILE], 0)
+            out_store(n, k, slot).start()
             return 0
 
         lax.fori_loop(0, 4, quarter_step, 0)
@@ -405,14 +429,25 @@
     def _():
         w_from_twin(0)
 
+    def when_task(tick, first, last):
+        def run(body):
+            @pl.when((tick >= 0) & (tick != TURN) & (tick <= CHAIN))
+            def _():
+                task = tick - jnp.where(tick > TURN, 1, 0)
+
+                @pl.when((task >= first) & (task < last))
+                def _():
+                    body(task)
+        return run
+
     def tick_step(tick, _):
         @pl.when(tick < 2)
         def _():
             start_all(ag_first(0, tick + 2, my_rows(x, tick + 2)))
 
-        @pl.when(tick < CHUNKS)
-        def _():
-            start_all(ag_first(2, tick, my_rows(g, tick)))
+        @pl.when((tick >= 2) & (tick < 2 + CHUNKS))
+        def _():
+            start_all(ag_first(2, tick - 2, my_rows(g, tick - 2)))
 
         for mtx in range(2):
             for n in range(2):
@@ -420,46 +455,42 @@
                 def _(mtx=mtx, n=n):
                     start_all(w_copies(mtx, n))
 
-        @pl.when((tick == CHUNKS) & (core == 0))
+        @pl.when((tick == TURN + 1) & (core == 0))
         def _():
             w_from_twin(1)
 
-        @pl.when((tick < CHAIN) & (tick % CHUNKS == 0))
-        def _():
-            block = (tick // CHUNKS) % 2
-            run_all([local(src.at[block], wbuf.at[n], l_sem.at[n]) for n, src in enumerate((wg, wi, wo))])
-
-        @pl.when(tick < CHUNKS)
-        def _():
-            forward(tick)
-
-        @pl.when((tick >= CHUNKS) & (tick < CHAIN))
-        def _():
-            backward(tick)
-
-        @pl.when(tick >= CHAIN)
-        def _():
-            grad_tile(tick - CHAIN)
+        @when_task(tick, 0, CHAIN)
+        def _(task):
+            @pl.when(task % CHUNKS == 0)
+            def _():
+                block = (task // CHUNKS) % 2
+                run_all([local(src.at[block], wbuf.at[n], l_sem.at[n]) for n, src in enumerate((wg, wi, wo))])
+
+        when_task(tick, 0, CHUNKS)(forward)
+        when_task(tick, CHUNKS, CHAIN)(backward)
+
+        @pl.when(tick > CHAIN)
+        def _():
+            grad_tile(tick - CHAIN - 1)
+
+        @pl.when((tick > CHAIN + SLOTS) & (tick <= CHAIN + SLOTS + TILES))
+        def _():
+            out_tile(tick - CHAIN - SLOTS - 1)
 
         @pl.when(tick < 2)
         def _():
             ag_forward(0, tick + 2)
 
-        @pl.when(tick < CHUNKS)
-        def _():
-            ag_forward(2, tick)
-
-        @pl.when((tick >= 3) & (tick < 3 + 2 * CHUNKS))
-        def _():
-            ag_forward(2 * ((tick - 3) // CHUNKS) + 1, (tick - 3) % CHUNKS)
-
-        @pl.when((tick >= 2) & (tick < 2 + CHAIN))
-        def _():
-            rs_last(tick - 2)
-
-        @pl.when((tick >= 1) & (tick < 1 + CHAIN))
-        def _():
-            rs_middle(tick - 1)
+        @when_task(tick - 3, 0, 2 * CHUNKS)
+        def _(task):
+            ag_forward(2 * (task // CHUNKS) + 1, task % CHUNKS)
+
+        when_task(tick - 2, 0, CHAIN)(rs_last)
+        when_task(tick - 1, 0, CHAIN)(rs_middle)
+
+        @pl.when((tick >= 2) & (tick < 2 + CHUNKS))
+        def _():
+            ag_forward(2, tick - 2)
 
         for mtx in range(2):
             for n in range(2):
@@ -468,7 +499,7 @@
                     w_pass_on(mtx, n)
         return 0
 
-    lax.fori_loop(0, CHAIN + GRAD_TILES, tick_step, 0)
+    lax.fori_loop(0, CHAIN + 1 + SENT_TILES, tick_step, 0)
 
     for n, dst in enumerate((dwg, dwi)):
         for k, came in enumerate(near):
@@ -476,6 +507,8 @@
             local(block, block, gr_recv.at[n, k]).wait()
     for slot in range(SLOTS):
         grad_sent(slot)
+    for slot in range(2):
+        out_store(0, 0, slot).wait()
     for i in range(CHUNKS):
         dx_copies(i, 0)[1].wait_recv()
     dx_sent(2)
@@ -531,10 +564,11 @@
             pltpu.VMEM((2, 2, 2, ROWS, TILE), F32), pltpu.VMEM((2, ROWS, WIDTH), F32), pltpu.VMEM((2, 2, ROWS, HALF), F32),
             pltpu.VMEM((2, 2, ROWS, HALF), F32), pltpu.VMEM((ROWS, WIDTH), F32), pltpu.VMEM((2, ROWS, WIDTH), BF16),
             pltpu.VMEM((2, ROWS, WIDTH), BF16), pltpu.VMEM((SLOTS, WIDTH, TILE), F32),
+            pltpu.VMEM((2, QUARTER, TILE), F32),
             dma((4, CHUNKS, 4)), dma((4, CHUNKS, 4)), dma((CHAIN, 4)), dma((CHAIN, 4)),
             dma((2, 2, 3)), dma((2, 2, 3)), dma((2, 2, 3)), dma((2, 2, 3)), dma((3,)), dma((3,)),
             dma((5,)), dma((CHUNKS, 5)), dma((CHUNKS, 2)), dma((CHUNKS,)), dma((SLOTS, 4)), dma((2, 3)),
-            dma((2,)), dma((4,)), dma((2, 4)),
+            dma((2,)), dma((4,)), dma((2, 4)), dma((2, 3)),
         ]
         results = pl.pallas_call(
             step_kernel, out_shape=out_shapes, in_specs=[any_space] * 5, out_specs=[any_space] * len(out_shapes),

time: 1320 us -> 1280 us (0.970)
  Pallas kernels: 1270 us -> 1220 us
    pallas_call x1, Pallas kernels: 1270 us -> 1220 us  [per_device(): pl.pallas_call(step_kernel, out_shape=out_shapes, in_specs=[any_space] *...]
where the time goes in v3:
time: 1280 us; the launch traced here: 1260 us
  Pallas kernels  1220 us (95%)
  local copies, waits for them, and re-layouts  37.5 us (3%)
    pallas_call x1, Pallas kernels, per_device(): pl.pallas_call(step_kernel, out_shape=out_shapes, in_specs=[any_space] *...  1220 us
    unnamed x20, local copies, waits for them, and re-layouts  37.5 us

profile of v3, /device:TPU:0, one launch (start us, length us, event | category | flops | bytes accessed | tf_op | source)
XLA Modules:
  0.0 1261.4 jit_solution(2285279678348223896)
XLA Ops:
  0.6 1223.2 %mlp_step.1 = (bf16[4,256,2048]{2,1,0:T(8,128)(2,1)}, f32[512,8192]{1,0:T(8,128)}, f32[512,8192]{1,0:T(8,128)}, f32[2048,2048]{1,0:T(8,128)}, bf16[4,4,512,2048]...) custom-call(bf16[4,256,2048]{2,1,0:T(8,128)(2,1)} %bitcast.20, ...), custom_call_target="tpu_custom_call" | custom-call | tf_op jit(solution)/shard_map/mlp_step/pallas_call | solution.py:573
  1223.9 0.0 slice-start.4
  1223.9 4.9 copy.13
  1228.8 0.0 slice-start.5
  1228.8 0.0 slice-start.6
  1228.8 0.0 slice-start.7
  1228.8 0.0 slice-start
  1228.8 0.0 slice-start.1
  1228.8 13.4 %copy.14 = f32[1,1,512,8192]{3,2,1,0:T(8,128)} copy(f32[1,1,512,8192]{3,2,1,0:T(8,128)} %bitcast.15) | data formatting | bytes 33554432
  1242.2 0.0 slice-done.4
  1242.3 0.0 slice-done.5
  1242.3 0.0 slice-done.6
  1242.3 1.9 slice-done.7
  1244.1 0.0 slice-start.2
  1244.1 0.0 slice-start.3
  1244.1 8.5 copy.15
  1252.6 0.0 slice-done
  1252.6 0.0 slice-done.1
  1252.6 1.4 slice-done.2
  1254.0 1.2 slice-done.3
  1255.2 6.2 copy.16
  (2 shorter events, 0.0 us)
Async XLA Ops:
  1223.9 18.4 %slice-start.4 = ((s8[16777216]{0:T(1024)(128)(4,1)}), s8[4194304]{0:T(1024)(128)(4,1)S(1)}, s32[]{:S(2)}) async-start(s8[16777216]{0:T(1024)(128)(4,1)} %bitcast.12), calls=%async_computation.4 | async-start | bytes 8388608
  1228.8 13.4 %slice-start.5 = ((s8[16777216]{0:T(1024)(128)(4,1)}), s8[4194304]{0:T(1024)(128)(4,1)S(1)}, s32[]{:S(2)}) async-start(s8[16777216]{0:T(1024)(128)(4,1)} %bitcast.12), calls=%async_computation.5 | async-start | bytes 8388608
  1228.8 13.4 %slice-start.6 = ((s8[16777216]{0:T(1024)(128)(4,1)}), s8[4194304]{0:T(1024)(128)(4,1)S(1)}, s32[]{:S(2)}) async-start(s8[16777216]{0:T(1024)(128)(4,1)} %bitcast.12), calls=%async_computation.6 | async-start | bytes 8388608
  1228.8 15.3 %slice-start.7 = ((s8[16777216]{0:T(1024)(128)(4,1)}), s8[4194304]{0:T(1024)(128)(4,1)S(1)}, s32[]{:S(2)}) async-start(s8[16777216]{0:T(1024)(128)(4,1)} %bitcast.12), calls=%async_computation.7 | async-start | bytes 8388608
  1228.8 23.8 %slice-start = ((s8[16777216]{0:T(1024)(128)(4,1)}), s8[4194304]{0:T(1024)(128)(4,1)S(1)}, s32[]{:S(2)}) async-start(s8[16777216]{0:T(1024)(128)(4,1)} %bitcast.9), calls=%async_computation | async-start | bytes 8388608
  1228.8 23.8 %slice-start.1 = ((s8[16777216]{0:T(1024)(128)(4,1)}), s8[4194304]{0:T(1024)(128)(4,1)S(1)}, s32[]{:S(2)}) async-start(s8[16777216]{0:T(1024)(128)(4,1)} %bitcast.9), calls=%async_computation.1 | async-start | bytes 8388608
  1244.1 9.9 slice-start.2
  1244.1 11.1 slice-start.3

commit v4 on v3

--- a/solution.py
+++ b/solution.py
@@ -21,6 +21,8 @@
 CHAIN = 3 * CHUNKS
 TURN = CHUNKS
 SENT_TILES = 2 * TILES
+LATE_TILES = 2
+SETTLE_FLOPS = 2 ** 30
 SLOTS = 4
 LO, HI = pl.ds(0, HALF), pl.ds(HALF, HALF)
 
@@ -41,7 +43,7 @@
 
 
 def step_kernel(x, g, wg_in, wi_in, wo_in,
-                dx, dwg, dwi, dwo, act, wg, wi, wo, part, ra1, rb1, ra2, rb2, lhs, rhs,
+                dx, dwg, dwi, dwo, late, act, wg, wi, wo, wx, part, ra1, rb1, ra2, rb2, lhs, rhs,
                 wbuf, ab, tb, dab, dbb, pst, keep, snd, ld, r2, own, new, outs, wo_out,
                 ag_send, ag_recv, rs_send, rs_recv, w_send, w_recv, f_send, f_recv, d_send, d_recv,
                 op_send, op_recv, dx_send, dx_recv, gr_send, gr_recv, p_sem, l_sem, t_sem, o_sem):
@@ -51,7 +53,6 @@
     near = (cy * 2 + (1 - cx), (1 - cy) * 2 + cx, (1 - cy) * 2 + (1 - cx))
     other = 1 - core
     x_dev, y_dev, twin = (near[0], core), (near[1], core), (chip, other)
-    w_ins, w_alls = (wg_in, wi_in), (wg, wi)
 
     def local(src, dst, sem):
         return pltpu.make_async_copy(src, dst, sem)
@@ -153,19 +154,32 @@
         def _():
             start_all(dx_copies(i, slot))
 
-    def w_copies(mtx, n):
-        rows = pl.ds(chip * QUARTER + n * TILE, TILE)
-        return [remote(w_ins[mtx].at[pl.ds(n * TILE, TILE), pl.ds(to * WIDTH, WIDTH)], w_alls[mtx].at[core, rows],
-                       w_send.at[mtx, n, k], w_recv.at[mtx, n, k], (to, core)) for k, to in enumerate(near)]
-
-    def w_forwards(mtx, n, block):
-        pieces = [w_alls[mtx].at[block, pl.ds(came * QUARTER + n * TILE, TILE)] for came in near]
-        return [remote(piece, piece, f_send.at[mtx, n, k], f_recv.at[mtx, n, k], twin) for k, piece in enumerate(pieces)]
-
-    def w_pass_on(mtx, n):
-        for came, onward in zip(w_copies(mtx, n), w_forwards(mtx, n, core)):
-            came.wait_recv()
-            onward.start()
+    def w_copies(mtx, block, n):
+        src, dst = ((wg_in, wx), (wx, wi_in))[mtx][block], (wg, wi)[mtx]
+        rows = pl.ds(chip * QUARTER + n * ROWS, ROWS)
+        return [remote(src.at[pl.ds(n * ROWS, ROWS), pl.ds(to * WIDTH, WIDTH)], dst.at[block, rows],
+                       w_send.at[block, n, k], w_recv.at[block, n, k], (to, core)) for k, to in enumerate(near)]
+
+    def w_forwards(mtx, block, n):
+        pieces = [(wg, wi)[mtx].at[block, pl.ds(came * QUARTER + n * ROWS, ROWS)] for came in near]
+        return [remote(piece, piece, f_send.at[block, n, k], f_recv.at[block, n, k], twin) for k, piece in enumerate(pieces)]
+
+    def w_start(block, n):
+        for mtx in range(2):
+            @pl.when(core == mtx)
+            def _(mtx=mtx):
+                start_all(w_copies(mtx, block, n))
+
+    def w_pass_on(block, n):
+        for mtx in range(2):
+            @pl.when(core == mtx)
+            def _(mtx=mtx):
+                for came, onward in zip(w_copies(mtx, block, n), w_forwards(mtx, block, n)):
+                    came.wait_recv()
+                    onward.start()
+
+    def w_hand(mtx):
+        return remote((wg_in, wi_in)[mtx], wx, d_send.at[3], d_recv.at[3], twin)
 
     def w_twin(block):
         rows, cols = pl.ds(chip * QUARTER, QUARTER), pl.ds(chip * WIDTH, WIDTH)
@@ -173,13 +187,15 @@
                 remote(wi_in.at[:, cols], wi.at[block, rows], d_send.at[1], d_recv.at[1], twin),
                 remote(wo_in, wo.at[block], d_send.at[2], d_recv.at[2], twin))
 
-    def w_from_twin(block):
-        for mtx in range(2):
-            for n in range(2):
-                for copy in w_forwards(mtx, n, block):
-                    copy.wait_recv()
-        for copy in w_twin(block):
-            copy.wait_recv()
+    def w_arrived(block):
+        for n in range(QUARTER // ROWS):
+            for copy in w_forwards(0, block, n):
+                copy.wait_recv()
+
+        @pl.when(core != block)
+        def _():
+            for copy in w_twin(block):
+                copy.wait_recv()
 
     def op_pairs(i, src):
         rows = pl.ds(i * BLOCK_ROWS, BLOCK_ROWS)
@@ -256,6 +272,8 @@
             return 0
 
         lax.fori_loop(0, TILES, tile_step, 0)
+
+    def forward_out(task):
         write_partials(task, lambda cols: mm(dab[...], wbuf[2, :, cols], 0))
 
     def backward(task):
@@ -302,6 +320,8 @@
         lax.fori_loop(0, TILES, tile_step, 0)
         for n in (1, 2, 3):
             op_start(n, i, block)
+
+    def backward_out(task):
         write_partials(task, lambda rows: mm(dab[...], wbuf[0, rows, :], 1) + mm(dbb[...], wbuf[1, rows, :], 1))
 
     def rhs_copies(mtx, n, slot):
@@ -337,13 +357,18 @@
             outs[slot, rows, :] = mm(wbuf[0, rows, :], tb[0, :, 0:TILE], 0) + mm(wbuf[1, rows, :], tb[0, :, TILE:2 * TILE], 0)
             cols = pl.ds(chip * WIDTH + col, TILE)
             for n, dst in enumerate((dwg, dwi)):
-                @pl.when((mtx == n) & (k < 3))
+                @pl.when((mtx == n) & (k < 3) & (t < SENT_TILES - LATE_TILES))
                 def _(n=n, dst=dst):
                     remote(outs.at[slot, rows], dst.at[:, cols], gr_send.at[slot, k], gr_recv.at[n, k], (to, core)).start()
 
-                @pl.when((mtx == n) & (k == 3))
+                @pl.when((mtx == n) & (k == 3) & (t < SENT_TILES - LATE_TILES))
                 def _(dst=dst):
                     local(outs.at[slot, rows], dst.at[:, cols], gr_send.at[slot, k]).start()
+
+            @pl.when(t >= SENT_TILES - LATE_TILES)
+            def _():
+                cols = pl.ds((t - SENT_TILES + LATE_TILES) * TILE, TILE)
+                local(outs.at[slot, rows], late.at[to, :, cols], gr_send.at[slot, k]).start()
             return 0
 
         lax.fori_loop(0, 4, quarter_step, 0)
@@ -398,9 +423,20 @@
 
     @pl.when(core == 0)
     def _():
-        for mtx in range(2):
-            for n in range(2):
-                start_all(w_copies(mtx, n))
+        w_hand(1).start()
+        for n in range(4):
+            start_all(w_copies(0, 0, n))
+
+    @pl.when(core == 1)
+    def _():
+        w_hand(0).start()
+
+    w_hand(0).wait_recv()
+
+    @pl.when(core == 1)
+    def _():
+        for n in range(4):
+            start_all(w_copies(1, 0, n))
 
     start_all(w_twin(core))
     rows, cols = pl.ds(chip * QUARTER, QUARTER), pl.ds(chip * WIDTH, WIDTH)
@@ -419,15 +455,9 @@
     for i in range(2):
         ag_forward(0, i)
 
-    @pl.when(core == 0)
-    def _():
-        for mtx in range(2):
-            for n in range(2):
-                w_pass_on(mtx, n)
-
-    @pl.when(core == 1)
-    def _():
-        w_from_twin(0)
+    for n in range(4):
+        w_pass_on(0, n)
+    w_arrived(0)
 
     def when_task(tick, first, last):
         def run(body):
@@ -449,15 +479,13 @@
         def _():
             start_all(ag_first(2, tick - 2, my_rows(g, tick - 2)))
 
-        for mtx in range(2):
-            for n in range(2):
-                @pl.when((tick == 2 * mtx + n) & (core == 1))
-                def _(mtx=mtx, n=n):
-                    start_all(w_copies(mtx, n))
-
-        @pl.when((tick == TURN + 1) & (core == 0))
-        def _():
-            w_from_twin(1)
+        @pl.when(tick < 4)
+        def _():
+            w_start(1, tick)
+
+        @pl.when(tick == TURN + 1)
+        def _():
+            w_arrived(1)
 
         @when_task(tick, 0, CHAIN)
         def _(task):
@@ -492,18 +520,18 @@
         def _():
             ag_forward(2, tick - 2)
 
-        for mtx in range(2):
-            for n in range(2):
-                @pl.when((tick == 2 * mtx + n) & (core == 1))
-                def _(mtx=mtx, n=n):
-                    w_pass_on(mtx, n)
+        @pl.when((tick >= 1) & (tick < 5))
+        def _():
+            w_pass_on(1, tick - 1)
+        when_task(tick, 0, CHUNKS)(forward_out)
+        when_task(tick, CHUNKS, CHAIN)(backward_out)
         return 0
 
     lax.fori_loop(0, CHAIN + 1 + SENT_TILES, tick_step, 0)
 
     for n, dst in enumerate((dwg, dwi)):
         for k, came in enumerate(near):
-            block = dst.at[:, pl.ds(came * WIDTH, WIDTH)]
+            block = dst.at[:, pl.ds(came * WIDTH, WIDTH - n * LATE_TILES * TILE)]
             local(block, block, gr_recv.at[n, k]).wait()
     for slot in range(SLOTS):
         grad_sent(slot)
@@ -530,12 +558,41 @@
     for task in (CHAIN - 2, CHAIN - 1):
         for copy in rs_second(task):
             copy.wait_send()
-    for mtx in range(2):
-        for n in range(2):
-            for copy in w_copies(mtx, n) + w_forwards(mtx, n, core):
+    for block in range(2):
+        for n in range(4):
+            for copy in w_copies(0, block, n) + w_forwards(0, block, n):
                 copy.wait_send()
-    for copy in w_twin(core):
+    for copy in w_twin(core) + (w_hand(0),):
         copy.wait_send()
+
+
+def settle_kernel(*refs):
+    for src, dst in zip(refs[:len(refs) // 2], refs[len(refs) // 2:]):
+        dst[...] = src[...]
+
+
+def settle(arrays, steps=16):
+    specs = [pl.BlockSpec((arr.shape[0] // steps, arr.shape[1]), lambda i: (i, 0)) for arr in arrays]
+    size = sum(arr.size * arr.dtype.itemsize for arr in arrays)
+    return pl.pallas_call(
+        settle_kernel, grid=(steps,), out_shape=[jax.ShapeDtypeStruct(arr.shape, arr.dtype) for arr in arrays], in_specs=specs, out_specs=specs,
+        name='settle', cost_estimate=pl.CostEstimate(flops=SETTLE_FLOPS, bytes_accessed=2 * size, transcendentals=0),
+        compiler_params=pltpu.CompilerParams(vmem_limit_bytes=48 * 2 ** 20),
+    )(*arrays)
+
+
+def insert_kernel(late, whole, out):
+    out[...] = late[0]
+
+
+def insert_late(whole, late):
+    chips, rows, cols = late.shape
+    step = rows // 2
+    return pl.pallas_call(
+        insert_kernel, grid=(chips, 2), out_shape=jax.ShapeDtypeStruct(whole.shape, whole.dtype),
+        in_specs=[pl.BlockSpec((1, step, cols), lambda c, r: (c, r, 0)), pl.BlockSpec(memory_space=pl.ANY)],
+        out_specs=pl.BlockSpec((step, cols), lambda c, r: (r, (c + 1) * (WIDTH // cols) - 1)), input_output_aliases={1: 0}, name='insert_late',
+    )(late, whole)
 
 
 def solution(mesh):
@@ -551,8 +608,8 @@
             return jax.ShapeDtypeStruct(shape, dtype)
 
         out_shapes = [
-            arr(*flat), arr(QUARTER, 4 * WIDTH, dtype=F32), arr(QUARTER, 4 * WIDTH, dtype=F32), arr(WIDTH, WIDTH, dtype=F32),
-            arr(4, CHUNKS, BLOCK_ROWS, WIDTH), arr(2, WIDTH, WIDTH), arr(2, WIDTH, WIDTH), arr(2, WIDTH, WIDTH),
+            arr(*flat), arr(QUARTER, 4 * WIDTH, dtype=F32), arr(QUARTER, 4 * WIDTH, dtype=F32), arr(WIDTH, WIDTH, dtype=F32), arr(4, QUARTER, LATE_TILES * TILE, dtype=F32),
+            arr(4, CHUNKS, BLOCK_ROWS, WIDTH), arr(2, WIDTH, WIDTH), arr(2, WIDTH, WIDTH), arr(2, WIDTH, WIDTH), arr(QUARTER, 4 * WIDTH),
             arr(CHAIN, 2, 2, ROWS, WIDTH, dtype=F32),
             arr(CHAIN, 2, ROWS, HALF, dtype=F32), arr(CHAIN, 2, ROWS, HALF, dtype=F32),
             arr(CHAIN, ROWS, HALF, dtype=F32), arr(CHAIN, ROWS, HALF, dtype=F32),
@@ -566,7 +623,7 @@
             pltpu.VMEM((2, ROWS, WIDTH), BF16), pltpu.VMEM((SLOTS, WIDTH, TILE), F32),
             pltpu.VMEM((2, QUARTER, TILE), F32),
             dma((4, CHUNKS, 4)), dma((4, CHUNKS, 4)), dma((CHAIN, 4)), dma((CHAIN, 4)),
-            dma((2, 2, 3)), dma((2, 2, 3)), dma((2, 2, 3)), dma((2, 2, 3)), dma((3,)), dma((3,)),
+            dma((2, 4, 3)), dma((2, 4, 3)), dma((2, 4, 3)), dma((2, 4, 3)), dma((4,)), dma((4,)),
             dma((5,)), dma((CHUNKS, 5)), dma((CHUNKS, 2)), dma((CHUNKS,)), dma((SLOTS, 4)), dma((2, 3)),
             dma((2,)), dma((4,)), dma((2, 4)), dma((2, 3)),
         ]
@@ -575,7 +632,10 @@
             scratch_shapes=scratch, name='mlp_step',
             compiler_params=pltpu.CompilerParams(collective_id=0, has_side_effects=True, vmem_limit_bytes=67_043_328),
         )(x.reshape(flat), g.reshape(flat), w_gate[0, 0], w_in[0, 0], w_out[0, 0])
-        dx, d_gate, d_in, d_out = results[:4]
+        dx, d_gate, d_in, d_out, late = results[:5]
+        late = lax.all_to_all(late, 'data', 0, 0)
+        dx, d_gate, d_in, d_out = settle((dx.reshape(-1, WIDTH), d_gate, d_in, d_out))
+        d_in = insert_late(d_in, late)
         return dx.reshape(x.shape), d_gate[None, None], d_in[None, None], d_out[None, None]
 
     return jax.shard_map(per_device, mesh=mesh, in_specs=(act_spec, act_spec, weight_spec, weight_spec, weight_spec),

time: 1280 us -> 1250 us (0.977)
  local copies, waits for them, and re-layouts: 37.5 us -> 2.18 us
    pallas_call x0 -> x2, Pallas kernels: none -> 43.2 us  [the longest x1 36.7 us: settle(): pl.pallas_call(settle_kernel, grid=(steps,), out_shape=[jax.ShapeDtypeStr...]
    pallas_call x1, Pallas kernels: 1220 us -> 1190 us  [per_device(): pl.pallas_call(step_kernel, out_shape=out_shapes, in_specs=[any_space] *...]
    unnamed x20 -> x2, local copies, waits for them, and re-layouts: 37.5 us -> 2.18 us
  transfers between devices with their start and end apart: 0 -> 1, of which waited for: 0 -> 1; matrix products, arithmetic and copies ran while one was open for 0% -> 0% of each run, Pallas kernels for 0% -> 3%
where the time goes in v4:
time: 1250 us; the launch traced here: 1240 us
  Pallas kernels  1230 us (98%)
    pallas_call x1, Pallas kernels, per_device(): pl.pallas_call(step_kernel, out_shape=out_shapes, in_specs=[any_space] *...  1190 us
    pallas_call x1, Pallas kernels, settle(): pl.pallas_call(settle_kernel, grid=(steps,), out_shape=[jax.ShapeDtypeStr...  36.7 us
  transfers between devices with their start and end apart: 1, of which 1 were waited for; matrix products, arithmetic and copies ran while one was open for 0% of the time, Pallas kernels for 3%

profile of v4, /device:TPU:0, one launch (start us, length us, event | category | flops | bytes accessed | tf_op | source)
XLA Modules:
  0.0 1243.5 jit_solution(559900990815257923)
XLA Ops:
  0.6 1185.3 %mlp_step.1 = (bf16[4,256,2048]{2,1,0:T(8,128)(2,1)}, f32[512,8192]{1,0:T(8,128)}, f32[512,8192]{1,0:T(8,128)}, f32[2048,2048]{1,0:T(8,128)}, f32[4,512,512]{2,1...) custom-call(bf16[4,256,2048]{2,1,0:T(8,128)(2,1)} %bitcast.15, ...), custom_call_target="tpu_custom_call" | custom-call | tf_op jit(solution)/shard_map/mlp_step/pallas_call | solution.py:630
  1186.0 4.8 all-to-all-start
  1190.8 0.0 copy-start
  1190.8 2.2 copy-done
  1193.0 36.7 %settle.1 = (bf16[1024,2048]{1,0:T(8,128)(2,1)}, f32[512,8192]{1,0:T(8,128)}, f32[512,8192]{1,0:T(8,128)}, f32[2048,2048]{1,0:T(8,128)}) custom-call(bf16[1024,2048]{1,0:T(8,128)(2,1)S(1)} %bitcast.10, f32[512,8192]{1,0:T(8,128)} %get-tuple-element.14.refs_1_, f32[512,8192]{1,0:T(8,128)} %get-tuple-element.15.refs_2_, f32[2048,2048]{1,0:T(8,128)} %get-tuple-element.16.refs_3_), custom_call_target="tpu_custom_call" | custom-call | flops 1073741824 | bytes 109051904 | tf_op jit(solution)/shard_map/settle/pallas_call | solution.py:577
  1229.7 7.2 all-to-all-done.late
  1236.9 6.6 insert_late.1
Async XLA Ops:
  1186.0 50.9 %all-to-all-start = ((f32[4,512,512]{2,1,0:T(8,128)}), f32[4,512,512]{2,1,0:T(8,128)}, u32[]{:S(2)}, u32[]{:S(2)}) async-start(f32[4,512,512]{2,1,0:T(8,128)} %get-tuple-element.19), calls=%async_computation | async-start | bytes 8388608 | tf_op jit(solution)/shard_map/all_to_all | solution.py:636
  1190.8 2.2 copy-start

commit v5 on v4

--- a/solution.py
+++ b/solution.py
@@ -20,6 +20,7 @@
 TILES = WIDTH // TILE
 CHAIN = 3 * CHUNKS
 TURN = CHUNKS
+G_TICKS = ((2, (0,)), (3, (1,)), (TURN + 1, (2, 3)))
 SENT_TILES = 2 * TILES
 LATE_TILES = 2
 SETTLE_FLOPS = 2 ** 30
@@ -470,14 +471,23 @@
                     body(task)
         return run
 
+    def when_g(tick):
+        def run(body):
+            for at, chunks in G_TICKS:
+                @pl.when(tick == at)
+                def _(chunks=chunks):
+                    for i in chunks:
+                        body(i)
+        return run
+
     def tick_step(tick, _):
         @pl.when(tick < 2)
         def _():
             start_all(ag_first(0, tick + 2, my_rows(x, tick + 2)))
 
-        @pl.when((tick >= 2) & (tick < 2 + CHUNKS))
-        def _():
-            start_all(ag_first(2, tick - 2, my_rows(g, tick - 2)))
+        @when_g(tick)
+        def _(i):
+            start_all(ag_first(2, i, my_rows(g, i)))
 
         @pl.when(tick < 4)
         def _():
@@ -516,9 +526,9 @@
         when_task(tick - 2, 0, CHAIN)(rs_last)
         when_task(tick - 1, 0, CHAIN)(rs_middle)
 
-        @pl.when((tick >= 2) & (tick < 2 + CHUNKS))
-        def _():
-            ag_forward(2, tick - 2)
+        @when_g(tick)
+        def _(i):
+            ag_forward(2, i)
 
         @pl.when((tick >= 1) & (tick < 5))
         def _():
@@ -577,7 +587,7 @@
     return pl.pallas_call(
         settle_kernel, grid=(steps,), out_shape=[jax.ShapeDtypeStruct(arr.shape, arr.dtype) for arr in arrays], in_specs=specs, out_specs=specs,
         name='settle', cost_estimate=pl.CostEstimate(flops=SETTLE_FLOPS, bytes_accessed=2 * size, transcendentals=0),
-        compiler_params=pltpu.CompilerParams(vmem_limit_bytes=48 * 2 ** 20),
+        compiler_params=pltpu.CompilerParams(vmem_limit_bytes=67_043_328),
     )(*arrays)
 
 
@@ -587,9 +597,9 @@
 
 def insert_late(whole, late):
     chips, rows, cols = late.shape
-    step = rows // 2
+    step = rows
     return pl.pallas_call(
-        insert_kernel, grid=(chips, 2), out_shape=jax.ShapeDtypeStruct(whole.shape, whole.dtype),
+        insert_kernel, grid=(chips, 1), out_shape=jax.ShapeDtypeStruct(whole.shape, whole.dtype),
         in_specs=[pl.BlockSpec((1, step, cols), lambda c, r: (c, r, 0)), pl.BlockSpec(memory_space=pl.ANY)],
         out_specs=pl.BlockSpec((step, cols), lambda c, r: (r, (c + 1) * (WIDTH // cols) - 1)), input_output_aliases={1: 0}, name='insert_late',
     )(late, whole)

time: 1250 us -> 1240 us (level)
  no operation moved by 1% of the time
where the time goes in v5:
time: 1240 us
  Pallas kernels  1230 us (99%)
    pallas_call x1, Pallas kernels, per_device(): pl.pallas_call(step_kernel, out_shape=out_shapes, in_specs=[any_space] *...  1190 us
    pallas_call x1, Pallas kernels, settle(): pl.pallas_call(settle_kernel, grid=(steps,), out_shape=[jax.ShapeDtypeStr...  38.1 us
  transfers between devices with their start and end apart: 1, of which 1 were waited for; matrix products, arithmetic and copies ran while one was open for 0% of the time, Pallas kernels for 3%

profile of v5, /device:TPU:0, one launch (start us, length us, event | category | flops | bytes accessed | tf_op | source)
XLA Modules:
  0.0 1241.5 jit_solution(8585163709618499632)
XLA Ops:
  0.6 1185.3 %mlp_step.1 = (bf16[4,256,2048]{2,1,0:T(8,128)(2,1)}, f32[512,8192]{1,0:T(8,128)}, f32[512,8192]{1,0:T(8,128)}, f32[2048,2048]{1,0:T(8,128)}, f32[4,512,512]{2,1...) custom-call(bf16[4,256,2048]{2,1,0:T(8,128)(2,1)} %bitcast.14, ...), custom_call_target="tpu_custom_call" | custom-call | tf_op jit(solution)/shard_map/mlp_step/pallas_call | solution.py:640
  1185.9 4.9 all-to-all-start
  1190.8 38.1 %settle.1 = (bf16[1024,2048]{1,0:T(8,128)(2,1)}, f32[512,8192]{1,0:T(8,128)}, f32[512,8192]{1,0:T(8,128)}, f32[2048,2048]{1,0:T(8,128)}) custom-call(bf16[1024,2048]{1,0:T(8,128)(2,1)} %bitcast.16, f32[512,8192]{1,0:T(8,128)} %get-tuple-element.14.refs_1_, f32[512,8192]{1,0:T(8,128)} %get-tuple-element.15.refs_2_, f32[2048,2048]{1,0:T(8,128)} %get-tuple-element.16.refs_3_), custom_call_target="tpu_custom_call" | custom-call | flops 1073741824 | bytes 109051904 | tf_op jit(solution)/shard_map/settle/pallas_call | solution.py:587
  1228.9 7.8 all-to-all-done.late
  1236.7 4.7 insert_late.1
Async XLA Ops:
  1185.9 50.8 %all-to-all-start = ((f32[4,512,512]{2,1,0:T(8,128)}), f32[4,512,512]{2,1,0:T(8,128)}, u32[]{:S(2)}, u32[]{:S(2)}) async-start(f32[4,512,512]{2,1,0:T(8,128)} %get-tuple-element.19), calls=%async_computation | async-start | bytes 8388608 | tf_op jit(solution)/shard_map/all_to_all | solution.py:646

commit v6 on v5

--- a/solution.py
+++ b/solution.py
@@ -32,6 +32,14 @@
     return lax.dot_general(lhs, rhs, (((1,), (rhs_dim,)), ((), ())), preferred_element_type=F32)
 
 
+def repeat(count, body):
+    def step(n, carry):
+        body(n)
+        return carry
+
+    lax.fori_loop(0, count, step, 0)
+
+
 def start_all(copies):
     for copy in copies:
         copy.start()
@@ -44,7 +52,7 @@
 
 
 def step_kernel(x, g, wg_in, wi_in, wo_in,
-                dx, dwg, dwi, dwo, late, act, wg, wi, wo, wx, part, ra1, rb1, ra2, rb2, lhs, rhs,
+                dx, dwg, dwi, dwo, late_far, late_x, late_y, late_own, act, wg, wi, wo, wx, part, ra1, rb1, ra2, rb2, lhs, rhs,
                 wbuf, ab, tb, dab, dbb, pst, keep, snd, ld, r2, own, new, outs, wo_out,
                 ag_send, ag_recv, rs_send, rs_recv, w_send, w_recv, f_send, f_recv, d_send, d_recv,
                 op_send, op_recv, dx_send, dx_recv, gr_send, gr_recv, p_sem, l_sem, t_sem, o_sem):
@@ -52,6 +60,7 @@
     core = lax.axis_index('stage')
     cx, cy = chip % 2, chip // 2
     near = (cy * 2 + (1 - cx), (1 - cy) * 2 + cx, (1 - cy) * 2 + (1 - cx))
+    far_first = (near[2], near[0], near[1])
     other = 1 - core
     x_dev, y_dev, twin = (near[0], core), (near[1], core), (chip, other)
 
@@ -126,7 +135,7 @@
         def _():
             dx_sent(i - 2)
 
-        def rows_step(r, _):
+        def rows_step(r):
             rows = pl.ds(r * 32, 32)
             total = keep[slot, rows, :] + r2[rows, :]
 
@@ -141,9 +150,8 @@
                 dot = jnp.mean(tok * total, axis=-1, keepdims=True)
                 resid = total * inv - tok * (inv * inv * inv * dot)
                 new[slot, rows, :] = (own[0, rows, :].astype(F32) + resid).astype(BF16)
-            return 0
-
-        lax.fori_loop(0, ROWS // 32, rows_step, 0)
+
+        repeat(ROWS // 32, rows_step)
 
         @pl.when(kind < 2)
         def _():
@@ -159,10 +167,10 @@
         src, dst = ((wg_in, wx), (wx, wi_in))[mtx][block], (wg, wi)[mtx]
         rows = pl.ds(chip * QUARTER + n * ROWS, ROWS)
         return [remote(src.at[pl.ds(n * ROWS, ROWS), pl.ds(to * WIDTH, WIDTH)], dst.at[block, rows],
-                       w_send.at[block, n, k], w_recv.at[block, n, k], (to, core)) for k, to in enumerate(near)]
+                       w_send.at[block, n, k], w_recv.at[block, n, k], (to, core)) for k, to in enumerate(far_first)]
 
     def w_forwards(mtx, block, n):
-        pieces = [(wg, wi)[mtx].at[block, pl.ds(came * QUARTER + n * ROWS, ROWS)] for came in near]
+        pieces = [(wg, wi)[mtx].at[block, pl.ds(came * QUARTER + n * ROWS, ROWS)] for came in far_first]
         return [remote(piece, piece, f_send.at[block, n, k], f_recv.at[block, n, k], twin) for k, piece in enumerate(pieces)]
 
     def w_start(block, n):
@@ -223,21 +231,20 @@
             remote(src, dst, op_send.at[n], op_recv.at[i, n], twin).wait_recv()
 
     def normalize():
-        def rows_step(r, _):
+        def rows_step(r):
             rows = pl.ds(r * 64, 64)
             tok = ab[0, rows, :].astype(F32)
             inv = lax.rsqrt(jnp.mean(tok * tok, axis=-1, keepdims=True) + EPS)
             ab[0, rows, :] = (tok * inv).astype(BF16)
-            return 0
-
-        lax.fori_loop(0, BLOCK_ROWS // 64, rows_step, 0)
+
+        repeat(BLOCK_ROWS // 64, rows_step)
 
     def write_partials(task, product):
         def tile_copy(n, slot):
             return local(pst.at[slot], part.at[task, :, :, :, pl.ds(n * TILE, TILE)], p_sem.at[slot])
 
-        def half_step(side, _):
-            def tile_step(t, _):
+        def half_step(side):
+            def tile_step(t):
                 n, slot = side * (TILES // 2) + t, t % 2
 
                 @pl.when(t >= 2)
@@ -246,9 +253,8 @@
 
                 pst[slot] = product(pl.ds(n * TILE, TILE)).reshape(2, 2, ROWS, TILE)
                 tile_copy(n, slot).start()
-                return 0
-
-            lax.fori_loop(0, TILES // 2, tile_step, 0)
+
+            repeat(TILES // 2, tile_step)
             last = (side + 1) * (TILES // 2)
             tile_copy(last - 2, 0).wait()
             tile_copy(last - 1, 1).wait()
@@ -256,23 +262,21 @@
                 @pl.when(side == n)
                 def _(n=n):
                     rs_first(task)[n].start()
-            return 0
-
-        lax.fori_loop(0, 2, half_step, 0)
+
+        repeat(2, half_step)
 
     def forward(task):
         ag_arrived(0, task)
         run_all((local(act.at[0, task], ab.at[0], l_sem.at[0]),))
         normalize()
 
-        def tile_step(t, _):
+        def tile_step(t):
             cols = pl.ds(t * TILE, TILE)
             pre_gate = mm(ab[0], wbuf[0, :, cols], 0)
             pre_in = mm(ab[0], wbuf[1, :, cols], 0)
             dab[:, cols] = (pre_gate * jax.nn.sigmoid(pre_gate) * pre_in).astype(BF16)
-            return 0
-
-        lax.fori_loop(0, TILES, tile_step, 0)
+
+        repeat(TILES, tile_step)
 
     def forward_out(task):
         write_partials(task, lambda cols: mm(dab[...], wbuf[2, :, cols], 0))
@@ -298,15 +302,14 @@
         op_start(4, i, block)
         normalize()
 
-        def turn_step(t, _):
+        def turn_step(t):
             cols = pl.ds(t * TILE, TILE)
             tb[0, cols, :] = ab[0, :, cols].T
-            return 0
-
-        lax.fori_loop(0, TILES, turn_step, 0)
+
+        repeat(TILES, turn_step)
         op_start(0, i, block)
 
-        def tile_step(t, _):
+        def tile_step(t):
             cols = pl.ds(t * TILE, TILE)
             pre_gate = mm(ab[0], wbuf[0, :, cols], 0)
             pre_in = mm(ab[0], wbuf[1, :, cols], 0)
@@ -316,9 +319,8 @@
             tb[1, cols, :] = (gate_act * pre_in).astype(BF16).T
             dab[:, cols] = (d_hidden * pre_in * sigma * (1.0 + pre_gate * (1.0 - sigma))).astype(BF16)
             dbb[:, cols] = (d_hidden * gate_act).astype(BF16)
-            return 0
-
-        lax.fori_loop(0, TILES, tile_step, 0)
+
+        repeat(TILES, tile_step)
         for n in (1, 2, 3):
             op_start(n, i, block)
 
@@ -351,8 +353,8 @@
         def _():
             grad_sent(slot)
 
-        def quarter_step(k, _):
-            ax, ay = 1 - k % 2, ((k + 1) // 2) % 2
+        def quarter_step(k):
+            ax, ay = 1 - k // 2, 1 - k % 2
             to = (cy + ay - 2 * cy * ay) * 2 + (cx + ax - 2 * cx * ax)
             rows = pl.ds(to * QUARTER, QUARTER)
             outs[slot, rows, :] = mm(wbuf[0, rows, :], tb[0, :, 0:TILE], 0) + mm(wbuf[1, rows, :], tb[0, :, TILE:2 * TILE], 0)
@@ -369,10 +371,12 @@
             @pl.when(t >= SENT_TILES - LATE_TILES)
             def _():
                 cols = pl.ds((t - SENT_TILES + LATE_TILES) * TILE, TILE)
-                local(outs.at[slot, rows], late.at[to, :, cols], gr_send.at[slot, k]).start()
-            return 0
-
-        lax.fori_loop(0, 4, quarter_step, 0)
+                for n, late in enumerate((late_far, late_x, late_y, late_own)):
+                    @pl.when(k == n)
+                    def _(late=late):
+                        local(outs.at[slot, rows], late.at[:, cols], gr_send.at[slot, k]).start()
+
+        repeat(4, quarter_step)
 
         @pl.when(t + 1 < SENT_TILES)
         def _():
@@ -390,7 +394,7 @@
         for copy in rhs_copies(2, n, 1):
             copy.wait()
 
-        def quarter_step(k, _):
+        def quarter_step(k):
             slot = k % 2
 
             @pl.when(k < 3)
@@ -407,9 +411,8 @@
             top, low = pl.ds(slot * HALF, QUARTER), pl.ds(slot * HALF + QUARTER, QUARTER)
             wo_out[slot] = mm(wbuf[2, top, :], tb[1, :, 0:TILE], 0) + mm(wbuf[2, low, :], tb[1, :, TILE:2 * TILE], 0)
             out_store(n, k, slot).start()
-            return 0
-
-        lax.fori_loop(0, 4, quarter_step, 0)
+
+        repeat(4, quarter_step)
 
     barrier = pltpu.get_barrier_semaphore()
     for dev in [(to, core) for to in near] + [twin]:
@@ -480,7 +483,7 @@
                         body(i)
         return run
 
-    def tick_step(tick, _):
+    def tick_step(tick):
         @pl.when(tick < 2)
         def _():
             start_all(ag_first(0, tick + 2, my_rows(x, tick + 2)))
@@ -535,12 +538,11 @@
             w_pass_on(1, tick - 1)
         when_task(tick, 0, CHUNKS)(forward_out)
         when_task(tick, CHUNKS, CHAIN)(backward_out)
-        return 0
-
-    lax.fori_loop(0, CHAIN + 1 + SENT_TILES, tick_step, 0)
+
+    repeat(CHAIN + 1 + SENT_TILES, tick_step)
 
     for n, dst in enumerate((dwg, dwi)):
-        for k, came in enumerate(near):
+        for k, came in enumerate((near[2], near[0], near[1])):
             block = dst.at[:, pl.ds(came * WIDTH, WIDTH - n * LATE_TILES * TILE)]
             local(block, block, gr_recv.at[n, k]).wait()
     for slot in range(SLOTS):
@@ -552,19 +554,17 @@
     dx_sent(2)
     dx_sent(3)
 
-    def drain_gathers(n, _):
+    def drain_gathers(n):
         kind, i = n // CHUNKS, n % CHUNKS
         for copy in ag_first(kind, i, shard(kind, i, 0)) + ag_second(kind, i):
             copy.wait_send()
-        return 0
-
-    def drain_sums(task, _):
+
+    def drain_sums(task):
         for copy in rs_first(task):
             copy.wait_send()
-        return 0
-
-    lax.fori_loop(0, 4 * CHUNKS, drain_gathers, 0)
-    lax.fori_loop(0, CHAIN, drain_sums, 0)
+
+    repeat(4 * CHUNKS, drain_gathers)
+    repeat(CHAIN, drain_sums)
     for task in (CHAIN - 2, CHAIN - 1):
         for copy in rs_second(task):
             copy.wait_send()
@@ -591,18 +591,22 @@
     )(*arrays)
 
 
-def insert_kernel(late, whole, out):
-    out[...] = late[0]
-
-
-def insert_late(whole, late):
-    chips, rows, cols = late.shape
-    step = rows
+def insert_kernel(spots, far, x_side, y_side, here, whole, out):
+    for k, late in enumerate((far, x_side, y_side, here)):
+        @pl.when(pl.program_id(0) == k)
+        def _(late=late):
+            out[...] = late[...]
+
+
+def insert_late(whole, late, spots):
+    rows, cols = late[0].shape
     return pl.pallas_call(
-        insert_kernel, grid=(chips, 1), out_shape=jax.ShapeDtypeStruct(whole.shape, whole.dtype),
-        in_specs=[pl.BlockSpec((1, step, cols), lambda c, r: (c, r, 0)), pl.BlockSpec(memory_space=pl.ANY)],
-        out_specs=pl.BlockSpec((step, cols), lambda c, r: (r, (c + 1) * (WIDTH // cols) - 1)), input_output_aliases={1: 0}, name='insert_late',
-    )(late, whole)
+        insert_kernel, out_shape=jax.ShapeDtypeStruct(whole.shape, whole.dtype),
+        grid_spec=pltpu.PrefetchScalarGridSpec(
+            num_scalar_prefetch=1, grid=(4,), in_specs=[pl.BlockSpec((rows, cols), lambda k, spots: (0, 0))] * 4 + [pl.BlockSpec(memory_space=pl.ANY)],
+            out_specs=pl.BlockSpec((rows, cols), lambda k, spots: (0, (spots[k] + 1) * (WIDTH // cols) - 1))),
+        input_output_aliases={5: 0}, name='insert_late',
+    )(spots, *late, whole)
 
 
 def solution(mesh):
@@ -618,7 +622,7 @@
             return jax.ShapeDtypeStruct(shape, dtype)
 
         out_shapes = [
-            arr(*flat), arr(QUARTER, 4 * WIDTH, dtype=F32), arr(QUARTER, 4 * WIDTH, dtype=F32), arr(WIDTH, WIDTH, dtype=F32), arr(4, QUARTER, LATE_TILES * TILE, dtype=F32),
+            arr(*flat), arr(QUARTER, 4 * WIDTH, dtype=F32), arr(QUARTER, 4 * WIDTH, dtype=F32), arr(WIDTH, WIDTH, dtype=F32), *[arr(QUARTER, LATE_TILES * TILE, dtype=F32)] * 4,
             arr(4, CHUNKS, BLOCK_ROWS, WIDTH), arr(2, WIDTH, WIDTH), arr(2, WIDTH, WIDTH), arr(2, WIDTH, WIDTH), arr(QUARTER, 4 * WIDTH),
             arr(CHAIN, 2, 2, ROWS, WIDTH, dtype=F32),
             arr(CHAIN, 2, ROWS, HALF, dtype=F32), arr(CHAIN, 2, ROWS, HALF, dtype=F32),
@@ -642,10 +646,13 @@
             scratch_shapes=scratch, name='mlp_step',
             compiler_params=pltpu.CompilerParams(collective_id=0, has_side_effects=True, vmem_limit_bytes=67_043_328),
         )(x.reshape(flat), g.reshape(flat), w_gate[0, 0], w_in[0, 0], w_out[0, 0])
-        dx, d_gate, d_in, d_out, late = results[:5]
-        late = lax.all_to_all(late, 'data', 0, 0)
+        dx, d_gate, d_in, d_out = results[:4]
+        chip = lax.axis_index('data')
+        hops = (3, 1, 2)
+        late = [lax.ppermute(tile, 'data', [(c, c ^ hop) for c in range(4)]) for tile, hop in zip(results[4:7], hops)] + [results[7]]
+        spots = jnp.stack([jnp.bitwise_xor(chip, hop) for hop in hops] + [chip]).astype(jnp.int32)
         dx, d_gate, d_in, d_out = settle((dx.reshape(-1, WIDTH), d_gate, d_in, d_out))
-        d_in = insert_late(d_in, late)
+        d_in = insert_late(d_in, late, spots)
         return dx.reshape(x.shape), d_gate[None, None], d_in[None, None], d_out[None, None]
 
     return jax.shard_map(per_device, mesh=mesh, in_specs=(act_spec, act_spec, weight_spec, weight_spec, weight_spec),

time: 1240 us -> 1240 us (level)
  transfers between devices with their start and end apart: 1 -> 3, of which waited for: 1 -> 1; matrix products, arithmetic and copies ran while one was open for 0% -> 0% of each run, Pallas kernels for 3% -> 3%
where the time goes in v6:
time: 1240 us
  Pallas kernels  1230 us (99%)
    pallas_call x1, Pallas kernels, per_device(): pl.pallas_call(step_kernel, out_shape=out_shapes, in_specs=[any_space] *...  1180 us
    pallas_call x1, Pallas kernels, settle(): pl.pallas_call(settle_kernel, grid=(steps,), out_shape=[jax.ShapeDtypeStr...  38.1 us
  transfers between devices with their start and end apart: 3, of which 1 were waited for; matrix products, arithmetic and copies ran while one was open for 0% of the time, Pallas kernels for 3%

profile of v6, /device:TPU:0, one launch (start us, length us, event | category | flops | bytes accessed | tf_op | source)
XLA Modules:
  0.0 1237.4 jit_solution(2214919734537589454)
XLA Ops:
  0.6 1184.7 %mlp_step.1 = (bf16[4,256,2048]{2,1,0:T(8,128)(2,1)}, f32[512,8192]{1,0:T(8,128)}, f32[512,8192]{1,0:T(8,128)}, f32[2048,2048]{1,0:T(8,128)}, f32[512,512]{1,0:T...) custom-call(bf16[4,256,2048]{2,1,0:T(8,128)(2,1)} %bitcast.18, ...), custom_call_target="tpu_custom_call" | custom-call | tf_op jit(solution)/shard_map/mlp_step/pallas_call | solution.py:644
  1185.4 1.0 collective-permute-start
  1186.4 1.7 collective-permute-start.1
  1188.1 0.8 collective-permute-start.2
  1188.9 38.1 %settle.1 = (bf16[1024,2048]{1,0:T(8,128)(2,1)}, f32[512,8192]{1,0:T(8,128)}, f32[512,8192]{1,0:T(8,128)}, f32[2048,2048]{1,0:T(8,128)}) custom-call(bf16[1024,2048]{1,0:T(8,128)(2,1)} %bitcast.20, f32[512,8192]{1,0:T(8,128)} %get-tuple-element.17.refs_1_, f32[512,8192]{1,0:T(8,128)} %get-tuple-element.18.refs_2_, f32[2048,2048]{1,0:T(8,128)} %get-tuple-element.19.refs_3_), custom_call_target="tpu_custom_call" | custom-call | flops 1073741824 | bytes 109051904 | tf_op jit(solution)/shard_map/settle/pallas_call | solution.py:587
  1226.9 0.7 pad_add_fusion.spots
  1227.6 0.0 collective-permute-done.far
  1227.6 4.4 collective-permute-done.1.x_side
  1232.0 0.0 collective-permute-done.2.y_side
  1232.1 5.3 insert_late.1
Async XLA Ops:
  1185.4 42.2 %collective-permute-start = (f32[512,512]{1,0:T(8,128)}, f32[512,512]{1,0:T(8,128)}, u32[]{:S(2)}, u32[]{:S(2)}) collective-permute-start(f32[512,512]{1,0:T(8,128)} %get-tuple-element.22), channel_id=1, source_target_pairs={{0,6},{2,4},{4,2},{6,0},{1,7},{3,5},{5,3},{7,1}} | collective-permute-start | bytes 3145736 | tf_op jit(solution)/shard_map/ppermute | solution.py:652
  1186.4 45.7 %collective-permute-start.1 = (f32[512,512]{1,0:T(8,128)}, f32[512,512]{1,0:T(8,128)}, u32[]{:S(2)}, u32[]{:S(2)}) collective-permute-start(f32[512,512]{1,0:T(8,128)} %get-tuple-element.23), channel_id=1, source_target_pairs={{0,2},{2,0},{4,6},{6,4},{1,3},{3,1},{5,7},{7,5}} | collective-permute-start | bytes 3145736 | tf_op jit(solution)/shard_map/ppermute | solution.py:652
  1188.1 44.0 %collective-permute-start.2 = (f32[512,512]{1,0:T(8,128)}, f32[512,512]{1,0:T(8,128)}, u32[]{:S(2)}, u32[]{:S(2)}) collective-permute-start(f32[512,512]{1,0:T(8,128)} %get-tuple-element.24), channel_id=1, source_target_pairs={{0,4},{2,6},{4,0},{6,2},{1,5},{3,7},{5,1},{7,3}} | collective-permute-start | bytes 3145736 | tf_op jit(solution)/shard_map/ppermute | solution.py:652

commit v7 on v1

v7 whole, which is shorter than its diff:
```python
import jax
import jax.numpy as jnp
from jax import lax
from jax.experimental import pallas as pl
from jax.experimental.pallas import tpu as pltpu
from jax.sharding import PartitionSpec as P

MESH = pl.DeviceIdType.MESH
F32 = jnp.float32
BF16 = jnp.bfloat16
EPS = 1e-6

CHUNKS = 4
ROWS = 128
BLOCK_ROWS = 4 * ROWS
WIDTH = 2048
HALF = WIDTH // 2
QUARTER = WIDTH // 4
TILE = 256
TILES = WIDTH // TILE
WIDE = 2 * TILE
WIDES = WIDTH // WIDE
PART = BLOCK_ROWS // 2
HIDDEN_TILES = 2 * WIDES
SUM_TILES = HALF // TILE
TASKS = 3 * CHUNKS
BACK_AT = 2 * CHUNKS
GRADS_AT = 4 * CHUNKS
SENT_TILES = 4 * TILES
SLOTS = 4
OUT_AT, OUT_EVERY = 8, 7
LATE_TILES = 6
LAG = 6
W_PASS, W_END = (2, 3), (7, 7)
TAKE_H1, PASS_H1 = 4, 6
PAIR = ZERO, ONE = range(2)
X, H1, G, E1 = range(4)


def mm(lhs, rhs, rhs_dim):
    return lax.dot_general(lhs, rhs, (((1,), (rhs_dim,)), ((), ())), preferred_element_type=F32)


def repeat(count, body):
    def step(n, carry):
        body(n)
        return carry

    lax.fori_loop(0, count, step, 0)


def start_all(copies):
    for copy in copies:
        copy.start()


def wait_all(copies):
    for copy in copies:
        copy.wait()


def run_all(copies):
    start_all(copies)
    wait_all(copies)


def step_kernel(x, g, wg_in, wi_in, wo_in,
                dx, dwg, dwi, dwo, late, act, wg, wi, wo, wx, part, rb, dots, kept, lhs_n, lhs_u, rhs_d, rhs_e,
                wcol, wrow, fab, ab, dd, ntb, utb, utw, pst, ld, tot, own, dsv, new, dxn, ecol, outs, wo_out,
                ag_send, ag_recv, rs_send, rs_recv, dt_send, dt_recv, w_send, w_recv, f_send, f_recv, h_send, h_recv, wo_send, wo_recv,
                op_send, op_recv, dx_send, dx_recv, gr_send, gr_recv, p_sem, l_sem, s_sem, k_sem, b_sem, o_sem, e_sem):
    chip = lax.axis_index('data')
    core = lax.axis_index('stage')
    cx, cy = chip % 2, chip // 2
    other = ONE - core
    x_chip, y_chip = cy * 2 + (ONE - cx), (ONE - cy) * 2 + cx
    twin = (chip, other)
    reds, nons = ((x_chip, core), (y_chip, core)), ((y_chip, core), (x_chip, core))
    rs, cs = (cx, cy), (cy, cx)

    def pick(pair, block):
        return pair[ZERO] + (pair[ONE] - pair[ZERO]) * block

    def red_of(block):
        return pick((x_chip, y_chip), block), core

    def local(src, dst, sem):
        return pltpu.make_async_copy(src, dst, sem)

    def remote(src, dst, send, recv, dev):
        return pltpu.make_async_remote_copy(src_ref=src, dst_ref=dst, send_sem=send, recv_sem=recv, device_id=dev, device_id_type=MESH)

    def arrived(ref, sem):
        local(ref, ref, sem).wait()

    def in_first(kind, i):
        block = kind // G
        mine = act.at[kind, :, :, i, ZERO, ZERO]
        return (remote(mine, act.at[kind, :, :, i, ONE, ZERO], ag_send.at[kind, i, ZERO], ag_recv.at[kind, i, ZERO], reds[block]),
                remote(mine, act.at[kind, :, :, i, ZERO, ONE], ag_send.at[kind, i, ONE], ag_recv.at[kind, i, ONE], nons[block]))

    def in_second(kind, i):
        block = kind // G
        return (remote(act.at[kind, :, :, i, ZERO, ONE], act.at[kind, :, :, i, ONE, ONE], ag_send.at[kind, i, 2], ag_recv.at[kind, i, 2], reds[block]),)

    def out_first(block, i):
        kind, c = (H1, E1)[block], cs[block]
        sends = [remote(act.at[kind, c, :, i, :, ZERO], act.at[kind, c, :, i, :, ONE], ag_send.at[kind, i, ZERO], ag_recv.at[kind, i, ZERO], reds[block])]
        for a in PAIR:
            sends.append(remote(act.at[kind, c, :, i, a, ZERO], act.at[kind, c, :, i, ONE - a, ZERO], ag_send.at[kind, i, ONE + a], ag_recv.at[kind, i, 2 - a], nons[block]))
        return sends

    def out_second(block, i):
        kind, c = (H1, E1)[block], cs[block]
        sends = []
        if block:
            sends.append(remote(act.at[kind, ONE - c, ZERO, i, :, ZERO], act.at[kind, ONE - c, ZERO, i, :, ONE], ag_send.at[kind, i, 3], ag_recv.at[kind, i, 3], reds[block]))
        for a in PAIR:
            for h in range(block, 2):
                sends.append(remote(act.at[kind, c, h, i, a, ONE], act.at[kind, c, h, i, ONE - a, ONE], ag_send.at[kind, i, 4 + 2 * a + h], ag_recv.at[kind, i, 6 - 2 * a + h], nons[block]))
        return sends

    def pass_on(first, second):
        for copy in first:
            copy.wait_recv()
        start_all(second)

    def all_recv(copies):
        for copy in copies:
            copy.wait_recv()

    def rs_copy(task):
        return remote(part.at[task, :, ONE], rb.at[task], rs_send.at[task], rs_recv.at[task], red_of((task // CHUNKS) % 2))

    def dot_copies(task):
        slot, n = task % 2, task - CHUNKS
        dev = pick((y_chip, x_chip), (task // CHUNKS) % 2), core
        return [remote(dsv.at[slot, b], dots.at[n, ONE - b], dt_send.at[n, b], dt_recv.at[n, ONE - b], dev) for b in PAIR]

    def own_half(kind_h, block, i):
        if block == ZERO:
            return act.at[X, cy, :, i, ZERO] if kind_h else act.at[E1, :, cy, i, ZERO]
        return act.at[H1, :, cx, i, ZERO] if kind_h else act.at[G, :, cx, i, ZERO]

    def rest_half(block, i):
        return act.at[X, ONE - cy, :, i, ZERO] if block == ZERO else act.at[H1, :, ONE - cx, i, ZERO]

    def when_kind(task):
        def run(body):
            for kind in range(3):
                @pl.when(task // CHUNKS == kind)
                def _(kind=kind):
                    body(kind)
        return run

    def send_result(block, i, slot):
        run_all([local(new.at[slot], act.at[(H1, E1)[block], cs[block], :, i, :, ZERO], l_sem.at[ZERO])])
        start_all(out_first(block, i))

    def pieces(body):
        def step(n):
            body(n // 4, (n // 2) % 2, pl.ds((n % 2) * (ROWS // 2), ROWS // 2))
        repeat(2 * 4, step)

    def rs_take(task):
        i, slot = task % CHUNKS, task % 2
        rs_copy(task).wait_recv()
        start_all([local(part.at[task, :, ZERO], ld.at[ZERO], l_sem.at[ZERO]), local(rb.at[task], ld.at[ONE], l_sem.at[ONE])])

        @when_kind(task)
        def _(kind):
            local(own_half(True, kind % 2, i), own.at[ZERO], l_sem.at[2]).start()

        wait_all([local(rb.at[task], ld.at[ZERO], l_sem.at[ZERO]), local(rb.at[task], ld.at[ONE], l_sem.at[ONE]), local(own_half(True, ZERO, i), own.at[ZERO], l_sem.at[2])])

        @pl.when(task < CHUNKS)
        def _():
            @pieces
            def _(q, b, rows):
                new[slot, q, b, rows, :] = own[ZERO, q, b, rows, :] + (ld[ZERO, q, b, rows, :] + ld[ONE, q, b, rows, :]).astype(BF16)

            send_result(ZERO, i, slot)

        @pl.when(task >= CHUNKS)
        def _():
            @pl.when(task >= CHUNKS + 2)
            def _():
                for copy in dot_copies(task - 2):
                    copy.wait_send()

            @pieces
            def _(q, b, rows):
                total = ld[ZERO, q, b, rows, :] + ld[ONE, q, b, rows, :]
                tot[slot, q, b, rows, :] = total
                dot = jnp.sum(total * own[ZERO, q, b, rows, :].astype(F32), axis=-ONE, keepdims=True) + jnp.zeros((ONE, ROWS), F32)

                @pl.when(q == ZERO)
                def _():
                    dsv[slot, b, rows, :] = dot

                @pl.when(q == ONE)
                def _():
                    dsv[slot, b, rows, :] = dsv[slot, b, rows, :] + dot

            start_all(dot_copies(task))

    def dx_copies(i, slot):
        spot = dx.at[i, pl.ds(core * ROWS, ROWS), pl.ds(cy * HALF, HALF)]
        return (local(dxn.at[slot, ZERO], spot, dx_send.at[i, ZERO]), remote(dxn.at[slot, ZERO], spot, dx_send.at[i, ONE], dx_recv.at[i, ZERO], twin),
                remote(dxn.at[slot, ONE], spot, dx_send.at[i, 2], dx_recv.at[i, ONE], (y_chip, core)),
                remote(dxn.at[slot, ONE], spot, dx_send.at[i, 3], dx_recv.at[i, 2], (y_chip, other)))

    def dx_sent(i):
        copies = dx_copies(i, i % 2)
        copies[ZERO].wait()
        for copy in copies[ONE:]:
            copy.wait_send()

    def rs_give(task):
        i, slot = task % CHUNKS, task % 2
        for b in PAIR:
            arrived(dots.at[task - CHUNKS, b], dt_recv.at[task - CHUNKS, b])
        local(dots.at[task - CHUNKS], ld.at[ZERO, ZERO, :, :, pl.ds(ZERO, ROWS)], l_sem.at[3]).start()
        for block in PAIR:
            @pl.when((task // CHUNKS) % 2 == block)
            def _(block=block):
                start_all([local(src, own.at[n], l_sem.at[n]) for n, src in enumerate((own_half(True, block, i), own_half(False, block, i), rest_half(block, i)))])
        wait_all([local(own_half(True, ZERO, i), own.at[n], l_sem.at[n]) for n in range(3)])
        local(dots.at[task - CHUNKS], ld.at[ZERO, ZERO, :, :, pl.ds(ZERO, ROWS)], l_sem.at[3]).wait()

        @pl.when(task >= 2 * CHUNKS + 2)
        def _():
            dx_sent(i - 2)

        def step(n):
            b, rows = n // 2, pl.ds((n % 2) * (ROWS // 2), ROWS // 2)

            def sq(slot_of, q):
                vals = own[slot_of, q, b, rows, :].astype(F32)
                return jnp.sum(vals * vals, axis=-ONE, keepdims=True)

            square = sq(ZERO, ZERO) + sq(ZERO, ONE) + sq(2, ZERO) + sq(2, ONE)
            inv = lax.rsqrt(square / WIDTH + EPS)
            dot = (dsv[slot, b, rows, ZERO:ONE] + ld[ZERO, ZERO, b, rows, ZERO:ONE]) / WIDTH
            for q in PAIR:
                tok = own[ZERO, q, b, rows, :].astype(F32)
                resid = tot[slot, q, b, rows, :] * inv - tok * (inv * inv * inv * dot)
                val = (own[ONE, q, b, rows, :].astype(F32) + resid).astype(BF16)
                new[slot, q, b, rows, :] = val
                dxn[slot, b, rows, pl.ds(q * QUARTER, QUARTER)] = val

        repeat(4, step)

        @pl.when(task < 2 * CHUNKS)
        def _():
            send_result(ONE, i, slot)

        @pl.when(task >= 2 * CHUNKS)
        def _():
            start_all(dx_copies(i, slot))

    def f_cols(block, place, fq):
        quarter = place + 2 * fq if block == ZERO else 2 * place + fq
        return pl.ds(quarter * WIDTH, WIDTH)

    def w_src(mtx, block):
        return ((wg_in, wx), (wx, wi_in))[mtx][block]

    def w_rows(mtx, block, fq, of):
        return (wg, wi)[mtx].at[block, fq, pl.ds(of * QUARTER, QUARTER)]

    def w_first(mtx, block, fq):
        src, mine = w_src(mtx, block), w_rows(mtx, block, fq, chip)
        return (remote(src.at[:, f_cols(block, rs[block], fq)], mine, w_send.at[block, fq, ZERO], w_recv.at[block, fq, ZERO], nons[block]),
                remote(src.at[:, f_cols(block, ONE - rs[block], fq)], mine, w_send.at[block, fq, ONE], w_recv.at[block, fq, ONE], reds[block]))

    def w_second(mtx, block, fq):
        piece = w_rows(mtx, block, fq, reds[block][ZERO])
        return remote(piece, piece, w_send.at[block, fq, 2], w_recv.at[block, fq, 2], nons[block])

    def w_twin(mtx, block, fq):
        far = 3 - chip
        srcs = [w_src(mtx, block).at[:, f_cols(block, rs[block], fq)]] + [w_rows(mtx, block, fq, of) for of in (nons[block][ZERO], reds[block][ZERO], far)]
        spots = [w_rows(mtx, block, fq, of) for of in (chip, nons[block][ZERO], reds[block][ZERO], far)]
        return [remote(src, spot, f_send.at[block, fq, n], f_recv.at[block, fq, n], twin) for n, (src, spot) in enumerate(zip(srcs, spots))]

    def per_mtx(body):
        for mtx in PAIR:
            @pl.when(core == mtx)
            def _(mtx=mtx):
                body(mtx)

    def w_start(block, to_red):
        @per_mtx
        def _(mtx):
            for fq in PAIR:
                w_first(mtx, block, fq)[to_red].start()
                if not to_red:
                    w_twin(mtx, block, fq)[ZERO].start()

    def w_pass(block, fq):
        @per_mtx
        def _(mtx):
            first, to_twin = w_first(mtx, block, fq), w_twin(mtx, block, fq)
            first[ONE].wait_recv()
            w_second(mtx, block, fq).start()
            to_twin[2].start()
            first[ZERO].wait_recv()
            to_twin[ONE].start()

    def w_end(block, fq):
        @per_mtx
        def _(mtx):
            w_second(mtx, block, fq).wait_recv()
            w_twin(mtx, block, fq)[3].start()

    def w_arrived(block):
        for fq in PAIR:
            all_recv(w_twin(ZERO, block, fq))

    def w_hand(mtx):
        return remote((wg_in, wi_in)[mtx], wx, h_send.at[ZERO], h_recv.at[ZERO], twin)

    def wo_copies(block, k):
        rows = pl.ds(k * QUARTER, QUARTER)
        spot, got = wo.at[block, cs[block], rows], wo.at[block, ONE - cs[block], rows]
        return (remote(wo_in.at[rows], spot, wo_send.at[block, ZERO, k], wo_recv.at[block, ZERO, k], twin),
                remote(wo_in.at[rows], spot, wo_send.at[block, ONE, k], wo_recv.at[block, ONE, k], nons[block]),
                remote(spot, spot, wo_send.at[block, ONE, k], wo_recv.at[block, ONE, k], nons[block]),
                remote(got, got, wo_send.at[block, 2, k], wo_recv.at[block, 2, k], twin))

    def halves(body):
        for half in PAIR:
            @pl.when(core == half)
            def _(half=half):
                for k in (2 * half, 2 * half + ONE):
                    body(k)

    def wo_hand(block):
        @pl.when(core == block)
        def _():
            for k in range(4):
                wo_copies(block, k)[ZERO].start()

    def wo_start(block):
        @pl.when(core == block)
        def _():
            for k in (2 * block, 2 * block + ONE):
                wo_copies(block, k)[ONE].start()

        @pl.when(core != block)
        def _():
            for k in range(4):
                wo_copies(block, k)[ZERO].wait_recv()
            for k in (2 - 2 * block, 3 - 2 * block):
                wo_copies(block, k)[2].start()

    def wo_pass(block):
        def body(k):
            wo_copies(block, k)[ONE].wait_recv()
            wo_copies(block, k)[3].start()
        halves(body)

    def wo_arrived(block):
        def body(k):
            wo_copies(block, 3 - k)[3].wait_recv()
        halves(body)

    def op_pairs(i, src):
        cols = pl.ds(i * BLOCK_ROWS, BLOCK_ROWS)
        return ((ntb, lhs_n.at[src, :, :, cols]), (utb, lhs_u.at[src, :, cols]), (dd.at[ZERO], rhs_d.at[ZERO, :, src, cols]),
                (dd.at[ONE], rhs_d.at[ONE, :, src, cols]), (ab.at[ONE], rhs_e.at[src, i]))

    def op_start(n, i, block):
        src, dst = op_pairs(i, core)[n]

        @pl.when(block == core)
        def _():
            local(src, dst, op_send.at[n]).start()

        @pl.when(block != core)
        def _():
            remote(src, dst, op_send.at[n], op_recv.at[i, n], twin).start()

    def op_sent(i):
        wait_all([local(src, dst, op_send.at[n]) for n, (src, dst) in enumerate(op_pairs(i, core))])

    def op_arrived(i):
        all_recv([remote(src, dst, op_send.at[n], op_recv.at[i, n], twin) for n, (src, dst) in enumerate(op_pairs(i, other))])

    def load_tokens(kind, i, slot):
        copies = []
        for hi in PAIR:
            for lo in PAIR:
                src = act.at[kind, lo, hi, i] if kind == E1 else act.at[kind, hi, lo, i]
                copies.append(local(src, ab.at[slot, :, :, :, pl.ds((2 * hi + lo) * QUARTER, QUARTER)], b_sem.at[slot, hi, lo]))
        return copies

    def tokens(slot):
        return ab[slot].reshape(BLOCK_ROWS, WIDTH)

    def normalize():
        def step(n):
            a, b, rows = n // 4, (n // 2) % 2, pl.ds((n % 2) * (ROWS // 2), ROWS // 2)
            tok = ab[ZERO, a, b, rows, :].astype(F32)
            inv = lax.rsqrt(jnp.mean(tok * tok, axis=-ONE, keepdims=True) + EPS)
            ab[ZERO, a, b, rows, :] = (tok * inv).astype(BF16)

        repeat(2 * 4, step)

    def stream(count, loads, body):
        start_all(loads(ZERO, ZERO))

        def step(n):
            slot = n % 2

            @pl.when(n + ONE < count)
            def _():
                start_all(loads(n + ONE, ONE - slot))

            wait_all(loads(n, slot))
            body(n, slot)

        repeat(count, step)

    def col_tile(n):
        return pl.ds((n % TILES) * TILE, TILE)

    def narrow(slot, n):
        return wcol.at[slot, n, :, pl.ds(ZERO, TILE)]

    def wide(n):
        return pl.ds((n % WIDES) * WIDE, WIDE)

    def w_cols(block, n, slot):
        return [local(src.at[block, n // WIDES, :, wide(n)], wcol.at[slot, m], s_sem.at[slot, m]) for m, src in enumerate((wg, wi))]

    def wo_rows(block, n, slot):
        return [local(wo.at[block, n // WIDES, pl.ds((n % WIDES) * WIDE + h * TILE, TILE)], wrow.at[slot, h], s_sem.at[slot, 2 + h]) for h in PAIR]

    def wo_tile(slot):
        return wrow[slot, ZERO:2].reshape(WIDE, WIDTH)

    def kept_load(which, i, n, slot):
        return local(kept.at[which, i, n], fab.at[which % 2, slot], k_sem.at[which % 2, slot])

    def kept_store(which, i, n, slot):
        return local(fab.at[which % 2, slot], kept.at[which, i, n], k_sem.at[which % 2, slot])

    def sum_cols(block, n):
        quarter = pick((2 * cy + n // 2, cx + 2 * (n // 2)), block)
        return pl.ds(quarter * QUARTER + (n % 2) * TILE, TILE)

    def sum_store(task, n, slot):
        return local(pst.at[slot], part.at[task, n // 2, :, :, :, pl.ds((n % 2) * TILE, TILE)], p_sem.at[slot])

    def write_sums(task, loads, product):
        def body(n, slot):
            @pl.when(n >= 2)
            def _():
                sum_store(task, n - 2, slot).wait()

            pst[slot] = product(slot).reshape(2, 2, ROWS, TILE)
            sum_store(task, n, slot).start()

        stream(SUM_TILES, loads, body)
        for slot in PAIR:
            sum_store(task, slot, slot).wait()
        rs_copy(task).start()

    def forward(i):
        all_recv(in_second(X, i))
        run_all(load_tokens(X, i, ZERO))
        normalize()

        def body(n, slot):
            pre_gate = mm(tokens(ZERO), wcol[slot, ZERO], ZERO)
            pre_in = mm(tokens(ZERO), wcol[slot, ONE], ZERO)

            @pl.when(n >= 2)
            def _():
                wait_all([kept_store(m, i, n - 2, slot) for m in PAIR])

            fab[ZERO, slot] = pre_gate
            fab[ONE, slot] = pre_in
            start_all([kept_store(m, i, n, slot) for m in PAIR])
            dd[i % 2, n // WIDES, :, wide(n)] = (pre_gate * jax.nn.sigmoid(pre_gate) * pre_in).astype(BF16)

        stream(HIDDEN_TILES, lambda n, slot: w_cols(ZERO, n, slot), body)
        wait_all([kept_store(m, i, slot, slot) for m in PAIR for slot in PAIR])

    def forward_out(i):
        def loads(n, slot):
            return [local(wo.at[ZERO, fq, :, sum_cols(ZERO, n)], narrow(slot, fq), s_sem.at[slot, fq]) for fq in PAIR]

        write_sums(i, loads, lambda slot: mm(dd[i % 2, ZERO], narrow(slot, ZERO)[...], ZERO) + mm(dd[i % 2, ONE], narrow(slot, ONE)[...], ZERO))

    def hidden_cotangent(i):
        all_recv(in_second(G, i))
        run_all(load_tokens(G, i, ONE))

        def body(n, slot):
            d_hidden = mm(tokens(ONE), wo_tile(slot), ONE)

            @pl.when(n >= 2)
            def _():
                kept_store(2, i, n - 2, slot).wait()

            fab[ZERO, slot] = d_hidden
            kept_store(2, i, n, slot).start()

        stream(HIDDEN_TILES, lambda n, slot: wo_rows(ONE, n, slot), body)
        wait_all([kept_store(2, i, slot, slot) for slot in PAIR])

    def gradients_of(n, h, pre_gate, pre_in, d_hidden):
        rows = pl.ds(h * PART, PART)
        sigma = jax.nn.sigmoid(pre_gate)
        gate_act = pre_gate * sigma
        utw[rows, :] = (gate_act * pre_in).astype(BF16)
        dd[ZERO, n // WIDES, rows, wide(n)] = (d_hidden * pre_in * sigma * (1.0 + pre_gate * (1.0 - sigma))).astype(BF16)
        dd[ONE, n // WIDES, rows, wide(n)] = (d_hidden * gate_act).astype(BF16)

    def keep_u(n, keeps_u):
        @pl.when(n // WIDES == keeps_u)
        def _():
            utb[wide(n), :] = utw[...].T

    def part_of(slot, h):
        return ab[slot, h].reshape(PART, WIDTH)

    def backward(task):
        i = task % CHUNKS
        block = (task // CHUNKS) % 2

        @pl.when(task > CHUNKS)
        def _():
            op_sent(i)

        @pl.when(block == ONE)
        def _():
            all_recv(out_second(ZERO, i))
            start_all(load_tokens(H1, i, ZERO) + load_tokens(G, i, ONE))

        @pl.when(block == ZERO)
        def _():
            all_recv(out_second(ONE, i))
            start_all(load_tokens(X, i, ZERO) + load_tokens(E1, i, ONE))

        wait_all(load_tokens(X, i, ZERO) + load_tokens(X, i, ONE))
        op_start(4, i, block)
        normalize()

        def turn(n):
            ntb[n] = ab[ZERO, :, :, :, sum_cols(block, n)].reshape(BLOCK_ROWS, TILE).T

        repeat(SUM_TILES, turn)
        op_start(ZERO, i, block)

        @pl.when(block == ONE)
        def _():
            def body(n, slot):
                for h in PAIR:
                    pre_gate = mm(part_of(ZERO, h), wcol[slot, ZERO], ZERO)
                    pre_in = mm(part_of(ZERO, h), wcol[slot, ONE], ZERO)
                    gradients_of(n, h, pre_gate, pre_in, fab[ZERO, slot, pl.ds(h * PART, PART)])
                keep_u(n, cx)

            stream(HIDDEN_TILES, lambda n, slot: w_cols(ONE, n, slot) + [kept_load(2, i, n, slot)], body)

        @pl.when(block == ZERO)
        def _():
            def body(n, slot):
                for h in PAIR:
                    rows = pl.ds(h * PART, PART)
                    gradients_of(n, h, fab[ZERO, slot, rows], fab[ONE, slot, rows], mm(part_of(ONE, h), wo_tile(slot), ONE))
                keep_u(n, cy)

            stream(HIDDEN_TILES, lambda n, slot: wo_rows(ZERO, n, slot) + [kept_load(m, i, n, slot) for m in PAIR], body)

        for n in (ONE, 2, 3):
            op_start(n, i, block)

    def backward_out(task):
        block = (task // CHUNKS) % 2

        def loads(n, slot):
            return [local(src.at[block, fq, sum_cols(block, n)], wrow.at[slot, 2 * m + fq], s_sem.at[slot, 2 * m + fq])
                    for m, src in enumerate((wg, wi)) for fq in PAIR]

        def product(slot):
            return sum(mm(dd[m, fq], wrow[slot, 2 * m + fq], ONE) for m in PAIR for fq in PAIR)

        write_sums(task, loads, product)

    def grad_loads(t, slot):
        return [local(rhs_d.at[t // (2 * TILES), (t // TILES) % 2, q, :, col_tile(t)], narrow(slot, q), s_sem.at[slot, q]) for q in PAIR]

    def grad_cols(t, place):
        fq = (t // TILES) % 2
        quarter = pick((place + 2 * fq, 2 * place + fq), core)
        return quarter * WIDTH + (t % TILES) * TILE

    def grad_sent(slot):
        for q in PAIR:
            local(outs.at[slot, q], dwg.at[:, pl.ds(ZERO, TILE)], gr_send.at[slot, q]).wait()

    my_place = pick(rs, core)

    def grad_tile(t):
        mtx, slot, at = t // (2 * TILES), t % SLOTS, t % 2

        @pl.when(t == ZERO)
        def _():
            op_sent(ZERO)
            for i in range(CHUNKS):
                op_arrived(i)
            start_all(grad_loads(ZERO, ZERO))
            run_all([local(lhs_n.at[q], wrow.at[q], l_sem.at[q]) for q in PAIR])

        @pl.when(t + ONE < SENT_TILES)
        def _():
            start_all(grad_loads(t + ONE, ONE - at))

        wait_all(grad_loads(t, at))

        @pl.when(t >= SLOTS)
        def _():
            grad_sent(slot)

        def half(n):
            q = (ONE - my_place) * (ONE - n) + my_place * n

            def rows(src):
                return wrow[src, pl.ds(2 * q, 2)].reshape(QUARTER, WIDTH)

            outs[slot, q] = mm(rows(ZERO), narrow(at, ZERO)[...], ZERO) + mm(rows(ONE), narrow(at, ONE)[...], ZERO)
            cols = pl.ds(grad_cols(t, my_place), TILE)
            for m, dst in enumerate((dwg, dwi)):
                @pl.when((mtx == m) & (n == ZERO) & (t < SENT_TILES - LATE_TILES))
                def _(m=m, dst=dst):
                    remote(outs.at[slot, q], dst.at[:, cols], gr_send.at[slot, q], gr_recv.at[m, (t // TILES) % 2], red_of(core)).start()

                @pl.when((mtx == m) & (n == ONE))
                def _(dst=dst):
                    local(outs.at[slot, q], dst.at[:, cols], gr_send.at[slot, q]).start()

            @pl.when((n == ZERO) & (t >= SENT_TILES - LATE_TILES))
            def _():
                local(outs.at[slot, q], late.at[:, pl.ds((t - SENT_TILES + LATE_TILES) * TILE, TILE)], gr_send.at[slot, q]).start()

        repeat(2, half)

    def out_loads(k, slot):
        return [local(lhs_u.at[q, pl.ds(k * QUARTER, QUARTER)], dd.at[slot, q], o_sem.at[slot, q]) for q in PAIR]

    def out_store(n, k, slot):
        return local(wo_out.at[slot], dwo.at[pl.ds(k * QUARTER, QUARTER), pl.ds(n * WIDE, WIDE)], o_sem.at[slot, 2])

    def out_tile(n):
        e_loads = [local(rhs_e.at[q, :, :, :, :, pl.ds(n * WIDE, WIDE)], ecol.at[q], e_sem.at[q]) for q in PAIR]
        start_all(e_loads + out_loads(ZERO, ZERO))
        wait_all(e_loads)

        def quarter(k):
            slot = k % 2

            @pl.when(k < 3)
            def _():
                start_all(out_loads(k + ONE, ONE - slot))

            wait_all(out_loads(k, slot))

            @pl.when(4 * n + k >= 2)
            def _():
                out_store(n, k, slot).wait()

            wo_out[slot] = mm(dd[slot, ZERO], ecol[ZERO].reshape(WIDTH, WIDE), ZERO) + mm(dd[slot, ONE], ecol[ONE].reshape(WIDTH, WIDE), ZERO)
            out_store(n, k, slot).start()

        repeat(4, quarter)

    barrier = pltpu.get_barrier_semaphore()
    for dev in (reds[ZERO], nons[ZERO], twin, (y_chip, other)):
        pl.semaphore_signal(barrier, inc=ONE, device_id=dev, device_id_type=MESH)
    pl.semaphore_wait(barrier, 4)

    for block in PAIR:
        wo_hand(block)
    per_mtx(lambda mtx: w_hand(ONE - mtx if mtx == ZERO else ZERO).start())

    def given(arr, i):
        return arr.at[i, pl.ds(core * ROWS, ROWS)]

    spots = [[ab.at[n, i // 2, i % 2] for i in range(CHUNKS)] for n in PAIR]
    run_all([local(given(arr, i), spots[n][i], b_sem.at[n, i // 2, i % 2]) for n, arr in enumerate((x, g)) for i in range(CHUNKS)])
    for hi in PAIR:
        for lo in PAIR:
            cols = pl.ds((2 * hi + lo) * QUARTER, QUARTER)
            run_all([local(spots[n][i].at[:, cols], act.at[kind, hi, lo, i, ZERO, ZERO], b_sem.at[n, i // 2, i % 2]) for n, kind in enumerate((X, G)) for i in range(CHUNKS)])

    start_all(in_first(X, ZERO))

    @pl.when(core == ZERO)
    def _():
        for to_red in (ONE, ZERO):
            w_start(ZERO, to_red)

    w_hand(ZERO).wait_recv()

    @pl.when(core == ONE)
    def _():
        for to_red in (ONE, ZERO):
            w_start(ZERO, to_red)

    for i in range(ONE, CHUNKS):
        start_all(in_first(X, i))

    @per_mtx
    def _(mtx):
        for block in PAIR:
            run_all([local(w_src(mtx, block).at[:, f_cols(block, rs[block], fq)], dd.at[ZERO, fq], o_sem.at[ZERO, fq]) for fq in PAIR])
            run_all([local(dd.at[ZERO, fq], w_rows(mtx, block, fq, chip), o_sem.at[ZERO, fq]) for fq in PAIR])
        rows = [pl.ds(k * QUARTER, QUARTER) for k in range(4)]
        run_all([local(wo_in.at[rows[k]], dd.at[k // 2, k % 2], o_sem.at[k // 2, k % 2]) for k in range(4)])
        run_all([local(dd.at[k // 2, k % 2], wo.at[mtx, cs[mtx], rows[k]], o_sem.at[k // 2, k % 2]) for k in range(4)])

    pass_on(in_first(X, ZERO), in_second(X, ZERO))
    for fq in PAIR:
        w_pass(ZERO, fq)
    for i in range(ONE, CHUNKS):
        pass_on(in_first(X, i), in_second(X, i))
    wo_start(ONE)
    wo_start(ZERO)
    w_start(ONE, ZERO)

    @pl.when(core == ZERO)
    def _():
        w_start(ONE, ONE)

    for fq in PAIR:
        w_end(ZERO, fq)
    w_arrived(ZERO)

    def when_forward(tick):
        def run(body):
            @pl.when((tick >= ZERO) & (tick < CHUNKS))
            def _():
                body(tick)
        return run

    def in_two_parts(offset, late):
        def run(body):
            @pl.when(((offset >= ZERO) & (offset < 2)) | ((offset >= late) & (offset < late + 2)))
            def _():
                body(jnp.where(offset < 2, offset, offset - late + 2))
        return run

    def tick_step(tick):
        for n in PAIR:
            @pl.when(tick == n)
            def _(n=n):
                for i in PAIR:
                    start_all(in_first(G, 2 * n + i))

        @pl.when(tick == CHUNKS)
        def _():
            wo_pass(ONE)
            wo_arrived(ONE)

        @pl.when(tick == BACK_AT)
        def _():
            w_arrived(ONE)

        when_forward(tick)(forward)

        @pl.when((tick >= CHUNKS) & (tick < BACK_AT))
        def _():
            hidden_cotangent(tick - CHUNKS)

        @pl.when((tick >= BACK_AT) & (tick < GRADS_AT))
        def _():
            backward(tick - CHUNKS)

        @pl.when(tick >= GRADS_AT)
        def _():
            grad_tile(tick - GRADS_AT)

        grad = tick - GRADS_AT

        @pl.when((grad >= OUT_AT) & ((grad - OUT_AT) % OUT_EVERY == ZERO))
        def _():
            out_tile((grad - OUT_AT) // OUT_EVERY)

        @in_two_parts(tick - PASS_H1, BACK_AT + ONE - PASS_H1)
        def _(i):
            pass_on(out_first(ZERO, i), out_second(ZERO, i))

        @pl.when((tick >= BACK_AT + 3) & (tick < BACK_AT + 3 + CHUNKS))
        def _():
            i = tick - BACK_AT - 3
            pass_on(out_first(ONE, i), out_second(ONE, i))

        last_give = tick == GRADS_AT + 2 * LAG

        @pl.when(((tick >= BACK_AT + 2) & (tick < GRADS_AT + ONE)) | last_give)
        def _():
            rs_give(jnp.where(last_give, TASKS - ONE, tick - CHUNKS - 2))

        in_two_parts(tick - TAKE_H1, BACK_AT - TAKE_H1)(rs_take)

        last_take = tick == GRADS_AT + LAG

        @pl.when(((tick >= BACK_AT + ONE) & (tick < GRADS_AT)) | last_take)
        def _():
            rs_take(jnp.where(last_take, TASKS - ONE, tick - CHUNKS - ONE))

        @pl.when(tick == ONE)
        def _():
            wo_pass(ZERO)
            wo_arrived(ZERO)

            @pl.when(core == ONE)
            def _():
                w_start(ONE, ONE)

        when_forward(tick - ONE)(forward_out)

        for n in PAIR:
            @pl.when(tick == 3 + n)
            def _(n=n):
                for i in PAIR:
                    pass_on(in_first(G, 2 * n + i), in_second(G, 2 * n + i))

            @pl.when(tick == W_PASS[n])
            def _(n=n):
                w_pass(ONE, n)

            @pl.when(tick == W_END[n])
            def _(n=n):
                w_end(ONE, n)

        @pl.when((tick >= BACK_AT) & (tick < GRADS_AT))
        def _():
            backward_out(tick - CHUNKS)

    repeat(GRADS_AT + SENT_TILES, tick_step)

    for m, dst in enumerate((dwg, dwi)):
        for fq in PAIR:
            arrived(dst.at[:, pl.ds(pick((ONE - cx + 2 * fq, 2 * (ONE - cy) + fq), core) * WIDTH, WIDTH - m * fq * LATE_TILES * TILE)], gr_recv.at[m, fq])
    for slot in range(SLOTS):
        grad_sent(slot)
    for slot in PAIR:
        out_store(ZERO, ZERO, slot).wait()
    for i in range(CHUNKS):
        all_recv(dx_copies(i, ZERO)[ONE:])
    for i in (CHUNKS - 2, CHUNKS - ONE):
        dx_sent(i)

    def sent(copies):
        for copy in copies:
            copy.wait_send()

    for i in range(CHUNKS):
        for kind in (X, G):
            sent(in_first(kind, i) + in_second(kind, i))
        for block in PAIR:
            sent(out_first(block, i) + out_second(block, i))
    repeat(TASKS, lambda task: rs_copy(task).wait_send())
    for task in (TASKS - 2, TASKS - ONE):
        sent(dot_copies(task))
    for block in PAIR:
        for fq in PAIR:
            sent(w_first(ZERO, block, fq) + (w_second(ZERO, block, fq),))
            sent(w_twin(ZERO, block, fq))
    for k in range(4):
        for block in PAIR:
            @pl.when(core == block)
            def _(block=block, k=k):
                wo_copies(block, k)[ZERO].wait_send()

    def wo_sent(k):
        for block in PAIR:
            sent((wo_copies(block, k)[ONE], wo_copies(block, k)[3]))

    halves(wo_sent)
    w_hand(ZERO).wait_send()


def settle_kernel(*refs):
    for src, dst in zip(refs[:4], refs[4:]):
        dst[...] = src[...]


def settle(arrays, steps=16):
    specs = [pl.BlockSpec((arr.shape[0] // steps, arr.shape[1]), lambda i: (i, 0)) for arr in arrays]
    size = sum(arr.size * arr.dtype.itemsize for arr in arrays)
    return pl.pallas_call(
        settle_kernel, grid=(steps,), out_shape=[jax.ShapeDtypeStruct(arr.shape, arr.dtype) for arr in arrays], in_specs=specs, out_specs=specs,
        name='settle', cost_estimate=pl.CostEstimate(flops=2 ** 30, bytes_accessed=2 * size, transcendentals=0),
        compiler_params=pltpu.CompilerParams(vmem_limit_bytes=67_043_328),
    )(*arrays)


def insert_kernel(spot, late, whole, out):
    out[...] = late[...]


def insert_late(whole, late, spot):
    block = (QUARTER, QUARTER)
    return pl.pallas_call(
        insert_kernel, out_shape=jax.ShapeDtypeStruct(whole.shape, whole.dtype),
        grid_spec=pltpu.PrefetchScalarGridSpec(
            num_scalar_prefetch=1, grid=(3,), in_specs=[pl.BlockSpec(block, lambda k, spot: (0, k)), pl.BlockSpec(memory_space=pl.ANY)],
            out_specs=pl.BlockSpec(block, lambda k, spot: (0, 4 * spot[0] + 1 + k))),
        input_output_aliases={2: 0}, name='insert_late',
    )(spot, late, whole)


def solution(mesh):
    act_spec = P(None, 'data', None, None)
    weight_spec = P('stage', None, 'data', None)

    def per_device(x, g, w_gate, w_in, w_out):
        flat = (CHUNKS, 2 * ROWS, WIDTH)
        any_space = pl.BlockSpec(memory_space=pl.ANY)
        pair = (2, 2)

        def arr(*shape, dtype=BF16):
            return jax.ShapeDtypeStruct(shape, dtype)

        def f32(*shape):
            return arr(*shape, dtype=F32)

        piece = (*pair, ROWS, QUARTER)
        out_shapes = [
            arr(*flat), f32(QUARTER, 4 * WIDTH), f32(QUARTER, 4 * WIDTH), f32(WIDTH, WIDTH), f32(QUARTER, LATE_TILES * TILE),
            arr(4, *pair, CHUNKS, *pair, ROWS, QUARTER), *[arr(*pair, WIDTH, WIDTH)] * 3, arr(QUARTER, 4 * WIDTH),
            f32(TASKS, 2, *piece), f32(TASKS, *piece), f32(2 * CHUNKS, 2, ROWS, ROWS), f32(3, CHUNKS, HIDDEN_TILES, BLOCK_ROWS, WIDE),
            arr(2, SUM_TILES, TILE, WIDTH), arr(2, WIDTH, WIDTH), arr(*pair, 2, WIDTH, WIDTH), arr(2, CHUNKS, *pair, ROWS, WIDTH),
        ]

        def bf(*shape):
            return pltpu.VMEM(shape, BF16)

        def fl(*shape):
            return pltpu.VMEM(shape, F32)

        scratch = [
            bf(*pair, WIDTH, WIDE), bf(2, 4, TILE, WIDTH), fl(*pair, BLOCK_ROWS, WIDE), bf(2, *pair, ROWS, WIDTH), bf(*pair, BLOCK_ROWS, WIDTH),
            bf(SUM_TILES, TILE, BLOCK_ROWS), bf(WIDTH, BLOCK_ROWS), bf(BLOCK_ROWS, WIDE), fl(2, *pair, ROWS, TILE), fl(2, *piece), fl(2, *piece), bf(3, *piece),
            fl(2, 2, ROWS, ROWS), bf(2, *piece), bf(2, 2, ROWS, HALF), bf(2, CHUNKS, *pair, ROWS, WIDE), fl(SLOTS, 2, QUARTER, TILE), fl(2, QUARTER, WIDE),
        ]
        counts = [(4, CHUNKS, 8), (4, CHUNKS, 8), (TASKS,), (TASKS,), (2 * CHUNKS, 2), (2 * CHUNKS, 2), (*pair, 3), (*pair, 3), (*pair, 4), (*pair, 4),
                  (1,), (1,), (2, 3, 4), (2, 3, 4), (5,), (CHUNKS, 5), (CHUNKS, 4), (CHUNKS, 3), (SLOTS, 2), pair, (2,), (4,), (2, 4), pair, (2, *pair), (2, 3), (2,)]
        results = pl.pallas_call(
            step_kernel, out_shape=out_shapes, in_specs=[any_space] * 5, out_specs=[any_space] * len(out_shapes),
            scratch_shapes=scratch + [pltpu.SemaphoreType.DMA(count) for count in counts], name='mlp_step',
            compiler_params=pltpu.CompilerParams(collective_id=0, has_side_effects=True, vmem_limit_bytes=67_043_328),
        )(x.reshape(flat), g.reshape(flat), w_gate[0, 0], w_in[0, 0], w_out[0, 0])
        late = lax.ppermute(results[4], ('data', 'stage'), [(2 * c + s, 2 * (c ^ (1 + s)) + s) for c in range(4) for s in PAIR])
        chip, core = lax.axis_index('data'), lax.axis_index('stage')
        spot = jnp.where(core == 0, 3 - chip % 2, 3 - 2 * (chip // 2))
        dx, d_gate, d_in, d_out = settle((results[0].reshape(-1, WIDTH), *results[1:4]))
        d_in = insert_late(d_in, late, spot.astype(jnp.int32).reshape(1))
        return dx.reshape(x.shape), d_gate[None, None], d_in[None, None], d_out[None, None]

    return jax.shard_map(per_device, mesh=mesh, in_specs=(act_spec, act_spec, weight_spec, weight_spec, weight_spec),
                         out_specs=(act_spec, weight_spec, weight_spec, weight_spec), check_vma=False)
```

time: 1710 us -> 1220 us (0.71)
  Pallas kernels: 0 us -> 1200 us
  waiting for transfers between devices: 842 us -> 0.01 us
  matrix products: 478 us -> 0 us
  local copies, waits for them, and re-layouts: 140 us -> 0 us
  other arithmetic: 110 us -> 0 us
  blocking collectives: 99.8 us -> 0 us
  starting transfers between devices: 22.1 us -> 1.57 us
    pallas_call x0 -> x3, Pallas kernels: none -> 1200 us  [the longest x1 1160 us: per_device(): pl.pallas_call(step_kernel, out_shape=out_shapes, in_specs=[any_space] *...]
    dot_general x28 -> x0, matrix products: 478 us -> none  [mm(): lax.dot_general(lhs, rhs, (((lhs_dim,), (rhs_dim,)), ((), ())), preferred...]
    all_to_all x3 -> x0, waiting for transfers between devices: 446 us -> none  [the longest x2 322 us: rows_of(): pieces = lax.all_to_all(full.reshape(chips, -1, cols), 'data', 0, 0)]
    all_gather x12 -> x0, waiting for transfers between devices: 198 us -> none  [the longest x8 181 us: everywhere(): return lax.all_gather(rows, 'data', axis=0, tiled=True)]
    reduce_scatter x9 -> x0, waiting for transfers between devices: 196 us -> none  [the longest x6 196 us: summed(): return lax.psum_scatter(partial, 'data', scatter_dimension=0, tiled=True)]
    all_to_all x1 -> x0, blocking collectives: 99.8 us -> none  [columns_of(): pieces = lax.all_to_all(shard.reshape(-1, chips, cols), 'data', 1, 0)]
    another operation x6 -> x0, other arithmetic: 59.6 us -> none  [the longest x3 55.3 us: per_device(): jnp.stack(parts)]
    transpose x2 -> x0, local copies, waits for them, and re-layouts: 41.8 us -> none  [rows_of(): return pieces.transpose(1, 0, 2).reshape(1, 1, -1, ffn)]
  transfers between devices with their start and end apart: 24 -> 1, of which waited for: 15 -> 0; matrix products, arithmetic and copies ran while one was open for 41% -> 0% of each run, Pallas kernels for 0% -> 3%
where the time goes in v7:
time: 1220 us; the launch traced here: 1210 us
  Pallas kernels  1200 us (98%)
    pallas_call x1, Pallas kernels, per_device(): pl.pallas_call(step_kernel, out_shape=out_shapes, in_specs=[any_space] *...  1160 us
    pallas_call x1, Pallas kernels, settle(): pl.pallas_call(settle_kernel, grid=(steps,), out_shape=[jax.ShapeDtypeStr...  38.1 us
  transfers between devices with their start and end apart: 1, of which 0 were waited for; matrix products, arithmetic and copies ran while one was open for 0% of the time, Pallas kernels for 3%

profile of v7, /device:TPU:0, one launch (start us, length us, event | category | flops | bytes accessed | tf_op | source)
XLA Modules:
  0.0 1206.1 jit_solution(10890321194590792813)
XLA Ops:
  0.6 1161.5 %mlp_step.1 = (bf16[4,256,2048]{2,1,0:T(8,128)(2,1)}, f32[512,8192]{1,0:T(8,128)}, f32[512,8192]{1,0:T(8,128)}, f32[2048,2048]{1,0:T(8,128)}, f32[512,1536]{1,0:...) custom-call(bf16[4,256,2048]{2,1,0:T(8,128)(2,1)} %bitcast.15, ...), custom_call_target="tpu_custom_call" | custom-call | tf_op jit(solution)/shard_map/mlp_step/pallas_call | solution.py:956
  1162.1 1.6 collective-permute-start
  1163.7 38.1 %settle.1 = (bf16[1024,2048]{1,0:T(8,128)(2,1)}, f32[512,8192]{1,0:T(8,128)}, f32[512,8192]{1,0:T(8,128)}, f32[2048,2048]{1,0:T(8,128)}) custom-call(bf16[1024,2048]{1,0:T(8,128)(2,1)} %bitcast.17, f32[512,8192]{1,0:T(8,128)} %get-tuple-element.14.refs_1_, f32[512,8192]{1,0:T(8,128)} %get-tuple-element.15.refs_2_, f32[2048,2048]{1,0:T(8,128)} %get-tuple-element.16.refs_3_), custom_call_target="tpu_custom_call" | custom-call | flops 1073741824 | bytes 109051904 | tf_op jit(solution)/shard_map/settle/pallas_call | solution.py:898
  1201.7 0.0 collective-permute-done.late
  1201.7 4.4 insert_late.1
Async XLA Ops:
  1162.1 39.6 %collective-permute-start = (f32[512,1536]{1,0:T(8,128)}, f32[512,1536]{1,0:T(8,128)}, u32[]{:S(2)}, u32[]{:S(2)}) collective-permute-start(f32[512,1536]{1,0:T(8,128)} %get-tuple-element.19), channel_id=1, source_target_pairs={{0,2},{1,5},{2,0},{3,7},{4,6},{5,1},{6,4},{7,3}} | collective-permute-start | bytes 9437192 | tf_op jit(solution)/shard_map/ppermute | solution.py:961

commit v8 on v7

--- a/solution.py
+++ b/solution.py
@@ -101,7 +101,10 @@
 
     def in_second(kind, i):
         block = kind // G
-        return (remote(act.at[kind, :, :, i, ZERO, ONE], act.at[kind, :, :, i, ONE, ONE], ag_send.at[kind, i, 2], ag_recv.at[kind, i, 2], reds[block]),)
+        sends = [remote(act.at[kind, :2 - (kind == X), :, i, ZERO, ONE], act.at[kind, :2 - (kind == X), :, i, ONE, ONE], ag_send.at[kind, i, 2], ag_recv.at[kind, i, 2], reds[block])]
+        if kind == X:
+            sends.append(remote(act.at[kind, ONE, :, i, ONE, ZERO], act.at[kind, ONE, :, i, ONE, ONE], ag_send.at[kind, i, 3], ag_recv.at[kind, i, 3], nons[block]))
+        return sends
 
     def out_first(block, i):
         kind, c = (H1, E1)[block], cs[block]
@@ -382,8 +385,9 @@
         def _():
             remote(src, dst, op_send.at[n], op_recv.at[i, n], twin).start()
 
-    def op_sent(i):
-        wait_all([local(src, dst, op_send.at[n]) for n, (src, dst) in enumerate(op_pairs(i, core))])
+    def op_sent(i, which):
+        for n in which:
+            local(*op_pairs(i, core)[n], op_send.at[n]).wait()
 
     def op_arrived(i):
         all_recv([remote(src, dst, op_send.at[n], op_recv.at[i, n], twin) for n, (src, dst) in enumerate(op_pairs(i, other))])
@@ -408,8 +412,9 @@
 
         repeat(2 * 4, step)
 
-    def stream(count, loads, body):
-        start_all(loads(ZERO, ZERO))
+    def stream(count, loads, body, started=False):
+        if not started:
+            start_all(loads(ZERO, ZERO))
 
         def step(n):
             slot = n % 2
@@ -454,7 +459,7 @@
     def sum_store(task, n, slot):
         return local(pst.at[slot], part.at[task, n // 2, :, :, :, pl.ds((n % 2) * TILE, TILE)], p_sem.at[slot])
 
-    def write_sums(task, loads, product):
+    def write_sums(task, loads, product, started=False):
         def body(n, slot):
             @pl.when(n >= 2)
             def _():
@@ -463,7 +468,7 @@
             pst[slot] = product(slot).reshape(2, 2, ROWS, TILE)
             sum_store(task, n, slot).start()
 
-        stream(SUM_TILES, loads, body)
+        stream(SUM_TILES, loads, body, started)
         for slot in PAIR:
             sum_store(task, slot, slot).wait()
         rs_copy(task).start()
@@ -473,6 +478,12 @@
         run_all(load_tokens(X, i, ZERO))
         normalize()
 
+        @pl.when(i > ZERO)
+        def _():
+            op_sent(i, PAIR)
+
+        turn_tokens(i, ZERO)
+
         def body(n, slot):
             pre_gate = mm(tokens(ZERO), wcol[slot, ZERO], ZERO)
             pre_in = mm(tokens(ZERO), wcol[slot, ONE], ZERO)
@@ -484,10 +495,13 @@
             fab[ZERO, slot] = pre_gate
             fab[ONE, slot] = pre_in
             start_all([kept_store(m, i, n, slot) for m in PAIR])
-            dd[i % 2, n // WIDES, :, wide(n)] = (pre_gate * jax.nn.sigmoid(pre_gate) * pre_in).astype(BF16)
+            hidden = (pre_gate * jax.nn.sigmoid(pre_gate) * pre_in).astype(BF16)
+            dd[i % 2, n // WIDES, :, wide(n)] = hidden
+            keep_u(n, cy, hidden)
 
         stream(HIDDEN_TILES, lambda n, slot: w_cols(ZERO, n, slot), body)
         wait_all([kept_store(m, i, slot, slot) for m in PAIR for slot in PAIR])
+        op_start(ONE, i, ZERO)
 
     def forward_out(i):
         def loads(n, slot):
@@ -516,14 +530,21 @@
         rows = pl.ds(h * PART, PART)
         sigma = jax.nn.sigmoid(pre_gate)
         gate_act = pre_gate * sigma
-        utw[rows, :] = (gate_act * pre_in).astype(BF16)
         dd[ZERO, n // WIDES, rows, wide(n)] = (d_hidden * pre_in * sigma * (1.0 + pre_gate * (1.0 - sigma))).astype(BF16)
         dd[ONE, n // WIDES, rows, wide(n)] = (d_hidden * gate_act).astype(BF16)
-
-    def keep_u(n, keeps_u):
+        return gate_act
+
+    def keep_u(n, keeps_u, hidden):
         @pl.when(n // WIDES == keeps_u)
         def _():
-            utb[wide(n), :] = utw[...].T
+            utb[wide(n), :] = hidden.T
+
+    def turn_tokens(i, block):
+        def turn(n):
+            ntb[n] = ab[ZERO, :, :, :, sum_cols(block, n)].reshape(BLOCK_ROWS, TILE).T
+
+        repeat(SUM_TILES, turn)
+        op_start(ZERO, i, block)
 
     def part_of(slot, h):
         return ab[slot, h].reshape(PART, WIDTH)
@@ -532,29 +553,38 @@
         i = task % CHUNKS
         block = (task // CHUNKS) % 2
 
+        def loads_1(n, slot):
+            return w_cols(ONE, n, slot) + [kept_load(2, i, n, slot)]
+
+        def loads_0(n, slot):
+            return wo_rows(ZERO, n, slot) + [kept_load(m, i, n, slot) for m in PAIR]
+
+        for n, loads in enumerate((loads_0, loads_1)):
+            @pl.when(block == n)
+            def _(loads=loads):
+                start_all(loads(ZERO, ZERO))
+
+        @pl.when(task <= BACK_AT)
+        def _():
+            op_sent(i, PAIR)
+
         @pl.when(task > CHUNKS)
         def _():
-            op_sent(i)
+            op_sent(i, range(2, 5))
 
         @pl.when(block == ONE)
         def _():
             all_recv(out_second(ZERO, i))
-            start_all(load_tokens(H1, i, ZERO) + load_tokens(G, i, ONE))
+            run_all(load_tokens(H1, i, ZERO) + load_tokens(G, i, ONE))
+            op_start(4, i, ONE)
+            normalize()
+            turn_tokens(i, ONE)
 
         @pl.when(block == ZERO)
         def _():
             all_recv(out_second(ONE, i))
-            start_all(load_tokens(X, i, ZERO) + load_tokens(E1, i, ONE))
-
-        wait_all(load_tokens(X, i, ZERO) + load_tokens(X, i, ONE))
-        op_start(4, i, block)
-        normalize()
-
-        def turn(n):
-            ntb[n] = ab[ZERO, :, :, :, sum_cols(block, n)].reshape(BLOCK_ROWS, TILE).T
-
-        repeat(SUM_TILES, turn)
-        op_start(ZERO, i, block)
+            run_all(load_tokens(E1, i, ONE))
+            op_start(4, i, ZERO)
 
         @pl.when(block == ONE)
         def _():
@@ -562,10 +592,11 @@
                 for h in PAIR:
                     pre_gate = mm(part_of(ZERO, h), wcol[slot, ZERO], ZERO)
                     pre_in = mm(part_of(ZERO, h), wcol[slot, ONE], ZERO)
-                    gradients_of(n, h, pre_gate, pre_in, fab[ZERO, slot, pl.ds(h * PART, PART)])
-                keep_u(n, cx)
-
-            stream(HIDDEN_TILES, lambda n, slot: w_cols(ONE, n, slot) + [kept_load(2, i, n, slot)], body)
+                    gate_act = gradients_of(n, h, pre_gate, pre_in, fab[ZERO, slot, pl.ds(h * PART, PART)])
+                    utw[pl.ds(h * PART, PART), :] = (gate_act * pre_in).astype(BF16)
+                keep_u(n, cx, utw[...])
+
+            stream(HIDDEN_TILES, loads_1, body, started=True)
 
         @pl.when(block == ZERO)
         def _():
@@ -573,24 +604,30 @@
                 for h in PAIR:
                     rows = pl.ds(h * PART, PART)
                     gradients_of(n, h, fab[ZERO, slot, rows], fab[ONE, slot, rows], mm(part_of(ONE, h), wo_tile(slot), ONE))
-                keep_u(n, cy)
-
-            stream(HIDDEN_TILES, lambda n, slot: wo_rows(ZERO, n, slot) + [kept_load(m, i, n, slot) for m in PAIR], body)
-
-        for n in (ONE, 2, 3):
+
+            stream(HIDDEN_TILES, loads_0, body, started=True)
+
+        @pl.when(block == ONE)
+        def _():
+            op_start(ONE, i, ONE)
+
+        for n in (2, 3):
             op_start(n, i, block)
+
+    def back_loads(block, n, slot):
+        return [local(src.at[block, fq, sum_cols(block, n)], wrow.at[slot, 2 * m + fq], s_sem.at[slot, 2 * m + fq])
+                for m, src in enumerate((wg, wi)) for fq in PAIR]
 
     def backward_out(task):
         block = (task // CHUNKS) % 2
 
         def loads(n, slot):
-            return [local(src.at[block, fq, sum_cols(block, n)], wrow.at[slot, 2 * m + fq], s_sem.at[slot, 2 * m + fq])
-                    for m, src in enumerate((wg, wi)) for fq in PAIR]
+            return back_loads(block, n, slot)
 
         def product(slot):
             return sum(mm(dd[m, fq], wrow[slot, 2 * m + fq], ONE) for m in PAIR for fq in PAIR)
 
-        write_sums(task, loads, product)
+        write_sums(task, loads, product, started=True)
 
     def grad_loads(t, slot):
         return [local(rhs_d.at[t // (2 * TILES), (t // TILES) % 2, q, :, col_tile(t)], narrow(slot, q), s_sem.at[slot, q]) for q in PAIR]
@@ -611,7 +648,7 @@
 
         @pl.when(t == ZERO)
         def _():
-            op_sent(ZERO)
+            op_sent(ZERO, range(2, 5))
             for i in range(CHUNKS):
                 op_arrived(i)
             start_all(grad_loads(ZERO, ZERO))
@@ -656,10 +693,11 @@
     def out_store(n, k, slot):
         return local(wo_out.at[slot], dwo.at[pl.ds(k * QUARTER, QUARTER), pl.ds(n * WIDE, WIDE)], o_sem.at[slot, 2])
 
+    def e_loads(n):
+        return [local(rhs_e.at[q, :, :, :, :, pl.ds(n * WIDE, WIDE)], ecol.at[q], e_sem.at[q]) for q in PAIR]
+
     def out_tile(n):
-        e_loads = [local(rhs_e.at[q, :, :, :, :, pl.ds(n * WIDE, WIDE)], ecol.at[q], e_sem.at[q]) for q in PAIR]
-        start_all(e_loads + out_loads(ZERO, ZERO))
-        wait_all(e_loads)
+        wait_all(e_loads(n))
 
         def quarter(k):
             slot = k % 2
@@ -787,6 +825,10 @@
 
         grad = tick - GRADS_AT
 
+        @pl.when((grad >= OUT_AT - 2) & ((grad - OUT_AT + 2) % OUT_EVERY == ZERO) & (grad < OUT_AT + 4 * OUT_EVERY - 2))
+        def _():
+            start_all(e_loads((grad - OUT_AT + 2) // OUT_EVERY) + out_loads(ZERO, ZERO))
+
         @pl.when((grad >= OUT_AT) & ((grad - OUT_AT) % OUT_EVERY == ZERO))
         def _():
             out_tile((grad - OUT_AT) // OUT_EVERY)
@@ -807,6 +849,10 @@
             rs_give(jnp.where(last_give, TASKS - ONE, tick - CHUNKS - 2))
 
         in_two_parts(tick - TAKE_H1, BACK_AT - TAKE_H1)(rs_take)
+
+        @pl.when((tick >= BACK_AT) & (tick < GRADS_AT))
+        def _():
+            start_all(back_loads((tick // CHUNKS + ONE) % 2, ZERO, ZERO))
 
         last_take = tick == GRADS_AT + LAG
 
@@ -863,7 +909,7 @@
 
     for i in range(CHUNKS):
         for kind in (X, G):
-            sent(in_first(kind, i) + in_second(kind, i))
+            sent([*in_first(kind, i), *in_second(kind, i)])
         for block in PAIR:
             sent(out_first(block, i) + out_second(block, i))
     repeat(TASKS, lambda task: rs_copy(task).wait_send())

time: 1220 us -> 1170 us (0.959)
  Pallas kernels: 1200 us -> 1160 us
    pallas_call x1, Pallas kernels: 1160 us -> 1120 us  [per_device(): pl.pallas_call(step_kernel, out_shape=out_shapes, in_specs=[any_space] *...]
where the time goes in v8:
time: 1170 us
  Pallas kernels  1160 us (99%)
    pallas_call x1, Pallas kernels, per_device(): pl.pallas_call(step_kernel, out_shape=out_shapes, in_specs=[any_space] *...  1120 us
    pallas_call x1, Pallas kernels, settle(): pl.pallas_call(settle_kernel, grid=(steps,), out_shape=[jax.ShapeDtypeStr...  38.1 us
  transfers between devices with their start and end apart: 1, of which 0 were waited for; matrix products, arithmetic and copies ran while one was open for 0% of the time, Pallas kernels for 3%

profile of v8, /device:TPU:0, one launch (start us, length us, event | category | flops | bytes accessed | tf_op | source)
XLA Modules:
  0.0 1165.6 jit_solution(4812394815357266317)
XLA Ops:
  0.6 1119.5 %mlp_step.1 = (bf16[4,256,2048]{2,1,0:T(8,128)(2,1)}, f32[512,8192]{1,0:T(8,128)}, f32[512,8192]{1,0:T(8,128)}, f32[2048,2048]{1,0:T(8,128)}, f32[512,1536]{1,0:...) custom-call(bf16[4,256,2048]{2,1,0:T(8,128)(2,1)} %bitcast.15, ...), custom_call_target="tpu_custom_call" | custom-call | tf_op jit(solution)/shard_map/mlp_step/pallas_call | solution.py:1002
  1120.1 2.9 collective-permute-start
  1123.1 38.1 %settle.1 = (bf16[1024,2048]{1,0:T(8,128)(2,1)}, f32[512,8192]{1,0:T(8,128)}, f32[512,8192]{1,0:T(8,128)}, f32[2048,2048]{1,0:T(8,128)}) custom-call(bf16[1024,2048]{1,0:T(8,128)(2,1)} %bitcast.17, f32[512,8192]{1,0:T(8,128)} %get-tuple-element.14.refs_1_, f32[512,8192]{1,0:T(8,128)} %get-tuple-element.15.refs_2_, f32[2048,2048]{1,0:T(8,128)} %get-tuple-element.16.refs_3_), custom_call_target="tpu_custom_call" | custom-call | flops 1073741824 | bytes 109051904 | tf_op jit(solution)/shard_map/settle/pallas_call | solution.py:944
  1161.1 0.0 collective-permute-done.late
  1161.1 4.4 insert_late.1
Async XLA Ops:
  1120.1 41.0 %collective-permute-start = (f32[512,1536]{1,0:T(8,128)}, f32[512,1536]{1,0:T(8,128)}, u32[]{:S(2)}, u32[]{:S(2)}) collective-permute-start(f32[512,1536]{1,0:T(8,128)} %get-tuple-element.19), channel_id=1, source_target_pairs={{0,2},{1,5},{2,0},{3,7},{4,6},{5,1},{6,4},{7,3}} | collective-permute-start | bytes 9437192 | tf_op jit(solution)/shard_map/ppermute | solution.py:1007

commit v9 on v8

--- a/solution.py
+++ b/solution.py
@@ -68,7 +68,7 @@
                 dx, dwg, dwi, dwo, late, act, wg, wi, wo, wx, part, rb, dots, kept, lhs_n, lhs_u, rhs_d, rhs_e,
                 wcol, wrow, fab, ab, dd, ntb, utb, utw, pst, ld, tot, own, dsv, new, dxn, ecol, outs, wo_out,
                 ag_send, ag_recv, rs_send, rs_recv, dt_send, dt_recv, w_send, w_recv, f_send, f_recv, h_send, h_recv, wo_send, wo_recv,
-                op_send, op_recv, dx_send, dx_recv, gr_send, gr_recv, p_sem, l_sem, s_sem, k_sem, b_sem, o_sem, e_sem):
+                op_send, op_recv, dx_send, dx_recv, gr_send, gr_recv, p_sem, l_sem, g_sem, s_sem, k_sem, b_sem, o_sem, e_sem):
     chip = lax.axis_index('data')
     core = lax.axis_index('stage')
     cx, cy = chip % 2, chip // 2
@@ -115,13 +115,11 @@
 
     def out_second(block, i):
         kind, c = (H1, E1)[block], cs[block]
-        sends = []
         if block:
-            sends.append(remote(act.at[kind, ONE - c, ZERO, i, :, ZERO], act.at[kind, ONE - c, ZERO, i, :, ONE], ag_send.at[kind, i, 3], ag_recv.at[kind, i, 3], reds[block]))
-        for a in PAIR:
-            for h in range(block, 2):
-                sends.append(remote(act.at[kind, c, h, i, a, ONE], act.at[kind, c, h, i, ONE - a, ONE], ag_send.at[kind, i, 4 + 2 * a + h], ag_recv.at[kind, i, 6 - 2 * a + h], nons[block]))
-        return sends
+            came, spot = act.at[kind, ONE - c, :, i, :, ZERO], act.at[kind, ONE - c, :, i, :, ONE]
+            return [remote(came, spot, ag_send.at[kind, i, 3], ag_recv.at[kind, i, 3], reds[block])]
+        return [remote(act.at[kind, c, h, i, a, ONE], act.at[kind, c, h, i, ONE - a, ONE], ag_send.at[kind, i, 4 + 2 * a + h], ag_recv.at[kind, i, 6 - 2 * a + h], nons[block])
+                for a in PAIR for h in PAIR]
 
     def pass_on(first, second):
         for copy in first:
@@ -162,8 +160,8 @@
 
     def pieces(body):
         def step(n):
-            body(n // 4, (n // 2) % 2, pl.ds((n % 2) * (ROWS // 2), ROWS // 2))
-        repeat(2 * 4, step)
+            body(n // 2, n % 2, pl.ds(ZERO, ROWS))
+        repeat(4, step)
 
     def rs_take(task):
         i, slot = task % CHUNKS, task % 2
@@ -219,16 +217,19 @@
         for copy in copies[ONE:]:
             copy.wait_send()
 
+    def give_loads(task):
+        for block in PAIR:
+            @pl.when((task // CHUNKS) % 2 == block)
+            def _(block=block):
+                i = task % CHUNKS
+                start_all([local(src, own.at[n], g_sem.at[n]) for n, src in enumerate((own_half(True, block, i), own_half(False, block, i), rest_half(block, i)))])
+
     def rs_give(task):
         i, slot = task % CHUNKS, task % 2
         for b in PAIR:
             arrived(dots.at[task - CHUNKS, b], dt_recv.at[task - CHUNKS, b])
         local(dots.at[task - CHUNKS], ld.at[ZERO, ZERO, :, :, pl.ds(ZERO, ROWS)], l_sem.at[3]).start()
-        for block in PAIR:
-            @pl.when((task // CHUNKS) % 2 == block)
-            def _(block=block):
-                start_all([local(src, own.at[n], l_sem.at[n]) for n, src in enumerate((own_half(True, block, i), own_half(False, block, i), rest_half(block, i)))])
-        wait_all([local(own_half(True, ZERO, i), own.at[n], l_sem.at[n]) for n in range(3)])
+        wait_all([local(own_half(True, ZERO, i), own.at[n], g_sem.at[n]) for n in range(3)])
         local(dots.at[task - CHUNKS], ld.at[ZERO, ZERO, :, :, pl.ds(ZERO, ROWS)], l_sem.at[3]).wait()
 
         @pl.when(task >= 2 * CHUNKS + 2)
@@ -771,6 +772,9 @@
     wo_start(ZERO)
     w_start(ONE, ZERO)
 
+    for i in PAIR:
+        start_all(in_first(G, i))
+
     @pl.when(core == ZERO)
     def _():
         w_start(ONE, ONE)
@@ -794,16 +798,23 @@
         return run
 
     def tick_step(tick):
-        for n in PAIR:
-            @pl.when(tick == n)
-            def _(n=n):
-                for i in PAIR:
-                    start_all(in_first(G, 2 * n + i))
+        @pl.when(tick == ONE)
+        def _():
+            for i in (2, 3):
+                start_all(in_first(G, i))
 
         @pl.when(tick == CHUNKS)
         def _():
             wo_pass(ONE)
             wo_arrived(ONE)
+
+        last_give = tick == GRADS_AT + 2 * LAG
+        gives = ((tick >= BACK_AT + 2) & (tick < GRADS_AT + ONE)) | last_give
+        given_task = jnp.where(last_give, TASKS - ONE, tick - CHUNKS - 2)
+
+        @pl.when(gives)
+        def _():
+            give_loads(given_task)
 
         @pl.when(tick == BACK_AT)
         def _():
@@ -842,11 +853,9 @@
             i = tick - BACK_AT - 3
             pass_on(out_first(ONE, i), out_second(ONE, i))
 
-        last_give = tick == GRADS_AT + 2 * LAG
-
-        @pl.when(((tick >= BACK_AT + 2) & (tick < GRADS_AT + ONE)) | last_give)
-        def _():
-            rs_give(jnp.where(last_give, TASKS - ONE, tick - CHUNKS - 2))
+        @pl.when(gives)
+        def _():
+            rs_give(given_task)
 
         in_two_parts(tick - TAKE_H1, BACK_AT - TAKE_H1)(rs_take)
 
@@ -998,7 +1007,7 @@
             fl(2, 2, ROWS, ROWS), bf(2, *piece), bf(2, 2, ROWS, HALF), bf(2, CHUNKS, *pair, ROWS, WIDE), fl(SLOTS, 2, QUARTER, TILE), fl(2, QUARTER, WIDE),
         ]
         counts = [(4, CHUNKS, 8), (4, CHUNKS, 8), (TASKS,), (TASKS,), (2 * CHUNKS, 2), (2 * CHUNKS, 2), (*pair, 3), (*pair, 3), (*pair, 4), (*pair, 4),
-                  (1,), (1,), (2, 3, 4), (2, 3, 4), (5,), (CHUNKS, 5), (CHUNKS, 4), (CHUNKS, 3), (SLOTS, 2), pair, (2,), (4,), (2, 4), pair, (2, *pair), (2, 3), (2,)]
+                  (1,), (1,), (2, 3, 4), (2, 3, 4), (5,), (CHUNKS, 5), (CHUNKS, 4), (CHUNKS, 3), (SLOTS, 2), pair, (2,), (4,), (3,), (2, 4), pair, (2, *pair), (2, 3), (2,)]
         results = pl.pallas_call(
             step_kernel, out_shape=out_shapes, in_specs=[any_space] * 5, out_specs=[any_space] * len(out_shapes),
             scratch_shapes=scratch + [pltpu.SemaphoreType.DMA(count) for count in counts], name='mlp_step',

time: 1170 us -> 1170 us (level)
  no operation moved by 1% of the time
where the time goes in v9:
time: 1170 us; the launch traced here: 1160 us
  Pallas kernels  1160 us (99%)
    pallas_call x1, Pallas kernels, per_device(): pl.pallas_call(step_kernel, out_shape=out_shapes, in_specs=[any_space] *...  1110 us
    pallas_call x1, Pallas kernels, settle(): pl.pallas_call(settle_kernel, grid=(steps,), out_shape=[jax.ShapeDtypeStr...  38.1 us
  transfers between devices with their start and end apart: 1, of which 0 were waited for; matrix products, arithmetic and copies ran while one was open for 0% of the time, Pallas kernels for 3%

profile of v9, /device:TPU:0, one launch (start us, length us, event | category | flops | bytes accessed | tf_op | source)
XLA Modules:
  0.0 1157.4 jit_solution(8097253945969106449)
XLA Ops:
  0.6 1113.6 %mlp_step.1 = (bf16[4,256,2048]{2,1,0:T(8,128)(2,1)}, f32[512,8192]{1,0:T(8,128)}, f32[512,8192]{1,0:T(8,128)}, f32[2048,2048]{1,0:T(8,128)}, f32[512,1536]{1,0:...) custom-call(bf16[4,256,2048]{2,1,0:T(8,128)(2,1)} %bitcast.15, ...), custom_call_target="tpu_custom_call" | custom-call | tf_op jit(solution)/shard_map/mlp_step/pallas_call | solution.py:1011
  1114.2 0.7 collective-permute-start
  1115.0 38.1 %settle.1 = (bf16[1024,2048]{1,0:T(8,128)(2,1)}, f32[512,8192]{1,0:T(8,128)}, f32[512,8192]{1,0:T(8,128)}, f32[2048,2048]{1,0:T(8,128)}) custom-call(bf16[1024,2048]{1,0:T(8,128)(2,1)} %bitcast.17, f32[512,8192]{1,0:T(8,128)} %get-tuple-element.14.refs_1_, f32[512,8192]{1,0:T(8,128)} %get-tuple-element.15.refs_2_, f32[2048,2048]{1,0:T(8,128)} %get-tuple-element.16.refs_3_), custom_call_target="tpu_custom_call" | custom-call | flops 1073741824 | bytes 109051904 | tf_op jit(solution)/shard_map/settle/pallas_call | solution.py:953
  1153.0 0.0 collective-permute-done.late
  1153.0 4.4 insert_late.1
Async XLA Ops:
  1114.2 38.8 %collective-permute-start = (f32[512,1536]{1,0:T(8,128)}, f32[512,1536]{1,0:T(8,128)}, u32[]{:S(2)}, u32[]{:S(2)}) collective-permute-start(f32[512,1536]{1,0:T(8,128)} %get-tuple-element.19), channel_id=1, source_target_pairs={{0,2},{1,5},{2,0},{3,7},{4,6},{5,1},{6,4},{7,3}} | collective-permute-start | bytes 9437192 | tf_op jit(solution)/shard_map/ppermute | solution.py:1016

commit v10 on v9

--- a/solution.py
+++ b/solution.py
@@ -28,7 +28,7 @@
 GRADS_AT = 4 * CHUNKS
 SENT_TILES = 4 * TILES
 SLOTS = 4
-OUT_AT, OUT_EVERY = 8, 7
+OUT_AT, OUT_EVERY = 4, 7
 LATE_TILES = 6
 LAG = 6
 W_PASS, W_END = (2, 3), (7, 7)

time: 1170 us -> 1160 us (level)
  no operation moved by 1% of the time
where the time goes in v10:
time: 1160 us; the launch traced here: 1150 us
  Pallas kernels  1150 us (99%)
    pallas_call x1, Pallas kernels, per_device(): pl.pallas_call(step_kernel, out_shape=out_shapes, in_specs=[any_space] *...  1100 us
    pallas_call x1, Pallas kernels, settle(): pl.pallas_call(settle_kernel, grid=(steps,), out_shape=[jax.ShapeDtypeStr...  38.1 us
  transfers between devices with their start and end apart: 1, of which 0 were waited for; matrix products, arithmetic and copies ran while one was open for 0% of the time, Pallas kernels for 3%

profile of v10, /device:TPU:0, one launch (start us, length us, event | category | flops | bytes accessed | tf_op | source)
XLA Modules:
  0.0 1147.7 jit_solution(7807328725462677757)
XLA Ops:
  0.6 1103.9 %mlp_step.1 = (bf16[4,256,2048]{2,1,0:T(8,128)(2,1)}, f32[512,8192]{1,0:T(8,128)}, f32[512,8192]{1,0:T(8,128)}, f32[2048,2048]{1,0:T(8,128)}, f32[512,1536]{1,0:...) custom-call(bf16[4,256,2048]{2,1,0:T(8,128)(2,1)} %bitcast.15, ...), custom_call_target="tpu_custom_call" | custom-call | tf_op jit(solution)/shard_map/mlp_step/pallas_call | solution.py:1011
  1104.5 0.7 collective-permute-start
  1105.3 38.1 %settle.1 = (bf16[1024,2048]{1,0:T(8,128)(2,1)}, f32[512,8192]{1,0:T(8,128)}, f32[512,8192]{1,0:T(8,128)}, f32[2048,2048]{1,0:T(8,128)}) custom-call(bf16[1024,2048]{1,0:T(8,128)(2,1)} %bitcast.17, f32[512,8192]{1,0:T(8,128)} %get-tuple-element.14.refs_1_, f32[512,8192]{1,0:T(8,128)} %get-tuple-element.15.refs_2_, f32[2048,2048]{1,0:T(8,128)} %get-tuple-element.16.refs_3_), custom_call_target="tpu_custom_call" | custom-call | flops 1073741824 | bytes 109051904 | tf_op jit(solution)/shard_map/settle/pallas_call | solution.py:953
  1143.3 0.0 collective-permute-done.late
  1143.3 4.4 insert_late.1
Async XLA Ops:
  1104.5 38.8 %collective-permute-start = (f32[512,1536]{1,0:T(8,128)}, f32[512,1536]{1,0:T(8,128)}, u32[]{:S(2)}, u32[]{:S(2)}) collective-permute-start(f32[512,1536]{1,0:T(8,128)} %get-tuple-element.19), channel_id=1, source_target_pairs={{0,2},{1,5},{2,0},{3,7},{4,6},{5,1},{6,4},{7,3}} | collective-permute-start | bytes 9437192 | tf_op jit(solution)/shard_map/ppermute | solution.py:1016
